TPU v7x, 32 devices: a whole 2x2x4 slice. The times are simulated.
32 devices in a mesh: wide: 4 (over x, core), narrow: 8 (over z, y).
Axes of the slice: x: 2, y: 2, z: 4, core: 2. Of those that a mesh axis runs over, the one named last changes fastest.
Arguments:
- inputs: bfloat16 [16384, 1024], P(('wide', 'narrow')), may hold values from -6 to 6
- w_first: bfloat16 [1024, 1024], replicated, may hold values from -0.1875 to 0.1875
- w_second: bfloat16 [1024, 256], replicated, may hold values from -0.1875 to 0.1875
- requests: int32 [128, 128], P(('wide', 'narrow')), may hold values from 0 to 511
- slots: int32 [16384, 15], P(('wide', 'narrow')), may hold values from 0 to 511
- counts: int32 [16384], P(('wide', 'narrow')), may hold values from 1 to 15
- edge_weight: int32 [16384, 15], P(('wide', 'narrow')), may hold values from 1 to 4
- offsets: int32 [4], replicated, may hold values from 0 to 511
Outputs:
- grad_first: float32 [1024, 1024], P('wide')
- grad_second: float32 [1024, 256], P('wide')
Inputs may be any that keep to these rules, and one draw needn't show every extreme that they name: requests of block d only name rows of blocks with the same narrow index as d.
All inputs are finite; a program needn't handle non-finite values.
Results may differ from a plain program's by a relative error of at most 0.0018.
Values may be sent and summed in bfloat16 or wider, within the bound.
No kernel may reach another device: no remote copies, remote signals or barrier semaphores. Data moves between devices by JAX's collectives and lax.ppermute only.
A program may use at most 64 MiB of HBM per device.

v0:
```python
import math

import jax
import jax.numpy as jnp
from jax import lax
from jax.sharding import PartitionSpec as P

NEGW = 8


def from_behind(block, axis, distance):
    devices = range(lax.axis_size(axis))
    route = [((i - distance) % len(devices), i) for i in devices]
    return lax.ppermute(block, axis, route)


def forward(block, w_first, w_second):
    pre = jnp.dot(block, w_first, preferred_element_type=jnp.float32)
    hidden = jnp.maximum(pre, 0.0).astype(jnp.bfloat16)
    codes = jnp.dot(hidden, w_second, preferred_element_type=jnp.float32)
    return (pre, hidden, codes)


def attract(codes, near, weight):
    diff = codes[:, None, :] - near.astype(jnp.float32)
    dist = jnp.sum(diff * diff, axis=-1) / diff.shape[-1]
    return jnp.sum((weight / (1.0 + dist))[:, :, None] * diff, axis=1)


def repel(codes, far):
    diff = codes[:, None, :] - far.astype(jnp.float32)
    dist = jnp.sum(diff * diff, axis=-1) / diff.shape[-1]
    onep = 1.0 + dist
    coef = 1.0 / (onep * onep * (dist / onep + 0.1))
    return -jnp.sum(coef[:, :, None] * diff, axis=1)


def negatives(block, offset, count):
    rows = block.shape[0]
    index = (
        jnp.arange(rows, dtype=jnp.int32)[:, None]
        + offset
        + jnp.arange(count, dtype=jnp.int32)[None, :]
    ) % rows
    return block[index]


def shards(inputs, w_first, w_second, requests, slots, counts, edge_weight, offsets):
    rows = inputs.shape[0]
    width = w_second.shape[1]
    peers = lax.axis_size("wide")
    total_rows = rows * peers * lax.axis_size("narrow")
    pre, hidden, codes = forward(inputs, w_first, w_second)
    sent = codes.astype(jnp.bfloat16)
    asked = lax.all_to_all(requests, "wide", split_axis=0, concat_axis=0, tiled=True)
    found = jnp.take(sent, asked.reshape(-1), axis=0).reshape(asked.shape[0], asked.shape[1], width)
    table = lax.all_to_all(found, "wide", split_axis=0, concat_axis=0, tiled=True).reshape(
        -1, width
    )
    near = jnp.take(table, slots, axis=0)
    live = jnp.arange(slots.shape[1], dtype=jnp.int32)[None, :] < counts[:, None]
    weight = jnp.where(live, edge_weight.astype(jnp.float32), jnp.float32(0.0))
    grad = attract(codes, near, weight)
    block = sent
    for step in range(offsets.shape[0]):
        block = from_behind(block, "narrow", 1)
        grad = grad + repel(codes, negatives(block, offsets[step], NEGW))
    scale = 2.0 / (slots.shape[1] * math.sqrt(total_rows))
    dcodes = (scale * grad).astype(jnp.bfloat16)
    part_second = jnp.dot(hidden.T, dcodes, preferred_element_type=jnp.float32)
    dhidden = jnp.dot(dcodes, w_second.T, preferred_element_type=jnp.float32)
    dpre = jnp.where(pre > 0, dhidden, jnp.float32(0.0)).astype(jnp.bfloat16)
    part_first = jnp.dot(inputs.T, dpre, preferred_element_type=jnp.float32)
    owned = (
        lax.psum_scatter(part_first, "wide", scatter_dimension=0, tiled=True),
        lax.psum_scatter(part_second, "wide", scatter_dimension=0, tiled=True),
    )
    grad_first, grad_second = lax.psum((owned[0], owned[1]), "narrow")
    return (grad_first, grad_second)


def solution(mesh):
    return jax.shard_map(
        shards,
        mesh=mesh,
        in_specs=(
            P(("wide", "narrow"), None),
            P(),
            P(),
            P(("wide", "narrow"), None),
            P(("wide", "narrow"), None),
            P(("wide", "narrow")),
            P(("wide", "narrow"), None),
            P(),
        ),
        out_specs=(P("wide", None), P("wide", None)),
        check_vma=False,
    )
```

profile of v0, /device:TPU:0, one launch (start us, length us, event | category | flops | bytes accessed | tf_op | source)
XLA Modules:
  0.0 354.1 jit_solution(8143698622113284613)
XLA Ops:
  7.2 1.6 copy-done
  8.8 2.5 fusion.52
  12.6 3.0 collective-permute-start
  15.6 3.2 all-to-all-start
  23.2 0.9 compare_select_fusion.2
  24.5 1.1 reshape.438
  28.0 2.0 gather_fusion
  30.8 3.4 all-to-all-start.1
  34.3 5.9 %all-to-all-done.1 = bf16[4,128,256]{2,1,0:T(8,128)(2,1)S(1)} async-done(((bf16[4,128,256]{2,1,0:T(8,128)(2,1)}), bf16[4,128,256]{2,1,0:T(8,128)(2,1)S(1)}, u32[]{:S(2)}, u32[]{:S(2)}) %all-to-all-start.1) | async-done | bytes 262176 | tf_op jit(solution)/shard_map/all_to_all | solution.py:57
  40.2 22.1 %gather_fusion.1 = bf16[7680,256]{1,0:T(8,128)(2,1)} fusion(bf16[512,256]{1,0:T(8,128)(2,1)S(1)} %bitcast.44, s32[8192]{0:T(1024)S(1)} %pad_clamp_fusion), kind=kCustom, calls=%fused_computation.1 | custom fusion | bytes 7895040 | tf_op jit(solution)/shard_map/jit(_take)/gather | solution.py:60
  62.2 6.8 %reshape.421 = bf16[512,15,256]{2,1,0:T(8,128)(2,1)} reshape(bf16[7680,256]{1,0:T(8,128)(2,1)} %gather_fusion.1) | data formatting | bytes 7864320 | tf_op jit(solution)/shard_map/jit(_take)/gather | solution.py:60
  69.0 1.6 collective-permute-start.1
  70.6 15.2 %multiply_reduce_fusion.1 = f32[512,15]{1,0:T(8,128)S(1)} fusion(f32[512,256]{1,0:T(8,128)S(1)} %get-tuple-element.26, bf16[512,15,256]{2,1,0:T(8,128)(2,1)} %reshape.421, pred[512,15]{1,0:T(8,128)(4,1)S(1)} %copy-done.10), kind=kLoop, calls=%fused_computation.7 | loop fusion | flops 9822720 | bytes 4494848 | tf_op jit(solution)/shard_map/reduce_sum | solution.py:26
  85.9 1.6 collective-permute-start.2
  87.5 4.1 %multiply_reduce_fusion = f32[512,256]{1,0:T(8,128)} fusion(f32[512,15]{1,0:T(8,128)S(1)} %add_divide_fusion, f32[512,256]{1,0:T(8,128)S(1)} %get-tuple-element.26, bf16[512,15,256]{2,1,0:T(8,128)(2,1)S(1)} %copy-done.1, pred[512,15]{1,0:T(8,128)(4,1)S(1)} %copy-done.10), kind=kLoop, calls=%fused_computation.6 | loop fusion | flops 9699328 | bytes 5019136 | tf_op jit(solution)/shard_map/reduce_sum | solution.py:27
  91.5 16.9 %gather_fusion.2 = bf16[4096,256]{1,0:T(8,128)(2,1)} fusion(bf16[512,256]{1,0:T(8,128)(2,1)S(1)} %collective-permute-done, s32[4096]{0:T(1024)S(1)} %broadcast_clamp_fusion.3), kind=kCustom, calls=%fused_computation.2 | custom fusion | bytes 4210688 | tf_op jit(solution)/shard_map/gather | solution.py:45
  108.4 1.5 collective-permute-start.3
  110.0 2.9 fusion.14
  112.9 1.0 copy.32
  114.8 16.9 %gather_fusion.3 = bf16[4096,256]{1,0:T(8,128)(2,1)} fusion(bf16[512,256]{1,0:T(8,128)(2,1)S(1)} %collective-permute-done.1, s32[4096]{0:T(1024)S(1)} %broadcast_clamp_fusion.2), kind=kCustom, calls=%fused_computation.3 | custom fusion | bytes 4210688 | tf_op jit(solution)/shard_map/gather | solution.py:45
  131.7 16.9 %gather_fusion.4 = bf16[4096,256]{1,0:T(8,128)(2,1)} fusion(bf16[512,256]{1,0:T(8,128)(2,1)S(1)} %collective-permute-done.2, s32[4096]{0:T(1024)S(1)} %broadcast_clamp_fusion.1), kind=kCustom, calls=%fused_computation.4 | custom fusion | bytes 4210688 | tf_op jit(solution)/shard_map/gather | solution.py:45
  148.7 16.9 %gather_fusion.5 = bf16[4096,256]{1,0:T(8,128)(2,1)} fusion(bf16[512,256]{1,0:T(8,128)(2,1)S(1)} %collective-permute-done.3, s32[4096]{0:T(1024)S(1)} %broadcast_clamp_fusion), kind=kCustom, calls=%fused_computation.5 | custom fusion | bytes 4210688 | tf_op jit(solution)/shard_map/gather | solution.py:45
  165.6 8.5 %fusion.15 = (f32[512,256]{1,0:T(8,128)}, f32[512,8]{1,0:T(8,128)S(1)}, f32[512,8]{1,0:T(8,128)}, f32[512,8]{1,0:T(8,128)S(1)}) fusion(bf16[4096,256]{1,0:T(8,128)(2,1)} %gather_fusion.2, f32[512,8]{1,0:T(8,128)S(1)} %copy-done.9, f32[512,256]{1,0:T(8,128)S(1)} %get-tuple-element.26, bf16[4096,256]{1,0:T(8,128)(2,1)} %gather_fusion.3, ...), kind=kLoop, calls=%fused_computation.28 | loop fusion | flops 16633856 | bytes 9502720 | tf_op jit(solution)/shard_map/reduce_sum | solution.py:35
  174.3 1.0 copy.36
  175.9 7.6 %fusion.11 = (f32[512,256]{1,0:T(8,128)S(1)}, f32[512,256]{1,0:T(8,128)S(1)}, f32[512,256]{1,0:T(8,128)S(1)}) fusion(bf16[4096,256]{1,0:T(8,128)(2,1)} %gather_fusion.3, f32[512,8]{1,0:T(8,128)S(1)} %copy.35, f32[512,256]{1,0:T(8,128)S(1)} %get-tuple-element.26, bf16[4096,256]{1,0:T(8,128)(2,1)} %gather_fusion.5, f32[512,8]{1,0:T(8,128)S(1)} %copy.39, ...), kind=kLoop, calls=%fused_computation.23 | loop fusion | flops 12189696 | bytes 8437760 | tf_op jit(solution)/shard_map/reduce_sum | solution.py:35
  183.7 1.5 fusion.17
  185.2 5.5 %convolution_bitcast_fusion = f32[1024,1024]{0,1:T(8,128)} fusion(bf16[512,1024]{1,0:T(8,128)(2,1)} %param.8, f32[512,1024]{1,0:T(8,128)} %copy-done.2, bf16[512,256]{1,0:T(8,128)(2,1)S(1)} %multiply_convert_fusion, bf16[1024,256]{1,0:T(8,128)(2,1)S(1)} %copy-done.5), kind=kOutput, calls=%fused_computation.30 | convolution fusion | flops 1343750144 | bytes 8126464 | tf_op jit(solution)/shard_map/dot_general | solution.py:73
  190.8 18.3 %reduce-scatter.5.cloned.1.call-done = f32[256,256]{1,0:T(8,128)} async-done(((f32[1024,256]{1,0:T(8,128)}), f32[256,256]{1,0:T(8,128)}) %reduce-scatter.5.cloned.1.call-update) | async-done | bytes 262160 | tf_op jit(solution)/shard_map/reduce_scatter | solution.py:76
  209.1 47.0 %reduce-scatter.3.cloned.1.call-done = f32[256,1024]{0,1:T(8,128)} async-done(((f32[1024,1024]{0,1:T(8,128)}), f32[256,1024]{0,1:T(8,128)}) %reduce-scatter.3.cloned.1.call-update) | async-done | bytes 1048592 | tf_op jit(solution)/shard_map/reduce_scatter | solution.py:75
  256.1 87.3 %all-reduce.3.cloned.1.call-done = (f32[256,1024]{0,1:T(8,128)}, f32[256,256]{1,0:T(8,128)}) async-done(((f32[256,1024]{0,1:T(8,128)}, f32[256,256]{1,0:T(8,128)}), (f32[256,1024]{0,1:T(8,128)}, f32[256,256]{1,0:T(8,128)})) %all-reduce.3.cloned.1.call-update) | async-done | bytes 1310736 | tf_op jit(solution)/shard_map/psum | solution.py:78
  343.4 2.5 copy.40
  345.9 1.7 copy.43
  (78 shorter events, 11.3 us)
Async XLA Ops:
  7.2 1.6 copy-start
  7.2 4.1 %copy-start.4 = (bf16[1024,256]{1,0:T(8,128)(2,1)S(1)}, bf16[1024,256]{1,0:T(8,128)(2,1)}, u32[]{:S(2)}) copy-start(bf16[1024,256]{1,0:T(8,128)(2,1)} %param.10) | copy-start | bytes 1572868
  7.2 11.6 %copy-start.11 = (s32[512,15]{0,1:T(8,128)S(1)}, s32[512,15]{0,1:T(8,128)}, u32[]{:S(2)}) copy-start(s32[512,15]{0,1:T(8,128)} %param.12) | copy-start | bytes 92164
  7.2 11.7 %copy-start.12 = (s32[4]{0:T(128)S(1)}, s32[4]{0:T(128)}, u32[]{:S(2)}) copy-start(s32[4]{0:T(128)} %param.15) | copy-start | bytes 52
  11.2 1.4 copy-start.2
  12.6 56.4 %collective-permute-start = (bf16[512,256]{1,0:T(8,128)(2,1)S(1)}, bf16[512,256]{1,0:T(8,128)(2,1)S(1)}, u32[]{:S(2)}, u32[]{:S(2)}) collective-permute-start(bf16[512,256]{1,0:T(8,128)(2,1)S(1)} %get-tuple-element.25), channel_id=1, source_target_pairs={{7,0},{0,1},{1,2},{2,3},{3,4},{4,5},{5,6},{6,7},{15,8},{8,9},{9,10... | collective-permute-start | bytes 786440 | tf_op jit(solution)/shard_map/ppermute | solution.py:14
  15.6 12.3 %all-to-all-start = ((s32[4,1,128]{2,1,0:T(1,128)}), s32[4,1,128]{2,1,0:T(1,128)S(1)}, u32[]{:S(2)}, u32[]{:S(2)}) async-start(s32[4,1,128]{2,1,0:T(1,128)} %bitcast), calls=%async_computation | async-start | bytes 4096 | tf_op jit(solution)/shard_map/all_to_all | solution.py:55
  30.8 9.4 %all-to-all-start.1 = ((bf16[4,128,256]{2,1,0:T(8,128)(2,1)}), bf16[4,128,256]{2,1,0:T(8,128)(2,1)S(1)}, u32[]{:S(2)}, u32[]{:S(2)}) async-start(bf16[4,128,256]{2,1,0:T(8,128)(2,1)} %broadcast_select_fusion.1), calls=%async_computation.1 | async-start | bytes 524288 | tf_op jit(solution)/shard_map/all_to_all | solution.py:57
  34.2 174.9 %reduce-scatter.5.cloned.1.call-start = ((), (), s32[]{:S(2)}) async-start(), calls=%async_computation.5 | async-start | bytes 1310720 | tf_op jit(solution)/shard_map/reduce_scatter | solution.py:76
  62.2 8.4 %copy-start.10 = (pred[512,15]{1,0:T(8,128)(4,1)S(1)}, pred[512,15]{1,0:T(8,128)(4,1)}, u32[]{:S(2)}) copy-start(pred[512,15]{1,0:T(8,128)(4,1)} %copy.30) | copy-start | bytes 23044
  69.0 16.8 %copy-start.8 = (f32[512,15]{1,0:T(8,128)S(1)}, f32[512,15]{1,0:T(8,128)}, u32[]{:S(2)}) copy-start(f32[512,15]{1,0:T(8,128)} %copy.29) | copy-start | bytes 92164
  69.0 16.8 %copy-start.13 = (s32[512]{0:T(512)S(1)}, s32[512]{0:T(512)}, u32[]{:S(2)}) copy-start(s32[512]{0:T(512)} %param.13) | copy-start | bytes 6148
  69.0 18.5 %copy-start.1 = (bf16[512,15,256]{2,1,0:T(8,128)(2,1)S(1)}, bf16[512,15,256]{2,1,0:T(8,128)(2,1)}, u32[]{:S(2)}) copy-start(bf16[512,15,256]{2,1,0:T(8,128)(2,1)} %reshape.421) | copy-start | bytes 11796484
  69.0 16.9 %collective-permute-start.1 = (bf16[512,256]{1,0:T(8,128)(2,1)S(1)}, bf16[512,256]{1,0:T(8,128)(2,1)S(1)}, u32[]{:S(2)}, u32[]{:S(2)}) collective-permute-start(bf16[512,256]{1,0:T(8,128)(2,1)S(1)} %collective-permute-done), channel_id=1, source_target_pairs={{7,0},{0,1},{1,2},{2,3},{3,4},{4,5},{5,6},{6,7},{15,8},{8,9},{9,10... | collective-permute-start | bytes 786440 | tf_op jit(solution)/shard_map/ppermute | solution.py:14
  85.9 22.5 %collective-permute-start.2 = (bf16[512,256]{1,0:T(8,128)(2,1)S(1)}, bf16[512,256]{1,0:T(8,128)(2,1)S(1)}, u32[]{:S(2)}, u32[]{:S(2)}) collective-permute-start(bf16[512,256]{1,0:T(8,128)(2,1)S(1)} %collective-permute-done.1), channel_id=1, source_target_pairs={{7,0},{0,1},{1,2},{2,3},{3,4},{4,5},{5,6},{6,7},{15,8},{8,9},{9,10... | collective-permute-start | bytes 786440 | tf_op jit(solution)/shard_map/ppermute | solution.py:14
  108.4 40.2 %collective-permute-start.3 = (bf16[512,256]{1,0:T(8,128)(2,1)S(1)}, bf16[512,256]{1,0:T(8,128)(2,1)S(1)}, u32[]{:S(2)}, u32[]{:S(2)}) collective-permute-start(bf16[512,256]{1,0:T(8,128)(2,1)S(1)} %collective-permute-done.2), channel_id=1, source_target_pairs={{7,0},{0,1},{1,2},{2,3},{3,4},{4,5},{5,6},{6,7},{15,8},{8,9},{9,10... | collective-permute-start | bytes 786440 | tf_op jit(solution)/shard_map/ppermute | solution.py:14
  148.7 16.9 %copy-start.9 = (f32[512,8]{1,0:T(8,128)S(1)}, f32[512,8]{1,0:T(8,128)}, u32[]{:S(2)}) copy-start(f32[512,8]{1,0:T(8,128)} %copy.33) | copy-start | bytes 49156
  175.8 7.7 %copy-start.6 = (f32[512,256]{1,0:T(8,128)S(1)}, f32[512,256]{1,0:T(8,128)}, u32[]{:S(2)}) copy-start(f32[512,256]{1,0:T(8,128)} %get-tuple-element.12) | copy-start | bytes 1572868
  175.8 7.7 %copy-start.7 = (f32[512,256]{1,0:T(8,128)S(1)}, f32[512,256]{1,0:T(8,128)}, u32[]{:S(2)}) copy-start(f32[512,256]{1,0:T(8,128)} %multiply_reduce_fusion) | copy-start | bytes 1572868
  175.9 7.8 %copy-start.3 = (f32[512,1024]{1,0:T(8,128)S(1)}, f32[512,1024]{1,0:T(8,128)}, u32[]{:S(2)}) copy-start(f32[512,1024]{1,0:T(8,128)} %copy-done.2) | copy-start | bytes 6291460
  183.5 1.8 copy-start.5
  185.2 70.9 %reduce-scatter.3.cloned.1.call-start = ((), (), s32[]{:S(2)}) async-start(), calls=%async_computation.4 | async-start | bytes 5242880 | tf_op jit(solution)/shard_map/reduce_scatter | solution.py:75
  190.7 152.7 %all-reduce.3.cloned.1.call-start = ((), (), s32[]{:S(2)}) async-start(), calls=%async_computation.6 | async-start | bytes 2621440 | tf_op jit(solution)/shard_map/psum | solution.py:78
Sparse Core Ops, SparseCore 0:
  185.3 23.7 reduce-scatter.4
  211.6 44.3 reduce-scatter.2
  259.7 83.6 all-reduce.2
where the time goes:
time: 355 us; the launch traced here: 354 us
  waiting for transfers between devices  159 us (45%)
  local copies, waits for them, and re-layouts  113 us (32%)
  other arithmetic  44.4 us (13%)
  starting transfers between devices  14.4 us (4%)
  between operations  14.1 us (4%)
  matrix products  9.82 us (3%)
    psum x1, waiting for transfers between devices, shards(): grad_first, grad_second = lax.psum((owned[0], owned[1]), 'narrow')  87.3 us
    gather x4, local copies, waits for them, and re-layouts, negatives(): return block[index]  67.6 us
    reduce_scatter x1, waiting for transfers between devices, shards(): lax.psum_scatter(part_first, 'wide', scatter_dimension=0, tiled=True)  47 us
    gather x2, local copies, waits for them, and re-layouts, shards(): near = jnp.take(table, slots, axis=0)  28.8 us
    reduce_scatter x1, waiting for transfers between devices, shards(): lax.psum_scatter(part_second, 'wide', scatter_dimension=0, tiled=True)  18.3 us
    reduce_sum x2, other arithmetic, repel(): return -jnp.sum(coef[:, :, None] * diff, axis=1)  16.1 us
    reduce_sum x1, other arithmetic, attract(): dist = jnp.sum(diff * diff, axis=-1) / diff.shape[-1]  15.2 us
    ppermute x4, starting transfers between devices, from_behind(): return lax.ppermute(block, axis, route)  7.66 us
  transfers between devices with their start and end apart: 9, of which 4 were waited for; matrix products, arithmetic and copies ran while one was open for 34% of the time, Pallas kernels for 0%

commit v1 on v0

v1 whole, which is shorter than its diff:
```python
import functools
import math

import jax
import jax.numpy as jnp
from jax import lax
from jax.experimental import pallas as pl
from jax.experimental.pallas import tpu as pltpu
from jax.sharding import PartitionSpec as P

NEGW = 8
LANES = 128
HALF = LANES // 2
FULL = 32000.0
STEPS = 128.0
TINY = 1e-30

F32 = jnp.float32
BF16 = jnp.bfloat16
I16 = jnp.int16
VMEM = pl.BlockSpec(memory_space=pltpu.VMEM)
SMEM = pl.BlockSpec(memory_space=pltpu.SMEM)


def call(body, out_shape, n_scalars, n_arrays, scratch=()):
    many = isinstance(out_shape, (list, tuple))
    return pl.pallas_call(
        body,
        out_shape=out_shape,
        in_specs=[SMEM] * n_scalars + [VMEM] * n_arrays,
        out_specs=[VMEM] * len(out_shape) if many else VMEM,
        scratch_shapes=list(scratch),
        compiler_params=pltpu.CompilerParams(vmem_limit_bytes=40 * 1024 * 1024),
    )


def dot(a, b):
    return lax.dot_general(a, b, (((1,), (0,)), ((), ())), preferred_element_type=F32)


def dot_nt(a, b):
    return lax.dot_general(a, b, (((1,), (1,)), ((), ())), preferred_element_type=F32)


def parts(value, count):
    out = []
    for _ in range(count):
        part = value.astype(BF16)
        out.append(part)
        value = value - part.astype(F32)
    return out


def distances(y, z):
    gram = sum(dot_nt(part, z) for part in parts(y, 3))
    zf = z.astype(F32)
    ones = jnp.ones((8, z.shape[1]), BF16)
    z_norm = sum(dot_nt(ones, part) for part in parts(zf * zf, 2))[0:1]
    y_norm = jnp.sum(y * y, axis=1, keepdims=True)
    return jnp.maximum(y_norm + z_norm - 2.0 * gram, 0.0) / z.shape[1]


def pull(y, z, coef):
    high, low = parts(coef, 2)
    total = jnp.sum(high.astype(F32) + low.astype(F32), axis=1, keepdims=True)
    return y * total - (dot(high, z) + dot(low, z))


def near_body(codes, table, slots, counts, edges, inputs, hidden, out, inputs_t, hidden_t):
    y, z = codes[...], table[...]
    column = lax.broadcasted_iota(jnp.int32, (y.shape[0], z.shape[0]), 1)
    weight = jnp.zeros((y.shape[0], z.shape[0]), F32)
    for k in range(slots.shape[1]):
        live = jnp.where(k < counts[...], edges[:, k : k + 1].astype(F32), 0.0)
        weight = weight + jnp.where(column == slots[:, k : k + 1], live, 0.0)
    out[...] = pull(y, z, weight / (1.0 + distances(y, z)))
    inputs_t[...] = inputs[...].T
    hidden_t[...] = hidden[...].T


def repulsion(y, z, offset):
    rows = z.shape[0]
    shape = (y.shape[0], rows)
    place = lax.broadcasted_iota(jnp.int32, shape, 1) - lax.broadcasted_iota(jnp.int32, shape, 0)
    place = place - offset
    place = jnp.where(place < 0, place + rows, place)
    place = jnp.where(place < 0, place + rows, place)
    dist = distances(y, z)
    onep = 1.0 + dist
    coef = jnp.where(place < NEGW, 1.0 / (onep * (dist + 0.1 * onep)), 0.0)
    return pull(y, z, coef)


def far_body(step, offsets, codes, block, grad, out):
    out[...] = grad[...] - repulsion(codes[...], block[...], offsets[step])


def pick_body(asked, sent, out):
    rows = sent.shape[0]
    for p in range(asked.shape[0]):
        hot = lax.broadcasted_iota(jnp.int32, (rows, asked.shape[1]), 0) == asked[p : p + 1, :]
        hot = jnp.where(hot, 1.0, 0.0).astype(BF16).T
        out[p] = dot(hot, sent[...]).astype(BF16)


def encode(value, first):
    quanta, codes = [], []
    for piece in (value[:, :first], value[:, first:]):
        top = jnp.maximum(jnp.max(jnp.abs(piece), axis=1, keepdims=True), TINY)
        code = jnp.ceil(jnp.log2(top) * STEPS)
        unit = FULL / jnp.exp2(code / STEPS)
        quanta.append(jnp.round(piece * unit))
        codes.append(code)
    lane = lax.broadcasted_iota(jnp.int32, (value.shape[0], LANES), 1)
    quanta.append(jnp.where(lane < HALF, codes[0], codes[1]))
    return [q.astype(jnp.int32).astype(I16) for q in quanta]


def decode(packed, first, width):
    code = packed[:, width:].astype(jnp.int32).astype(F32)
    out = []
    for lane, low, high in ((0, 0, first), (HALF, first, width)):
        unit = jnp.exp2(code[:, lane : lane + 1] / STEPS) / FULL
        out.append(packed[:, low:high].astype(jnp.int32).astype(F32) * unit)
    return out


def put_encoded(ref, value, first):
    width = value.shape[1]
    a, b, c = encode(value, first)
    ref[:, :first] = a
    ref[:, first:width] = b
    ref[:, width:] = c


def gradients(step, scale, offsets, codes, block, grad, w_second, hidden):
    total = grad[...] - repulsion(codes[...], block[...], offsets[step])
    dcodes = (scale * total).astype(BF16)
    dhidden = dot_nt(dcodes, w_second[...])
    dpre = jnp.where(hidden[...] > 0, dhidden, 0.0).astype(BF16)
    return dcodes, dpre


def last_body(step, scale, offsets, bit, codes, block, grad, w_second, hidden, inputs_t, hidden_t, keep, send):
    dcodes, dpre = gradients(step, scale, offsets, codes, block, grad, w_second, hidden)
    first = dpre.shape[1]
    rows = keep.shape[1]
    mine = bit[0]
    for a in range(keep.shape[0]):
        rows_of = pl.ds(pl.multiple_of((2 * a + 1 - mine) * rows, rows), rows)
        piece = jnp.concatenate([dot(inputs_t[rows_of, :], dpre), dot(hidden_t[rows_of, :], dcodes)], axis=1)
        put_encoded(send.at[a], piece, first)
    for a in range(keep.shape[0]):
        rows_of = pl.ds(pl.multiple_of((2 * a + mine) * rows, rows), rows)
        keep[a, :, :first] = dot(inputs_t[rows_of, :], dpre)
        keep[a, :, first:] = dot(hidden_t[rows_of, :], dcodes)


def last_plain_body(step, scale, offsets, codes, block, grad, w_second, hidden, inputs_t, hidden_t, one, two):
    dcodes, dpre = gradients(step, scale, offsets, codes, block, grad, w_second, hidden)
    one[...] = dot(inputs_t[...], dpre)
    two[...] = dot(hidden_t[...], dcodes)


def stage_body(first, bit, held, got, keep, send):
    width = held.shape[3]
    mine = bit[0]
    for a in range(held.shape[0]):
        for ref, index in ((send, 1 - mine), (keep, mine)):
            pieces = decode(got.at[a, index], first, width)
            piece = held[a, index] + jnp.concatenate(pieces, axis=1)
            if ref is send:
                put_encoded(send.at[a], piece, first)
            else:
                keep[a] = piece


def close_body(first, held, got, out):
    width = held.shape[1]
    put_encoded(out, held[...] + jnp.concatenate(decode(got, first, width), axis=1), first)


def spread_body(first, me, *refs):
    one, two = refs[-2:]
    rows = refs[0].shape[1]
    width = first + two.shape[1]
    place = 0
    for ref in refs[:-2]:
        for j in range(ref.shape[0]):
            at = pl.ds(pl.multiple_of((me[0] ^ place) * rows, rows), rows)
            one[at, :], two[at, :] = decode(ref.at[j], first, width)
            place += 1


def from_behind(block, axis, distance):
    devices = range(lax.axis_size(axis))
    route = [((i - distance) % len(devices), i) for i in devices]
    return lax.ppermute(block, axis, route)


def swapped(block, axis, bit):
    return lax.ppermute(block, axis, [(i, i ^ bit) for i in range(lax.axis_size(axis))])


def bits(count):
    return [1 << b for b in range(count.bit_length() - 1)]


def shards(inputs, w_first, w_second, requests, slots, counts, edge_weight, offsets):
    rows = inputs.shape[0]
    width = w_second.shape[1]
    peers = lax.axis_size("wide")
    group = lax.axis_size("narrow")
    din, hid = w_first.shape
    total_rows = rows * peers * group
    asked = lax.all_to_all(requests, "wide", split_axis=0, concat_axis=0, tiled=True)
    pre = jnp.dot(inputs, w_first, preferred_element_type=F32)
    hidden = jnp.maximum(pre, 0.0).astype(BF16)
    codes = jnp.dot(hidden, w_second, preferred_element_type=F32)
    sent = codes.astype(BF16)
    steps = offsets.shape[0]
    blocks = []
    for step in range(steps):
        blocks.append(from_behind(sent if step < 2 else blocks[step - 2], "narrow", min(step, 1) + 1))
    found = call(pick_body, jax.ShapeDtypeStruct(asked.shape + (width,), BF16), 0, 2)(asked, sent)
    table = lax.all_to_all(found, "wide", split_axis=0, concat_axis=0, tiled=True).reshape(-1, width)
    like = functools.partial(jax.ShapeDtypeStruct, codes.shape, F32)
    grad, inputs_t, hidden_t = call(
        near_body,
        (
            like(),
            jax.ShapeDtypeStruct((din, rows), BF16),
            jax.ShapeDtypeStruct((hid, rows), BF16),
        ),
        0,
        7,
    )(codes, table, slots, counts[:, None], edge_weight, inputs, hidden)
    for step in range(steps - 1):
        grad = call(functools.partial(far_body, step), like(), 1, 3)(offsets, codes, blocks[step], grad)
    scale = 2.0 / (slots.shape[1] * math.sqrt(total_rows))
    wide, narrow = lax.axis_index("wide"), lax.axis_index("narrow")
    chunk = din // (peers * group)
    powers = peers & (peers - 1) == 0 and group & (group - 1) == 0 and peers > 1 and group > 1
    if din != hid or not powers or chunk % 16 or din % (peers * group):
        one, two = call(
            functools.partial(last_plain_body, steps - 1, scale),
            (jax.ShapeDtypeStruct((din, hid), F32), jax.ShapeDtypeStruct((hid, width), F32)),
            1,
            7,
        )(offsets, codes, blocks[-1], grad, w_second, hidden, inputs_t, hidden_t)
        owned = (
            lax.psum_scatter(one, "wide", scatter_dimension=0, tiled=True),
            lax.psum_scatter(two, "wide", scatter_dimension=0, tiled=True),
        )
        return lax.psum(owned, "narrow")

    first, full = hid, hid + width

    def half(groups, lines):
        return (
            jax.ShapeDtypeStruct((groups, lines, full), F32),
            jax.ShapeDtypeStruct((groups, lines, full + LANES), I16),
        )

    plan = [("wide", bit, peers // (2 * bit), din // peers) for bit in bits(peers)]
    low, *high = bits(group)
    plan.append(("narrow", low, group // 2, chunk))
    plan += [("narrow", bit, 1, chunk * bit // 2) for bit in reversed(high)]

    def side(axis, bit):
        index = wide if axis == "wide" else narrow
        return ((index // bit) % 2).reshape(1).astype(jnp.int32)

    axis, bit, groups, lines = plan[0]
    keep, send = call(functools.partial(last_body, steps - 1, scale), half(groups, lines), 2, 7)(
        offsets, side(axis, bit), codes, blocks[-1], grad, w_second, hidden, inputs_t, hidden_t
    )
    got = swapped(send, axis, bit)
    for axis, bit, groups, lines in plan[1:]:
        keep, send = call(functools.partial(stage_body, first), half(groups, lines), 1, 2)(
            side(axis, bit),
            keep.reshape(groups, 2, lines, full),
            got.reshape(groups, 2, lines, full + LANES),
        )
        got = swapped(send, axis, bit)
    mine = call(
        functools.partial(close_body, first), jax.ShapeDtypeStruct((chunk, full + LANES), I16), 0, 2
    )(keep.reshape(chunk, full), got.reshape(chunk, full + LANES))
    held = {0: mine[None]}
    for bit in high + [low]:
        places = sorted(held)
        moved = swapped(jnp.concatenate([held[p] for p in places]), "narrow", bit)
        held.update({p ^ bit: moved[j : j + 1] for j, p in enumerate(places)})
    return call(
        functools.partial(spread_body, first),
        (
            jax.ShapeDtypeStruct((din // peers, hid), F32),
            jax.ShapeDtypeStruct((hid // peers, width), F32),
        ),
        1,
        1,
    )(narrow.reshape(1).astype(jnp.int32), jnp.concatenate([held[p] for p in range(group)]))


def solution(mesh):
    return jax.shard_map(
        shards,
        mesh=mesh,
        in_specs=(
            P(("wide", "narrow"), None),
            P(),
            P(),
            P(("wide", "narrow"), None),
            P(("wide", "narrow"), None),
            P(("wide", "narrow")),
            P(("wide", "narrow"), None),
            P(),
        ),
        out_specs=(P("wide", None), P("wide", None)),
        check_vma=False,
    )
```

time: 355 us -> 146 us (0.41)
  local copies, waits for them, and re-layouts: 113 us -> 16.9 us
  waiting for transfers between devices: 159 us -> 70.1 us
  other arithmetic: 44.4 us -> 0.06 us
  Pallas kernels: 0 us -> 26.7 us
  between operations: 14.1 us -> 0.89 us
  starting transfers between devices: 14.4 us -> 21.6 us
  matrix products: 9.82 us -> 2.92 us
  blocking collectives: 0 us -> 6.33 us
    gather x7 -> x0, local copies, waits for them, and re-layouts: 98.4 us -> none  [the longest x4 67.6 us: negatives(): return block[index]]
    psum x1 -> x0, waiting for transfers between devices: 87.3 us -> none  [shards(): grad_first, grad_second = lax.psum((owned[0], owned[1]), 'narrow')]
    reduce_scatter x2 -> x0, waiting for transfers between devices: 65.3 us -> none  [the longest x1 47 us: shards(): lax.psum_scatter(part_first, 'wide', scatter_dimension=0, tiled=True)]
    ppermute x0 -> x8, waiting for transfers between devices: none -> 58 us  [swapped(): lax.ppermute(block, axis, [(i, i ^ bit) for i in range(lax.axis_size(axis...]
    reduce_sum x5 -> x0, other arithmetic: 38.3 us -> none  [the longest x2 16.1 us: repel(): return -jnp.sum(coef[:, :, None] * diff, axis=1)]
    pallas_call x0 -> x12, Pallas kernels: none -> 26.7 us  [the longest x3 9.39 us: shards(): call(functools.partial(far_body, step), like(), 1, 3)]
    ppermute x0 -> x8, starting transfers between devices: none -> 12.1 us  [swapped(): lax.ppermute(block, axis, [(i, i ^ bit) for i in range(lax.axis_size(axis...]
    unnamed x30 -> x47, local copies, waits for them, and re-layouts: 6.7 us -> 16 us
  transfers between devices with their start and end apart: 9 -> 13, of which waited for: 4 -> 10; matrix products, arithmetic and copies ran while one was open for 34% -> 2% of each run, Pallas kernels for 0% -> 11%
where the time goes in v1:
time: 146 us; the launch traced here: 145 us
  waiting for transfers between devices  70.1 us (48%)
  Pallas kernels  26.7 us (18%)
  starting transfers between devices  21.6 us (15%)
  local copies, waits for them, and re-layouts  16.9 us (12%)
  blocking collectives  6.33 us (4%)
  matrix products  2.92 us (2%)
    ppermute x8, waiting for transfers between devices, swapped(): lax.ppermute(block, axis, [(i, i ^ bit) for i in range(lax.axis_size(axis...  58 us
    unnamed x47, local copies, waits for them, and re-layouts  16 us
    ppermute x8, starting transfers between devices, swapped(): lax.ppermute(block, axis, [(i, i ^ bit) for i in range(lax.axis_size(axis...  12.1 us
    pallas_call x3, Pallas kernels, shards(): call(functools.partial(far_body, step), like(), 1, 3)  9.39 us
    ppermute x4, waiting for transfers between devices, from_behind(): return lax.ppermute(block, axis, route)  8.73 us
    all_to_all x1, blocking collectives, shards(): lax.all_to_all(requests, 'wide', split_axis=0, concat_axis=0, tiled=True)  6.33 us
    ppermute x4, starting transfers between devices, from_behind(): return lax.ppermute(block, axis, route)  6.09 us
    pallas_call x1, Pallas kernels, shards(): call(functools.partial(last_body, steps - 1, scale), half(groups, lines),...  6.05 us
  transfers between devices with their start and end apart: 13, of which 10 were waited for; matrix products, arithmetic and copies ran while one was open for 2% of the time, Pallas kernels for 11%

profile of v1, /device:TPU:0, one launch (start us, length us, event | category | flops | bytes accessed | tf_op | source)
XLA Modules:
  0.0 145.4 jit_solution(12001358957642280887)
XLA Ops:
  0.7 1.6 %copy-done = bf16[1024,1024]{1,0:T(8,128)(2,1)S(1)} copy-done((bf16[1024,1024]{1,0:T(8,128)(2,1)S(1)}, bf16[1024,1024]{1,0:T(8,128)(2,1)}, u32[]{:S(2)}) %copy-start) | copy-done | bytes 2097176
  2.2 2.5 %maximum_convert_fusion.hidden = bf16[512,1024]{1,0:T(8,128)(2,1)S(1)} fusion(bf16[512,1024]{1,0:T(8,128)(2,1)} %inputs.1, bf16[1024,1024]{1,0:T(8,128)(2,1)S(1)} %copy-done), kind=kOutput, calls=%fused_computation | convolution fusion | flops 1074790400 | bytes 4194304 | tf_op jit(solution)/shard_map/dot_general | solution.py:217
  6.2 3.0 %collective-permute-start.2 = (bf16[512,256]{1,0:T(8,128)(2,1)S(1)}, bf16[512,256]{1,0:T(8,128)(2,1)}, u32[]{:S(2)}, u32[]{:S(2)}) collective-permute-start(bf16[512,256]{1,0:T(8,128)(2,1)S(1)} %get-tuple-element.28.sent), channel_id=1, source_target_pairs={{7,0},{0,1},{1,2},{2,3},{3,4},{4,5},{5,6},{6,7},{15,8},{8,9},{9,10... | collective-permute-start | bytes 786440 | tf_op jit(solution)/shard_map/ppermute | solution.py:198
  9.2 1.6 %collective-permute-start = (bf16[512,256]{1,0:T(8,128)(2,1)S(1)}, bf16[512,256]{1,0:T(8,128)(2,1)}, u32[]{:S(2)}, u32[]{:S(2)}) collective-permute-start(bf16[512,256]{1,0:T(8,128)(2,1)S(1)} %get-tuple-element.28.sent), channel_id=1, source_target_pairs={{6,0},{7,1},{0,2},{1,3},{2,4},{3,5},{4,6},{5,7},{14,8},{15,9},{8,1... | collective-permute-start | bytes 786440 | tf_op jit(solution)/shard_map/ppermute | solution.py:198
  10.8 8.7 %collective-permute-done.2.block = bf16[512,256]{1,0:T(8,128)(2,1)} collective-permute-done((bf16[512,256]{1,0:T(8,128)(2,1)S(1)}, bf16[512,256]{1,0:T(8,128)(2,1)}, u32[]{:S(2)}, u32[]{:S(2)}) %collective-permute-start.2) | collective-permute-done | bytes 262176 | tf_op jit(solution)/shard_map/ppermute | solution.py:198
  19.5 1.5 %collective-permute-start.1 = (bf16[512,256]{1,0:T(8,128)(2,1)}, bf16[512,256]{1,0:T(8,128)(2,1)}, u32[]{:S(2)}, u32[]{:S(2)}) collective-permute-start(bf16[512,256]{1,0:T(8,128)(2,1)} %collective-permute-done.block), channel_id=1, source_target_pairs={{6,0},{7,1},{0,2},{1,3},{2,4},{3,5},{4,6},{5,7},{14,8},{15,9},{8,1... | collective-permute-start | bytes 786440 | tf_op jit(solution)/shard_map/ppermute | solution.py:198
  21.0 6.3 %all_to_all.16 = s32[4,1,128]{2,1,0:T(1,128)S(1)} all-to-all(s32[4,1,128]{2,1,0:T(1,128)S(1)} %bitcast.42), channel_id=1, replica_groups=mesh['wide'=4,'narrow'=8] {'wide'}, dimensions={0} | all-to-all | bytes 4096 | tf_op jit(solution)/shard_map/all_to_all | solution.py:216
  28.4 3.4 %all-to-all-start.1 = ((bf16[4,128,256]{2,1,0:T(8,128)(2,1)}), bf16[4,128,256]{2,1,0:T(8,128)(2,1)S(1)}, u32[]{:S(2)}, u32[]{:S(2)}) async-start(bf16[4,128,256]{2,1,0:T(8,128)(2,1)} %copy-done.13), calls=%async_computation.1 | async-start | bytes 524288 | tf_op jit(solution)/shard_map/all_to_all | solution.py:226
  34.4 3.4 %all-to-all-done.1 = bf16[4,128,256]{2,1,0:T(8,128)(2,1)S(1)} async-done(((bf16[4,128,256]{2,1,0:T(8,128)(2,1)}), bf16[4,128,256]{2,1,0:T(8,128)(2,1)S(1)}, u32[]{:S(2)}, u32[]{:S(2)}) %all-to-all-start.1) | async-done | bytes 262176 | tf_op jit(solution)/shard_map/all_to_all | solution.py:226
  37.8 1.2 copy-done.2
  43.1 5.7 %shard_map.96 = (f32[512,256]{1,0:T(8,128)S(1)}, bf16[1024,512]{1,0:T(8,128)(2,1)S(1)}, bf16[1024,512]{1,0:T(8,128)(2,1)S(1)}) custom-call(f32[512,256]{1,0:T(8,128)S(1)} %get-tuple-element.29.codes, bf16[512,256]{1,0:T(8,128)(2,1)S(1)} %bitcast.32, s32[512,15]{1,0:T(8,128)S(1)} %copy-done.9, s32[512,1]{1,0:T(8,128)S(1)} %copy-done.10, ...), custom_call_target="tpu_custom_call" | custom-call | tf_op jit(solution)/shard_map/pallas_call | solution.py:228
  48.8 3.1 %shard_map.97.grad = f32[512,256]{1,0:T(8,128)S(1)} custom-call(s32[4]{0:T(128)S(1)} %copy-done.14, f32[512,256]{1,0:T(8,128)S(1)} %get-tuple-element.29.codes, bf16[512,256]{1,0:T(8,128)(2,1)} %collective-permute-done.2.block, f32[512,256]{1,0:T(8,128)S(1)} %get-tuple-element.15.grad), custom_call_target="tpu_custom_call" | custom-call | tf_op jit(solution)/shard_map/pallas_call | solution.py:239
  51.9 3.2 %shard_map.98.grad = f32[512,256]{1,0:T(8,128)S(1)} custom-call(s32[4]{0:T(128)S(1)} %copy-done.14, f32[512,256]{1,0:T(8,128)S(1)} %get-tuple-element.29.codes, bf16[512,256]{1,0:T(8,128)(2,1)} %collective-permute-done.block, f32[512,256]{1,0:T(8,128)S(1)} %shard_map.97.grad), custom_call_target="tpu_custom_call" | custom-call | tf_op jit(solution)/shard_map/pallas_call | solution.py:239
  55.2 3.1 %shard_map.99.grad = f32[512,256]{1,0:T(8,128)S(1)} custom-call(s32[4]{0:T(128)S(1)} %copy-done.14, f32[512,256]{1,0:T(8,128)S(1)} %get-tuple-element.29.codes, bf16[512,256]{1,0:T(8,128)(2,1)} %collective-permute-done.3.block, f32[512,256]{1,0:T(8,128)S(1)} %shard_map.98.grad), custom_call_target="tpu_custom_call" | custom-call | tf_op jit(solution)/shard_map/pallas_call | solution.py:239
  58.3 6.1 %shard_map.100 = (f32[2,256,1280]{2,1,0:T(8,128)S(1)}, s16[2,256,1408]{2,1,0:T(8,128)(2,1)}) custom-call(s32[4]{0:T(128)S(1)} %copy-done.14, s32[1]{0:T(128)} %bitcast.5.bit, f32[512,256]{1,0:T(8,128)S(1)} %get-tuple-element.29.codes, bf16[512,256]{1,0:T(8,128)(2,1)} %collective-permute-done.1.block, f32[512,256]{1,0:T(8,128)S(1)} %shard_map.99.grad, ...), custom_call_target="tpu_custom_call" | custom-call | tf_op jit(solution)/shard_map/pallas_call | solution.py:275
  64.3 1.5 %copy-done.4 = f32[2,256,1280]{2,1,0:T(8,128)} copy-done((f32[2,256,1280]{2,1,0:T(8,128)}, f32[2,256,1280]{2,1,0:T(8,128)S(1)}, u32[]{:S(2)}) %copy-start.4) | copy-done | bytes 2621464
  65.8 3.4 %collective-permute-done.4 = s16[2,256,1408]{2,1,0:T(8,128)(2,1)S(1)} collective-permute-done((s16[2,256,1408]{2,1,0:T(8,128)(2,1)}, s16[2,256,1408]{2,1,0:T(8,128)(2,1)S(1)}, u32[]{:S(2)}, u32[]{:S(2)}) %collective-permute-start.4) | collective-permute-done | bytes 1441824 | tf_op jit(solution)/shard_map/ppermute | solution.py:202
  69.3 1.7 %copy-done.5 = f32[2,256,1280]{2,1,0:T(8,128)S(1)} copy-done((f32[2,256,1280]{2,1,0:T(8,128)S(1)}, f32[2,256,1280]{2,1,0:T(8,128)}, u32[]{:S(2)}) %copy-start.5) | copy-done | bytes 2621464
  71.0 1.4 shard_map.101
  73.9 18.0 %collective-permute-done.5 = s16[1,256,1408]{2,1,0:T(8,128)(2,1)S(1)} collective-permute-done((s16[1,256,1408]{2,1,0:T(8,128)(2,1)}, s16[1,256,1408]{2,1,0:T(8,128)(2,1)S(1)}, u32[]{:S(2)}, u32[]{:S(2)}) %collective-permute-start.5) | collective-permute-done | bytes 720928 | tf_op jit(solution)/shard_map/ppermute | solution.py:202
  91.9 1.3 copy-done.8
  94.4 4.8 %collective-permute-start.6 = (s16[4,32,1408]{2,1,0:T(8,128)(2,1)}, s16[4,32,1408]{2,1,0:T(8,128)(2,1)S(1)}, u32[]{:S(2)}, u32[]{:S(2)}) collective-permute-start(s16[4,32,1408]{2,1,0:T(8,128)(2,1)} %get-tuple-element.23), channel_id=1, source_target_pairs={{0,1},{1,0},{2,3},{3,2},{4,5},{5,4},{6,7},{7,6},{8,9},{9,8},{10,11... | collective-permute-start | bytes 1081352 | tf_op jit(solution)/shard_map/ppermute | solution.py:202
  99.2 8.1 %collective-permute-done.6 = s16[4,32,1408]{2,1,0:T(8,128)(2,1)S(1)} collective-permute-done((s16[4,32,1408]{2,1,0:T(8,128)(2,1)}, s16[4,32,1408]{2,1,0:T(8,128)(2,1)S(1)}, u32[]{:S(2)}, u32[]{:S(2)}) %collective-permute-start.6) | collective-permute-done | bytes 360480 | tf_op jit(solution)/shard_map/ppermute | solution.py:202
  108.2 2.4 %collective-permute-start.7 = (s16[1,64,1408]{2,1,0:T(8,128)(2,1)}, s16[1,64,1408]{2,1,0:T(8,128)(2,1)S(1)}, u32[]{:S(2)}, u32[]{:S(2)}) collective-permute-start(s16[1,64,1408]{2,1,0:T(8,128)(2,1)} %get-tuple-element.25), channel_id=1, source_target_pairs={{0,4},{1,5},{2,6},{3,7},{4,0},{5,1},{6,2},{7,3},{8,12},{9,13},{10,... | collective-permute-start | bytes 540680 | tf_op jit(solution)/shard_map/ppermute | solution.py:202
  110.5 7.8 %collective-permute-done.7 = s16[1,64,1408]{2,1,0:T(8,128)(2,1)S(1)} collective-permute-done((s16[1,64,1408]{2,1,0:T(8,128)(2,1)}, s16[1,64,1408]{2,1,0:T(8,128)(2,1)S(1)}, u32[]{:S(2)}, u32[]{:S(2)}) %collective-permute-start.7) | collective-permute-done | bytes 180256 | tf_op jit(solution)/shard_map/ppermute | solution.py:202
  119.2 4.0 %collective-permute-done.8 = s16[1,32,1408]{2,1,0:T(8,128)(2,1)S(1)} collective-permute-done((s16[1,32,1408]{2,1,0:T(8,128)(2,1)S(1)}, s16[1,32,1408]{2,1,0:T(8,128)(2,1)S(1)}, u32[]{:S(2)}, u32[]{:S(2)}) %collective-permute-start.8) | collective-permute-done | bytes 90144 | tf_op jit(solution)/shard_map/ppermute | solution.py:202
  124.0 4.0 %collective-permute-done.9 = s16[1,32,1408]{2,1,0:T(8,128)(2,1)S(1)} collective-permute-done((s16[1,32,1408]{2,1,0:T(8,128)(2,1)S(1)}, s16[1,32,1408]{2,1,0:T(8,128)(2,1)S(1)}, u32[]{:S(2)}, u32[]{:S(2)}) %collective-permute-start.9) | collective-permute-done | bytes 90144 | tf_op jit(solution)/shard_map/ppermute | solution.py:202
  128.0 1.9 %collective-permute-start.10 = (s16[2,32,1408]{2,1,0:T(8,128)(2,1)S(1)}, s16[2,32,1408]{2,1,0:T(8,128)(2,1)S(1)}, u32[]{:S(2)}, u32[]{:S(2)}) collective-permute-start(s16[2,32,1408]{2,1,0:T(8,128)(2,1)S(1)} %pad_add_fusion.1), channel_id=1, source_target_pairs={{0,4},{1,5},{2,6},{3,7},{4,0},{5,1},{6,2},{7,3},{8,12},{9,13},{10,... | collective-permute-start | bytes 540680 | tf_op jit(solution)/shard_map/ppermute | solution.py:202
  129.9 6.6 %collective-permute-done.10 = s16[2,32,1408]{2,1,0:T(8,128)(2,1)S(1)} collective-permute-done((s16[2,32,1408]{2,1,0:T(8,128)(2,1)S(1)}, s16[2,32,1408]{2,1,0:T(8,128)(2,1)S(1)}, u32[]{:S(2)}, u32[]{:S(2)}) %collective-permute-start.10) | collective-permute-done | bytes 180256 | tf_op jit(solution)/shard_map/ppermute | solution.py:202
  136.6 1.4 collective-permute-start.11
  137.9 6.1 %collective-permute-done.11 = s16[4,32,1408]{2,1,0:T(8,128)(2,1)S(1)} collective-permute-done((s16[4,32,1408]{2,1,0:T(8,128)(2,1)S(1)}, s16[4,32,1408]{2,1,0:T(8,128)(2,1)S(1)}, u32[]{:S(2)}, u32[]{:S(2)}) %collective-permute-start.11) | collective-permute-done | bytes 360480 | tf_op jit(solution)/shard_map/ppermute | solution.py:202
  144.2 1.2 shard_map.106
  (60 shorter events, 14.5 us)
Async XLA Ops:
  0.6 1.6 %copy-start = (bf16[1024,1024]{1,0:T(8,128)(2,1)S(1)}, bf16[1024,1024]{1,0:T(8,128)(2,1)}, u32[]{:S(2)}) copy-start(bf16[1024,1024]{1,0:T(8,128)(2,1)} %param.9) | copy-start | bytes 6291460
  0.6 4.1 %copy-start.6 = (bf16[1024,256]{1,0:T(8,128)(2,1)S(1)}, bf16[1024,256]{1,0:T(8,128)(2,1)}, u32[]{:S(2)}) copy-start(bf16[1024,256]{1,0:T(8,128)(2,1)} %w_second.1) | copy-start | bytes 1572868
  4.7 16.3 %copy-start.18 = (s32[4,128]{1,0:T(4,128)S(1)}, s32[4,128]{1,0:T(4,128)}, u32[]{:S(2)}) copy-start(s32[4,128]{1,0:T(4,128)} %param.11) | copy-start | bytes 6148
  4.7 27.1 %copy-start.15 = (s32[512,15]{0,1:T(8,128)S(1)}, s32[512,15]{0,1:T(8,128)}, u32[]{:S(2)}) copy-start(s32[512,15]{0,1:T(8,128)} %param.12) | copy-start | bytes 92164
  4.7 27.9 %copy-start.17 = (s32[512]{0:T(512)S(1)}, s32[512]{0:T(512)}, u32[]{:S(2)}) copy-start(s32[512]{0:T(512)} %param.13) | copy-start | bytes 6148
  4.8 28.8 %copy-start.16 = (s32[512,15]{0,1:T(8,128)S(1)}, s32[512,15]{0,1:T(8,128)}, u32[]{:S(2)}) copy-start(s32[512,15]{0,1:T(8,128)} %param.14) | copy-start | bytes 92164
  5.2 1.0 copy-start.1
  6.2 13.3 %collective-permute-start.2 = (bf16[512,256]{1,0:T(8,128)(2,1)S(1)}, bf16[512,256]{1,0:T(8,128)(2,1)}, u32[]{:S(2)}, u32[]{:S(2)}) collective-permute-start(bf16[512,256]{1,0:T(8,128)(2,1)S(1)} %get-tuple-element.28.sent), channel_id=1, source_target_pairs={{7,0},{0,1},{1,2},{2,3},{3,4},{4,5},{5,6},{6,7},{15,8},{8,9},{9,10... | collective-permute-start | bytes 786440 | tf_op jit(solution)/shard_map/ppermute | solution.py:198
  9.2 10.3 %collective-permute-start = (bf16[512,256]{1,0:T(8,128)(2,1)S(1)}, bf16[512,256]{1,0:T(8,128)(2,1)}, u32[]{:S(2)}, u32[]{:S(2)}) collective-permute-start(bf16[512,256]{1,0:T(8,128)(2,1)S(1)} %get-tuple-element.28.sent), channel_id=1, source_target_pairs={{6,0},{7,1},{0,2},{1,3},{2,4},{3,5},{4,6},{5,7},{14,8},{15,9},{8,1... | collective-permute-start | bytes 786440 | tf_op jit(solution)/shard_map/ppermute | solution.py:198
  19.5 35.7 %collective-permute-start.3 = (bf16[512,256]{1,0:T(8,128)(2,1)}, bf16[512,256]{1,0:T(8,128)(2,1)}, u32[]{:S(2)}, u32[]{:S(2)}) collective-permute-start(bf16[512,256]{1,0:T(8,128)(2,1)} %collective-permute-done.2.block), channel_id=1, source_target_pairs={{6,0},{7,1},{0,2},{1,3},{2,4},{3,5},{4,6},{5,7},{14,8},{15,9},{8,1... | collective-permute-start | bytes 786440 | tf_op jit(solution)/shard_map/ppermute | solution.py:198
  19.5 38.8 %collective-permute-start.1 = (bf16[512,256]{1,0:T(8,128)(2,1)}, bf16[512,256]{1,0:T(8,128)(2,1)}, u32[]{:S(2)}, u32[]{:S(2)}) collective-permute-start(bf16[512,256]{1,0:T(8,128)(2,1)} %collective-permute-done.block), channel_id=1, source_target_pairs={{6,0},{7,1},{0,2},{1,3},{2,4},{3,5},{4,6},{5,7},{14,8},{15,9},{8,1... | collective-permute-start | bytes 786440 | tf_op jit(solution)/shard_map/ppermute | solution.py:198
  27.7 0.7 copy-start.13
  28.4 9.4 %all-to-all-start.1 = ((bf16[4,128,256]{2,1,0:T(8,128)(2,1)}), bf16[4,128,256]{2,1,0:T(8,128)(2,1)S(1)}, u32[]{:S(2)}, u32[]{:S(2)}) async-start(bf16[4,128,256]{2,1,0:T(8,128)(2,1)} %copy-done.13), calls=%async_computation.1 | async-start | bytes 524288 | tf_op jit(solution)/shard_map/all_to_all | solution.py:226
  32.7 16.1 %copy-start.14 = (s32[4]{0:T(128)S(1)}, s32[4]{0:T(128)}, u32[]{:S(2)}) copy-start(s32[4]{0:T(128)} %offsets.7) | copy-start | bytes 52
  37.8 1.2 copy-start.2
  39.0 0.9 copy-start.9
  40.0 0.9 copy-start.10
  40.9 0.9 copy-start.11
  41.9 1.2 copy-start.12
  51.9 6.3 %copy-start.3 = (bf16[512,1024]{1,0:T(8,128)(2,1)S(1)}, bf16[512,1024]{1,0:T(8,128)(2,1)}, u32[]{:S(2)}) copy-start(bf16[512,1024]{1,0:T(8,128)(2,1)} %copy-done.1) | copy-start | bytes 3145732
  64.3 1.5 %copy-start.4 = (f32[2,256,1280]{2,1,0:T(8,128)}, f32[2,256,1280]{2,1,0:T(8,128)S(1)}, u32[]{:S(2)}) copy-start(f32[2,256,1280]{2,1,0:T(8,128)S(1)} %get-tuple-element.18) | copy-start | bytes 7864324
  65.8 3.4 %collective-permute-start.4 = (s16[2,256,1408]{2,1,0:T(8,128)(2,1)}, s16[2,256,1408]{2,1,0:T(8,128)(2,1)S(1)}, u32[]{:S(2)}, u32[]{:S(2)}) collective-permute-start(s16[2,256,1408]{2,1,0:T(8,128)(2,1)} %get-tuple-element.19), channel_id=1, source_target_pairs={{0,8},{8,0},{16,24},{24,16},{1,9},{9,1},{17,25},{25,17},{2,10},{10... | collective-permute-start | bytes 4325384 | tf_op jit(solution)/shard_map/ppermute | solution.py:202
  69.3 1.7 %copy-start.5 = (f32[2,256,1280]{2,1,0:T(8,128)S(1)}, f32[2,256,1280]{2,1,0:T(8,128)}, u32[]{:S(2)}) copy-start(f32[2,256,1280]{2,1,0:T(8,128)} %copy-done.4) | copy-start | bytes 7864324
  72.4 1.1 copy-start.7
  73.5 18.4 %collective-permute-start.5 = (s16[1,256,1408]{2,1,0:T(8,128)(2,1)}, s16[1,256,1408]{2,1,0:T(8,128)(2,1)S(1)}, u32[]{:S(2)}, u32[]{:S(2)}) collective-permute-start(s16[1,256,1408]{2,1,0:T(8,128)(2,1)} %get-tuple-element.21), channel_id=1, source_target_pairs={{0,16},{8,24},{16,0},{24,8},{1,17},{9,25},{17,1},{25,9},{2,18},{10... | collective-permute-start | bytes 2162696 | tf_op jit(solution)/shard_map/ppermute | solution.py:202
  91.9 1.3 copy-start.8
  94.4 12.9 %collective-permute-start.6 = (s16[4,32,1408]{2,1,0:T(8,128)(2,1)}, s16[4,32,1408]{2,1,0:T(8,128)(2,1)S(1)}, u32[]{:S(2)}, u32[]{:S(2)}) collective-permute-start(s16[4,32,1408]{2,1,0:T(8,128)(2,1)} %get-tuple-element.23), channel_id=1, source_target_pairs={{0,1},{1,0},{2,3},{3,2},{4,5},{5,4},{6,7},{7,6},{8,9},{9,8},{10,11... | collective-permute-start | bytes 1081352 | tf_op jit(solution)/shard_map/ppermute | solution.py:202
  108.2 10.1 %collective-permute-start.7 = (s16[1,64,1408]{2,1,0:T(8,128)(2,1)}, s16[1,64,1408]{2,1,0:T(8,128)(2,1)S(1)}, u32[]{:S(2)}, u32[]{:S(2)}) collective-permute-start(s16[1,64,1408]{2,1,0:T(8,128)(2,1)} %get-tuple-element.25), channel_id=1, source_target_pairs={{0,4},{1,5},{2,6},{3,7},{4,0},{5,1},{6,2},{7,3},{8,12},{9,13},{10,... | collective-permute-start | bytes 540680 | tf_op jit(solution)/shard_map/ppermute | solution.py:202
  118.5 4.6 %collective-permute-start.8 = (s16[1,32,1408]{2,1,0:T(8,128)(2,1)S(1)}, s16[1,32,1408]{2,1,0:T(8,128)(2,1)S(1)}, u32[]{:S(2)}, u32[]{:S(2)}) collective-permute-start(s16[1,32,1408]{2,1,0:T(8,128)(2,1)S(1)} %get-tuple-element.27), channel_id=1, source_target_pairs={{0,2},{1,3},{2,0},{3,1},{4,6},{5,7},{6,4},{7,5},{8,10},{9,11},{10,... | collective-permute-start | bytes 270344 | tf_op jit(solution)/shard_map/ppermute | solution.py:202
  123.3 4.6 %collective-permute-start.9 = (s16[1,32,1408]{2,1,0:T(8,128)(2,1)S(1)}, s16[1,32,1408]{2,1,0:T(8,128)(2,1)S(1)}, u32[]{:S(2)}, u32[]{:S(2)}) collective-permute-start(s16[1,32,1408]{2,1,0:T(8,128)(2,1)S(1)} %bitcast.28), channel_id=1, source_target_pairs={{0,2},{1,3},{2,0},{3,1},{4,6},{5,7},{6,4},{7,5},{8,10},{9,11},{10,... | collective-permute-start | bytes 270344 | tf_op jit(solution)/shard_map/ppermute | solution.py:202
  128.0 8.6 %collective-permute-start.10 = (s16[2,32,1408]{2,1,0:T(8,128)(2,1)S(1)}, s16[2,32,1408]{2,1,0:T(8,128)(2,1)S(1)}, u32[]{:S(2)}, u32[]{:S(2)}) collective-permute-start(s16[2,32,1408]{2,1,0:T(8,128)(2,1)S(1)} %pad_add_fusion.1), channel_id=1, source_target_pairs={{0,4},{1,5},{2,6},{3,7},{4,0},{5,1},{6,2},{7,3},{8,12},{9,13},{10,... | collective-permute-start | bytes 540680 | tf_op jit(solution)/shard_map/ppermute | solution.py:202
  136.6 7.5 %collective-permute-start.11 = (s16[4,32,1408]{2,1,0:T(8,128)(2,1)S(1)}, s16[4,32,1408]{2,1,0:T(8,128)(2,1)S(1)}, u32[]{:S(2)}, u32[]{:S(2)}) collective-permute-start(s16[4,32,1408]{2,1,0:T(8,128)(2,1)S(1)} %pad_add_fusion), channel_id=1, source_target_pairs={{0,1},{1,0},{2,3},{3,2},{4,5},{5,4},{6,7},{7,6},{8,9},{9,8},{10,11... | collective-permute-start | bytes 1081352 | tf_op jit(solution)/shard_map/ppermute | solution.py:202

commit v2 on v1

v2 whole, which is shorter than its diff:
```python
import functools
import math

import jax
import jax.numpy as jnp
from jax import lax
from jax.experimental import pallas as pl
from jax.experimental.pallas import tpu as pltpu
from jax.sharding import PartitionSpec as P

NEGW = 8
TILE = 128
PACK = 16
LANES = 128
HALF = LANES // 2
FULL = 32000.0
STEPS = 128.0
TINY = 1e-30

F32 = jnp.float32
BF16 = jnp.bfloat16
I16 = jnp.int16
VMEM = pl.BlockSpec(memory_space=pltpu.VMEM)
SMEM = pl.BlockSpec(memory_space=pltpu.SMEM)


def call(body, out_shape, n_scalars, n_arrays, scratch=(), mib=16):
    many = isinstance(out_shape, (list, tuple))
    return pl.pallas_call(
        body,
        out_shape=out_shape,
        in_specs=[SMEM] * n_scalars + [VMEM] * n_arrays,
        out_specs=[VMEM] * len(out_shape) if many else VMEM,
        scratch_shapes=list(scratch),
        compiler_params=pltpu.CompilerParams(vmem_limit_bytes=mib * 1024 * 1024),
    )


def dot(a, b):
    return lax.dot_general(a, b, (((1,), (0,)), ((), ())), preferred_element_type=F32)


def dot_nt(a, b):
    return lax.dot_general(a, b, (((1,), (1,)), ((), ())), preferred_element_type=F32)


def parts(value, count):
    out = []
    for _ in range(count):
        part = value.astype(BF16)
        out.append(part)
        value = value - part.astype(F32)
    return out


def norms(z):
    zf = z.astype(F32)
    ones = jnp.ones((8, z.shape[1]), BF16)
    return sum(dot_nt(ones, part) for part in parts(zf * zf, 2))[0:1]


def distances(y, z, z_norm):
    gram = sum(dot_nt(part, z) for part in parts(y, 3))
    y_norm = jnp.sum(y * y, axis=1, keepdims=True)
    return jnp.maximum(y_norm + z_norm - 2.0 * gram, 0.0) * (1.0 / z.shape[1])


def pull(y, z, coef):
    high, low = parts(coef, 2)
    total = jnp.sum(high.astype(F32) + low.astype(F32), axis=1, keepdims=True)
    return y * total - (dot(high, z) + dot(low, z))


def flip_body(inputs, hidden, inputs_t, hidden_t):
    inputs_t[...] = inputs[...].T
    hidden_t[...] = hidden[...].T


def near_body(me, codes, requests, slots, counts, edges, grad, *rest):
    out, table = rest[-2:]
    cap = requests.shape[1]
    place = 0
    for ref in rest[:-2]:
        for j in range(ref.shape[0]):
            rows = ref.shape[1]
            asked = requests[pl.ds(me[0] ^ place, 1), :]
            hot = lax.broadcasted_iota(jnp.int32, (rows, cap), 0) == asked
            hot = jnp.where(hot, 1.0, 0.0).astype(BF16).T
            at = pl.ds(pl.multiple_of((me[0] ^ place) * cap, cap), cap)
            table[at, :] = dot(hot, ref[j]).astype(BF16)
            place += 1
    z = table[...]
    z_norm = norms(z)
    tile = min(codes.shape[0], TILE)
    column = lax.broadcasted_iota(jnp.int32, (tile, z.shape[0]), 1)
    for at in range(0, codes.shape[0], tile):
        rows_of = slice(at, at + tile)
        y = codes[rows_of, :]
        weight = jnp.zeros((tile, z.shape[0]), F32)
        live = lax.broadcasted_iota(jnp.int32, (tile, edges.shape[1]), 1) < counts[rows_of, :]
        live = jnp.where(live, edges[rows_of, :].astype(F32), 0.0)
        for k in range(slots.shape[1]):
            weight = weight + jnp.where(column == slots[rows_of, k : k + 1], live[:, k : k + 1], 0.0)
        out[rows_of, :] = grad[rows_of, :] + pull(y, z, weight / (1.0 + distances(y, z, z_norm)))


def repulsion(codes, block, offset, twice, put):
    rows = block.shape[0]
    tile = min(rows, TILE)
    window = tile + max(tile, LANES)
    for at in range(0, twice.shape[0], rows):
        end = min(rows, twice.shape[0] - at)
        twice[at : at + end, :] = block[:end, :]
    start = (offset // PACK) * PACK
    shape = (tile, window)
    place = lax.broadcasted_iota(jnp.int32, shape, 1) - lax.broadcasted_iota(jnp.int32, shape, 0)
    place = place - (offset - start)
    band = (place >= 0) & (place < NEGW)
    for at in range(0, rows, tile):
        y = codes[at : at + tile, :]
        z = twice[pl.ds(pl.multiple_of(start + at, PACK), window), :]
        dist = distances(y, z, norms(z))
        onep = 1.0 + dist
        coef = jnp.where(band, 1.0 / (onep * (dist + 0.1 * onep)), 0.0)
        put(slice(at, at + tile), pull(y, z, coef))


def twice_of(rows, width):
    tile = min(rows, TILE)
    return pltpu.VMEM((2 * rows + max(tile, LANES), width), BF16)


def far_body(step, started, offsets, codes, block, *rest):
    grad, out, twice = rest if started else (None,) + rest

    def put(at, value):
        out[at, :] = grad[at, :] - value if started else -value

    repulsion(codes, block, offsets[step], twice, put)


def encode(one, two):
    quanta, codes = [], []
    for piece in (one, two):
        top = jnp.maximum(jnp.max(jnp.abs(piece), axis=1, keepdims=True), TINY)
        code = jnp.ceil(jnp.log2(top) * STEPS)
        unit = FULL / jnp.exp2(code * (1.0 / STEPS))
        quanta.append(jnp.round(piece * unit))
        codes.append(code)
    lane = lax.broadcasted_iota(jnp.int32, (one.shape[0], LANES), 1)
    quanta.append(jnp.where(lane < HALF, codes[0], codes[1]))
    return [q.astype(jnp.int32).astype(I16) for q in quanta]


def decode(packed, first, width):
    code = packed[:, width:].astype(jnp.int32).astype(F32)
    out = []
    for lane, low, high in ((0, 0, first), (HALF, first, width)):
        unit = jnp.exp2(code[:, lane : lane + 1] * (1.0 / STEPS)) * (1.0 / FULL)
        out.append(packed[:, low:high].astype(jnp.int32).astype(F32) * unit)
    return out


def put_encoded(ref, one, two):
    first, width = one.shape[1], one.shape[1] + two.shape[1]
    ref[:, :first], ref[:, first:width], ref[:, width:] = encode(one, two)


def gradients(step, scale, offsets, codes, block, grad, w_second, hidden, twice, dcodes, dpre):
    def put(at, value):
        small = (scale * (grad[at, :] - value)).astype(BF16)
        dcodes[at, :] = small
        wide = dot_nt(small, w_second[...])
        dpre[at, :] = jnp.where(hidden[at, :] > 0, wide, 0.0).astype(BF16)

    repulsion(codes, block, offsets[step], twice, put)


def last_body(step, scale, offsets, bit, codes, block, grad, w_second, hidden, inputs_t, hidden_t, keep, send, *scratch):
    gradients(step, scale, offsets, codes, block, grad, w_second, hidden, *scratch)
    dcodes, dpre = scratch[1:]
    first = dpre.shape[1]
    rows = keep.shape[1]
    mine = bit[0]
    for a in range(keep.shape[0]):
        rows_of = pl.ds(pl.multiple_of((2 * a + 1 - mine) * rows, rows), rows)
        one, two = dot(inputs_t[rows_of, :], dpre[...]), dot(hidden_t[rows_of, :], dcodes[...])
        put_encoded(send.at[a], one, two)
    for a in range(keep.shape[0]):
        rows_of = pl.ds(pl.multiple_of((2 * a + mine) * rows, rows), rows)
        keep[a, :, :first] = dot(inputs_t[rows_of, :], dpre[...])
        keep[a, :, first:] = dot(hidden_t[rows_of, :], dcodes[...])


def last_plain_body(step, scale, offsets, codes, block, grad, w_second, hidden, inputs_t, hidden_t, one, two, *scratch):
    gradients(step, scale, offsets, codes, block, grad, w_second, hidden, *scratch)
    dcodes, dpre = scratch[1:]
    one[...] = dot(inputs_t[...], dpre[...])
    two[...] = dot(hidden_t[...], dcodes[...])


def summed(held, got, first):
    one, two = decode(got, first, held.shape[-1])
    return held[:, :first] + one, held[:, first:] + two


def stage_body(first, bit, held, got, keep, send):
    mine = bit[0]
    for a in range(held.shape[0]):
        put_encoded(send.at[a], *summed(held.at[a, 1 - mine], got.at[a, 1 - mine], first))
    for a in range(held.shape[0]):
        keep[a, :, :first], keep[a, :, first:] = summed(held.at[a, mine], got.at[a, mine], first)


def deal_body(first, me, held, got, keep, *sends):
    for k in range(1, held.shape[0]):
        put_encoded(sends[k - 1], *summed(held.at[me[0] ^ k], got.at[me[0] ^ k], first))
    keep[:, :first], keep[:, first:] = summed(held.at[me[0]], got.at[me[0]], first)


def close_body(first, held, *refs):
    one, two = held[:, :first], held[:, first:]
    for got in refs[:-1]:
        more = decode(got, first, held.shape[1])
        one, two = one + more[0], two + more[1]
    put_encoded(refs[-1], one, two)


def spread_body(first, me, *refs):
    one, two = refs[-2:]
    width = first + two.shape[1]
    for place, ref in enumerate(refs[:-2]):
        rows = ref.shape[0]
        at = pl.ds(pl.multiple_of((me[0] ^ place) * rows, rows), rows)
        one[at, :], two[at, :] = decode(ref, first, width)


def from_behind(block, axis, distance):
    devices = range(lax.axis_size(axis))
    route = [((i - distance) % len(devices), i) for i in devices]
    return lax.ppermute(block, axis, route)


def swapped(block, axis, bit):
    return lax.ppermute(block, axis, [(i, i ^ bit) for i in range(lax.axis_size(axis))])


def bits(count):
    return [1 << b for b in range(count.bit_length() - 1)]


def shards(inputs, w_first, w_second, requests, slots, counts, edge_weight, offsets):
    rows = inputs.shape[0]
    width = w_second.shape[1]
    peers = lax.axis_size("wide")
    group = lax.axis_size("narrow")
    din, hid = w_first.shape
    total_rows = rows * peers * group
    powers = peers & (peers - 1) == 0 and group & (group - 1) == 0 and peers > 1 and group > 1
    assert powers, "axis sizes"
    wide, narrow = lax.axis_index("wide"), lax.axis_index("narrow")
    w_id, n_id = (index.reshape(1).astype(jnp.int32) for index in (wide, narrow))
    pre = jnp.dot(inputs, w_first, preferred_element_type=F32)
    hidden = jnp.maximum(pre, 0.0).astype(BF16)
    codes = jnp.dot(hidden, w_second, preferred_element_type=F32)
    sent = codes.astype(BF16)
    steps = offsets.shape[0]
    blocks = []
    for step in range(steps):
        blocks.append(from_behind(sent if step < 2 else blocks[step - 2], "narrow", min(step, 1) + 1))
    near = [sent[None]]
    for bit in bits(peers):
        moved = near[0] if bit == 1 else jnp.concatenate(near)
        near.append(swapped(moved, "wide", bit))
    inputs_t, hidden_t = call(
        flip_body,
        (jax.ShapeDtypeStruct((din, rows), BF16), jax.ShapeDtypeStruct((hid, rows), BF16)),
        0,
        2,
    )(inputs, hidden)
    like = jax.ShapeDtypeStruct(codes.shape, F32)
    twice = twice_of(rows, width)

    def far(step, grad):
        given = () if grad is None else (grad,)
        body = functools.partial(far_body, step, bool(given))
        return call(body, like, 1, 2 + len(given), [twice])(offsets, codes, blocks[step], *given)

    grad = None
    early = max(steps - 2, 1)
    for step in range(early):
        grad = far(step, grad)
    table = pltpu.VMEM((peers * requests.shape[1], width), BF16)
    grad = call(near_body, like, 1, 6 + len(near), [table])(
        w_id, codes, requests, slots, counts[:, None], edge_weight, grad, *near
    )
    for step in range(early, steps - 1):
        grad = far(step, grad)
    scale = 2.0 / (slots.shape[1] * math.sqrt(total_rows))
    chunk = din // (peers * group)
    scratch = [twice, pltpu.VMEM((rows, width), BF16), pltpu.VMEM((rows, hid), BF16)]
    if din != hid or chunk % 16 or din % (peers * group):
        one, two = call(
            functools.partial(last_plain_body, steps - 1, scale),
            (jax.ShapeDtypeStruct((din, hid), F32), jax.ShapeDtypeStruct((hid, width), F32)),
            1,
            7,
            scratch,
        )(offsets, codes, blocks[-1], grad, w_second, hidden, inputs_t, hidden_t)
        owned = (
            lax.psum_scatter(one, "wide", scatter_dimension=0, tiled=True),
            lax.psum_scatter(two, "wide", scatter_dimension=0, tiled=True),
        )
        return lax.psum(owned, "narrow")

    first, full = hid, hid + width

    def plain(*shape):
        return jax.ShapeDtypeStruct((*shape, full), F32)

    def coded(*shape):
        return jax.ShapeDtypeStruct((*shape, full + LANES), I16)

    plan = [(bit, peers // (2 * bit), din // peers) for bit in bits(peers)]
    keep = got = None
    for bit, groups, lines in plan:
        side = (w_id // bit) % 2
        halves = (plain(groups, lines), coded(groups, lines))
        if keep is None:
            body = functools.partial(last_body, steps - 1, scale)
            keep, send = call(body, halves, 2, 7, scratch)(
                offsets, side, codes, blocks[-1], grad, w_second, hidden, inputs_t, hidden_t
            )
        else:
            keep, send = call(functools.partial(stage_body, first), halves, 1, 2)(
                side, keep.reshape(groups, 2, lines, full), got.reshape(groups, 2, lines, full + LANES)
            )
        got = swapped(send, "wide", bit)
    keep, *sends = call(
        functools.partial(deal_body, first), (plain(chunk),) + (coded(chunk),) * (group - 1), 1, 2
    )(n_id, keep.reshape(group, chunk, full), got.reshape(group, chunk, full + LANES))
    gots = [swapped(send, "narrow", k + 1) for k, send in enumerate(sends)]
    mine = call(functools.partial(close_body, first), coded(chunk), 0, group)(keep, *gots)
    pieces = [mine] + [swapped(mine, "narrow", k) for k in range(1, group)]
    return call(
        functools.partial(spread_body, first),
        (
            jax.ShapeDtypeStruct((din // peers, hid), F32),
            jax.ShapeDtypeStruct((hid // peers, width), F32),
        ),
        1,
        group,
    )(n_id, *pieces)


def solution(mesh):
    return jax.shard_map(
        shards,
        mesh=mesh,
        in_specs=(
            P(("wide", "narrow"), None),
            P(),
            P(),
            P(("wide", "narrow"), None),
            P(("wide", "narrow"), None),
            P(("wide", "narrow")),
            P(("wide", "narrow"), None),
            P(),
        ),
        out_specs=(P("wide", None), P("wide", None)),
        check_vma=False,
    )
```

time: 146 us -> 123 us (0.84)
  waiting for transfers between devices: 70.1 us -> 44.6 us
  starting transfers between devices: 21.6 us -> 38.6 us
  local copies, waits for them, and re-layouts: 16.9 us -> 9.62 us
  blocking collectives: 6.33 us -> 0 us
    ppermute x8 -> x18, waiting for transfers between devices: 58 us -> 35.7 us  [swapped(): lax.ppermute(block, axis, [(i, i ^ bit) for i in range(lax.axis_size(axis...]
    ppermute x8 -> x18, starting transfers between devices: 12.1 us -> 34.2 us  [swapped(): lax.ppermute(block, axis, [(i, i ^ bit) for i in range(lax.axis_size(axis...]
    unnamed x47 -> x42, local copies, waits for them, and re-layouts: 16 us -> 8.75 us
    all_to_all x1 -> x0, blocking collectives: 6.33 us -> none  [shards(): lax.all_to_all(requests, 'wide', split_axis=0, concat_axis=0, tiled=True)]
    all_to_all x1 -> x0, starting transfers between devices: 3.41 us -> none  [shards(): lax.all_to_all(found, 'wide', split_axis=0, concat_axis=0, tiled=True)]
    all_to_all x1 -> x0, waiting for transfers between devices: 3.41 us -> none  [shards(): lax.all_to_all(found, 'wide', split_axis=0, concat_axis=0, tiled=True)]
    ppermute x4, starting transfers between devices: 6.09 us -> 4.45 us  [from_behind(): return lax.ppermute(block, axis, route)]
    pallas_call x11 -> x9, Pallas kernels: 25.4 us -> 24.2 us  [the longest x3 7.9 us: far(): call(body, like, 1, 2 + len(given), [twice])]
  transfers between devices with their start and end apart: 13 -> 22, of which waited for: 10 -> 9; matrix products, arithmetic and copies ran while one was open for 2% -> 2% of each run, Pallas kernels for 11% -> 12%
where the time goes in v2:
time: 123 us
  waiting for transfers between devices  44.6 us (36%)
  starting transfers between devices  38.6 us (31%)
  Pallas kernels  25.4 us (21%)
  local copies, waits for them, and re-layouts  9.62 us (8%)
  matrix products  2.93 us (2%)
    ppermute x18, waiting for transfers between devices, swapped(): lax.ppermute(block, axis, [(i, i ^ bit) for i in range(lax.axis_size(axis...  35.7 us
    ppermute x18, starting transfers between devices, swapped(): lax.ppermute(block, axis, [(i, i ^ bit) for i in range(lax.axis_size(axis...  34.2 us
    ppermute x4, waiting for transfers between devices, from_behind(): return lax.ppermute(block, axis, route)  8.89 us
    unnamed x42, local copies, waits for them, and re-layouts  8.75 us
    pallas_call x3, Pallas kernels, far(): call(body, like, 1, 2 + len(given), [twice])  7.9 us
    pallas_call x1, Pallas kernels, shards(): call(near_body, like, 1, 6 + len(near), [table])  6.48 us
    pallas_call x1, Pallas kernels, shards(): call(body, halves, 2, 7, scratch)  5.61 us
    ppermute x4, starting transfers between devices, from_behind(): return lax.ppermute(block, axis, route)  4.45 us
  transfers between devices with their start and end apart: 22, of which 9 were waited for; matrix products, arithmetic and copies ran while one was open for 2% of the time, Pallas kernels for 12%

profile of v2, /device:TPU:0, one launch (start us, length us, event | category | flops | bytes accessed | tf_op | source)
XLA Modules:
  0.0 123.1 jit_solution(181925742651024397)
XLA Ops:
  0.7 1.6 %copy-done = bf16[1024,1024]{1,0:T(8,128)(2,1)S(1)} copy-done((bf16[1024,1024]{1,0:T(8,128)(2,1)S(1)}, bf16[1024,1024]{1,0:T(8,128)(2,1)}, u32[]{:S(2)}) %copy-start) | copy-done | bytes 2097176
  2.2 2.5 %maximum_convert_fusion.hidden = bf16[512,1024]{1,0:T(8,128)(2,1)S(1)} fusion(bf16[512,1024]{1,0:T(8,128)(2,1)} %inputs.1, bf16[1024,1024]{1,0:T(8,128)(2,1)S(1)} %copy-done), kind=kOutput, calls=%fused_computation | convolution fusion | flops 1074790400 | bytes 4194304 | tf_op jit(solution)/shard_map/dot_general | solution.py:263
  6.7 1.2 collective-permute-done.4.rest_1_
  8.8 2.8 %collective-permute-start.5 = (bf16[2,512,256]{2,1,0:T(8,128)(2,1)}, bf16[2,512,256]{2,1,0:T(8,128)(2,1)}, u32[]{:S(2)}, u32[]{:S(2)}) collective-permute-start(bf16[2,512,256]{2,1,0:T(8,128)(2,1)} %pad_maximum_fusion), channel_id=1, source_target_pairs={{0,16},{8,24},{16,0},{24,8},{1,17},{9,25},{17,1},{25,9},{2,18},{10... | collective-permute-start | bytes 1572872 | tf_op jit(solution)/shard_map/ppermute | solution.py:245
  11.6 1.5 %collective-permute-start.2 = (bf16[512,256]{1,0:T(8,128)(2,1)S(1)}, bf16[512,256]{1,0:T(8,128)(2,1)}, u32[]{:S(2)}, u32[]{:S(2)}) collective-permute-start(bf16[512,256]{1,0:T(8,128)(2,1)S(1)} %get-tuple-element.30), channel_id=1, source_target_pairs={{7,0},{0,1},{1,2},{2,3},{3,4},{4,5},{5,6},{6,7},{15,8},{8,9},{9,10... | collective-permute-start | bytes 786440 | tf_op jit(solution)/shard_map/ppermute | solution.py:241
  13.2 1.6 %collective-permute-start = (bf16[512,256]{1,0:T(8,128)(2,1)S(1)}, bf16[512,256]{1,0:T(8,128)(2,1)}, u32[]{:S(2)}, u32[]{:S(2)}) collective-permute-start(bf16[512,256]{1,0:T(8,128)(2,1)S(1)} %get-tuple-element.30), channel_id=1, source_target_pairs={{6,0},{7,1},{0,2},{1,3},{2,4},{3,5},{4,6},{5,7},{14,8},{15,9},{8,1... | collective-permute-start | bytes 786440 | tf_op jit(solution)/shard_map/ppermute | solution.py:241
  14.7 8.9 %collective-permute-done.2.block = bf16[512,256]{1,0:T(8,128)(2,1)} collective-permute-done((bf16[512,256]{1,0:T(8,128)(2,1)S(1)}, bf16[512,256]{1,0:T(8,128)(2,1)}, u32[]{:S(2)}, u32[]{:S(2)}) %collective-permute-start.2) | collective-permute-done | bytes 262176 | tf_op jit(solution)/shard_map/ppermute | solution.py:241
  23.6 1.3 %collective-permute-start.1 = (bf16[512,256]{1,0:T(8,128)(2,1)}, bf16[512,256]{1,0:T(8,128)(2,1)}, u32[]{:S(2)}, u32[]{:S(2)}) collective-permute-start(bf16[512,256]{1,0:T(8,128)(2,1)} %collective-permute-done.block), channel_id=1, source_target_pairs={{6,0},{7,1},{0,2},{1,3},{2,4},{3,5},{4,6},{5,7},{14,8},{15,9},{8,1... | collective-permute-start | bytes 786440 | tf_op jit(solution)/shard_map/ppermute | solution.py:241
  25.0 1.2 copy-done.2
  26.2 1.2 copy-done.8
  32.6 2.7 %shard_map.95.rest_0_ = f32[512,256]{1,0:T(8,128)S(1)} custom-call(s32[4]{0:T(128)S(1)} %copy-done.15, f32[512,256]{1,0:T(8,128)S(1)} %get-tuple-element.31.codes, bf16[512,256]{1,0:T(8,128)(2,1)} %collective-permute-done.2.block), custom_call_target="tpu_custom_call" | custom-call | tf_op jit(solution)/shard_map/pallas_call | solution.py:287
  35.3 2.6 %shard_map.96.grad = f32[512,256]{1,0:T(8,128)S(1)} custom-call(s32[4]{0:T(128)S(1)} %copy-done.15, f32[512,256]{1,0:T(8,128)S(1)} %get-tuple-element.31.codes, bf16[512,256]{1,0:T(8,128)(2,1)} %collective-permute-done.block, f32[512,256]{1,0:T(8,128)S(1)} %shard_map.95.rest_0_), custom_call_target="tpu_custom_call" | custom-call | tf_op jit(solution)/shard_map/pallas_call | solution.py:287
  38.0 6.5 %shard_map.97.rest_0_ = f32[512,256]{1,0:T(8,128)S(1)} custom-call(s32[1]{0:T(128)} %bitcast.1.me, f32[512,256]{1,0:T(8,128)S(1)} %get-tuple-element.31.codes, s32[4,128]{1,0:T(4,128)S(1)} %copy-done.16, s32[512,15]{1,0:T(8,128)S(1)} %copy-done.5, s32[512,1]{1,0:T(8,128)S(1)} %copy-done.6, s32[512,15]{1,0:T(8,128)S(1)} %copy-done.7, ...), custom_call_target="tpu_custom_call" | custom-call | tf_op jit(solution)/shard_map/pallas_call | solution.py:294
  44.5 2.6 %shard_map.98.grad = f32[512,256]{1,0:T(8,128)S(1)} custom-call(s32[4]{0:T(128)S(1)} %copy-done.15, f32[512,256]{1,0:T(8,128)S(1)} %get-tuple-element.31.codes, bf16[512,256]{1,0:T(8,128)(2,1)} %collective-permute-done.3.block, f32[512,256]{1,0:T(8,128)S(1)} %shard_map.97.rest_0_), custom_call_target="tpu_custom_call" | custom-call | tf_op jit(solution)/shard_map/pallas_call | solution.py:287
  47.2 5.6 %shard_map.100 = (f32[2,256,1280]{2,1,0:T(8,128)S(1)}, s16[2,256,1408]{2,1,0:T(8,128)(2,1)S(1)}) custom-call(s32[4]{0:T(128)S(1)} %copy-done.15, s32[1]{0:T(128)S(6)} %select_n.19.bit, f32[512,256]{1,0:T(8,128)S(1)} %get-tuple-element.31.codes, bf16[512,256]{1,0:T(8,128)(2,1)} %collective-permute-done.1.block, f32[512,256]{1,0:T(8,128)S(1)} %shard_map.98.grad, ...), custom_call_target="tpu_custom_call" | custom-call | tf_op jit(solution)/shard_map/pallas_call | solution.py:331
  52.9 3.2 %collective-permute-done.6 = s16[2,256,1408]{2,1,0:T(8,128)(2,1)S(1)} collective-permute-done((s16[2,256,1408]{2,1,0:T(8,128)(2,1)S(1)}, s16[2,256,1408]{2,1,0:T(8,128)(2,1)S(1)}, u32[]{:S(2)}, u32[]{:S(2)}) %collective-permute-start.6) | collective-permute-done | bytes 1441824 | tf_op jit(solution)/shard_map/ppermute | solution.py:245
  56.1 1.5 %shard_map.101 = (f32[1,256,1280]{2,1,0:T(8,128)S(1)}, s16[1,256,1408]{2,1,0:T(8,128)(2,1)}) custom-call(s32[1]{0:T(128)S(6)} %select_n.18.bit, f32[1,2,256,1280]{3,2,1,0:T(8,128)S(1)} %bitcast.12, s16[1,2,256,1408]{3,2,1,0:T(8,128)(2,1)S(1)} %bitcast.16), custom_call_target="tpu_custom_call" | custom-call | tf_op jit(solution)/shard_map/pallas_call | solution.py:335
  58.1 18.0 %collective-permute-done.7 = s16[1,256,1408]{2,1,0:T(8,128)(2,1)} collective-permute-done((s16[1,256,1408]{2,1,0:T(8,128)(2,1)}, s16[1,256,1408]{2,1,0:T(8,128)(2,1)}, u32[]{:S(2)}, u32[]{:S(2)}) %collective-permute-start.7) | collective-permute-done | bytes 720928 | tf_op jit(solution)/shard_map/ppermute | solution.py:245
  76.1 1.8 %shard_map.102 = (f32[32,1280]{1,0:T(8,128)S(1)}, s16[32,1408]{1,0:T(8,128)(2,1)S(1)}, s16[32,1408]{1,0:T(8,128)(2,1)S(1)}, s16[32,1408]{1,0:T(8,128)(2,1)S(1)},...) custom-call(s32[1]{0:T(128)} %bitcast.me, ...), custom_call_target="tpu_custom_call" | custom-call | tf_op jit(solution)/shard_map/pallas_call | solution.py:339
  77.9 4.9 %collective-permute-start.8 = (s16[32,1408]{1,0:T(8,128)(2,1)S(1)}, s16[32,1408]{1,0:T(8,128)(2,1)S(1)}, u32[]{:S(2)}, u32[]{:S(2)}) collective-permute-start(s16[32,1408]{1,0:T(8,128)(2,1)S(1)} %get-tuple-element.23), channel_id=1, source_target_pairs={{0,1},{1,0},{2,3},{3,2},{4,5},{5,4},{6,7},{7,6},{8,9},{9,8},{10,11... | collective-permute-start | bytes 270344 | tf_op jit(solution)/shard_map/ppermute | solution.py:245
  82.8 1.4 %collective-permute-start.9 = (s16[32,1408]{1,0:T(8,128)(2,1)S(1)}, s16[32,1408]{1,0:T(8,128)(2,1)S(1)}, u32[]{:S(2)}, u32[]{:S(2)}) collective-permute-start(s16[32,1408]{1,0:T(8,128)(2,1)S(1)} %get-tuple-element.24), channel_id=1, source_target_pairs={{0,2},{1,3},{2,0},{3,1},{4,6},{5,7},{6,4},{7,5},{8,10},{9,11},{10,... | collective-permute-start | bytes 270344 | tf_op jit(solution)/shard_map/ppermute | solution.py:245
  84.3 2.8 %collective-permute-start.11 = (s16[32,1408]{1,0:T(8,128)(2,1)S(1)}, s16[32,1408]{1,0:T(8,128)(2,1)S(1)}, u32[]{:S(2)}, u32[]{:S(2)}) collective-permute-start(s16[32,1408]{1,0:T(8,128)(2,1)S(1)} %get-tuple-element.26), channel_id=1, source_target_pairs={{0,4},{1,5},{2,6},{3,7},{4,0},{5,1},{6,2},{7,3},{8,12},{9,13},{10,... | collective-permute-start | bytes 270344 | tf_op jit(solution)/shard_map/ppermute | solution.py:245
  87.2 1.5 %collective-permute-start.12 = (s16[32,1408]{1,0:T(8,128)(2,1)S(1)}, s16[32,1408]{1,0:T(8,128)(2,1)S(1)}, u32[]{:S(2)}, u32[]{:S(2)}) collective-permute-start(s16[32,1408]{1,0:T(8,128)(2,1)S(1)} %get-tuple-element.27), channel_id=1, source_target_pairs={{0,5},{1,4},{2,7},{3,6},{4,1},{5,0},{6,3},{7,2},{8,13},{9,12},{10,... | collective-permute-start | bytes 270344 | tf_op jit(solution)/shard_map/ppermute | solution.py:245
  88.7 3.8 %collective-permute-start.13 = (s16[32,1408]{1,0:T(8,128)(2,1)S(1)}, s16[32,1408]{1,0:T(8,128)(2,1)S(1)}, u32[]{:S(2)}, u32[]{:S(2)}) collective-permute-start(s16[32,1408]{1,0:T(8,128)(2,1)S(1)} %get-tuple-element.28), channel_id=1, source_target_pairs={{0,6},{1,7},{2,4},{3,5},{4,2},{5,3},{6,0},{7,1},{8,14},{9,15},{10,... | collective-permute-start | bytes 270344 | tf_op jit(solution)/shard_map/ppermute | solution.py:245
  92.5 8.9 %collective-permute-done.12.refs_4_ = s16[32,1408]{1,0:T(8,128)(2,1)S(1)} collective-permute-done((s16[32,1408]{1,0:T(8,128)(2,1)S(1)}, s16[32,1408]{1,0:T(8,128)(2,1)S(1)}, u32[]{:S(2)}, u32[]{:S(2)}) %collective-permute-start.12) | collective-permute-done | bytes 90144 | tf_op jit(solution)/shard_map/ppermute | solution.py:245
  101.7 2.6 %collective-permute-start.21 = (s16[32,1408]{1,0:T(8,128)(2,1)S(1)}, s16[32,1408]{1,0:T(8,128)(2,1)S(1)}, u32[]{:S(2)}, u32[]{:S(2)}) collective-permute-start(s16[32,1408]{1,0:T(8,128)(2,1)S(1)} %shard_map.103.refs_0_), channel_id=1, source_target_pairs={{0,7},{1,6},{2,5},{3,4},{4,3},{5,2},{6,1},{7,0},{8,15},{9,14},{10,... | collective-permute-start | bytes 270344 | tf_op jit(solution)/shard_map/ppermute | solution.py:245
  104.3 1.1 collective-permute-start.20
  105.5 3.7 %collective-permute-start.19 = (s16[32,1408]{1,0:T(8,128)(2,1)S(1)}, s16[32,1408]{1,0:T(8,128)(2,1)S(1)}, u32[]{:S(2)}, u32[]{:S(2)}) collective-permute-start(s16[32,1408]{1,0:T(8,128)(2,1)S(1)} %shard_map.103.refs_0_), channel_id=1, source_target_pairs={{0,5},{1,4},{2,7},{3,6},{4,1},{5,0},{6,3},{7,2},{8,13},{9,12},{10,... | collective-permute-start | bytes 270344 | tf_op jit(solution)/shard_map/ppermute | solution.py:245
  109.4 1.5 %collective-permute-start.17 = (s16[32,1408]{1,0:T(8,128)(2,1)S(1)}, s16[32,1408]{1,0:T(8,128)(2,1)S(1)}, u32[]{:S(2)}, u32[]{:S(2)}) collective-permute-start(s16[32,1408]{1,0:T(8,128)(2,1)S(1)} %shard_map.103.refs_0_), channel_id=1, source_target_pairs={{0,3},{1,2},{2,1},{3,0},{4,7},{5,6},{6,5},{7,4},{8,11},{9,10},{10,... | collective-permute-start | bytes 270344 | tf_op jit(solution)/shard_map/ppermute | solution.py:245
  111.0 6.3 %collective-permute-start.16 = (s16[32,1408]{1,0:T(8,128)(2,1)S(1)}, s16[32,1408]{1,0:T(8,128)(2,1)S(1)}, u32[]{:S(2)}, u32[]{:S(2)}) collective-permute-start(s16[32,1408]{1,0:T(8,128)(2,1)S(1)} %shard_map.103.refs_0_), channel_id=1, source_target_pairs={{0,2},{1,3},{2,0},{3,1},{4,6},{5,7},{6,4},{7,5},{8,10},{9,11},{10,... | collective-permute-start | bytes 270344 | tf_op jit(solution)/shard_map/ppermute | solution.py:245
  117.3 3.2 %collective-permute-done.19.refs_5_ = s16[32,1408]{1,0:T(8,128)(2,1)S(1)} collective-permute-done((s16[32,1408]{1,0:T(8,128)(2,1)S(1)}, s16[32,1408]{1,0:T(8,128)(2,1)S(1)}, u32[]{:S(2)}, u32[]{:S(2)}) %collective-permute-start.19) | collective-permute-done | bytes 90144 | tf_op jit(solution)/shard_map/ppermute | solution.py:245
  121.8 1.2 shard_map.104
  (68 shorter events, 10.8 us)
Async XLA Ops:
  6.2 23.9 %copy-start.17 = (s32[512,15]{0,1:T(8,128)S(1)}, s32[512,15]{0,1:T(8,128)}, u32[]{:S(2)}) copy-start(s32[512,15]{0,1:T(8,128)} %param.12) | copy-start | bytes 92164
  6.2 24.7 %copy-start.19 = (s32[512]{0:T(512)S(1)}, s32[512]{0:T(512)}, u32[]{:S(2)}) copy-start(s32[512]{0:T(512)} %param.13) | copy-start | bytes 6148
  6.2 25.6 %copy-start.18 = (s32[512,15]{0,1:T(8,128)S(1)}, s32[512,15]{0,1:T(8,128)}, u32[]{:S(2)}) copy-start(s32[512,15]{0,1:T(8,128)} %param.14) | copy-start | bytes 92164
  6.2 26.5 %copy-start.15 = (s32[4]{0:T(128)S(1)}, s32[4]{0:T(128)}, u32[]{:S(2)}) copy-start(s32[4]{0:T(128)} %offsets.7) | copy-start | bytes 52
  6.2 1.7 %collective-permute-start.4 = (bf16[1,512,256]{2,1,0:T(8,128)(2,1)S(1)}, bf16[1,512,256]{2,1,0:T(8,128)(2,1)S(1)}, u32[]{:S(2)}, u32[]{:S(2)}) collective-permute-start(bf16[1,512,256]{2,1,0:T(8,128)(2,1)S(1)} %bitcast.13), channel_id=1, source_target_pairs={{0,8},{8,0},{16,24},{24,16},{1,9},{9,1},{17,25},{25,17},{2,10},{10... | collective-permute-start | bytes 786440 | tf_op jit(solution)/shard_map/ppermute | solution.py:245
  7.9 15.7 %copy-start.9 = (bf16[1,512,256]{2,1,0:T(8,128)(2,1)}, bf16[1,512,256]{2,1,0:T(8,128)(2,1)S(1)}, u32[]{:S(2)}) copy-start(bf16[1,512,256]{2,1,0:T(8,128)(2,1)S(1)} %collective-permute-done.4.rest_1_) | copy-start | bytes 786436
  8.8 29.2 %collective-permute-start.5 = (bf16[2,512,256]{2,1,0:T(8,128)(2,1)}, bf16[2,512,256]{2,1,0:T(8,128)(2,1)}, u32[]{:S(2)}, u32[]{:S(2)}) collective-permute-start(bf16[2,512,256]{2,1,0:T(8,128)(2,1)} %pad_maximum_fusion), channel_id=1, source_target_pairs={{0,16},{8,24},{16,0},{24,8},{1,17},{9,25},{17,1},{25,9},{2,18},{10... | collective-permute-start | bytes 1572872 | tf_op jit(solution)/shard_map/ppermute | solution.py:245
  11.6 12.0 %collective-permute-start.2 = (bf16[512,256]{1,0:T(8,128)(2,1)S(1)}, bf16[512,256]{1,0:T(8,128)(2,1)}, u32[]{:S(2)}, u32[]{:S(2)}) collective-permute-start(bf16[512,256]{1,0:T(8,128)(2,1)S(1)} %get-tuple-element.30), channel_id=1, source_target_pairs={{7,0},{0,1},{1,2},{2,3},{3,4},{4,5},{5,6},{6,7},{15,8},{8,9},{9,10... | collective-permute-start | bytes 786440 | tf_op jit(solution)/shard_map/ppermute | solution.py:241
  13.2 10.5 %collective-permute-start = (bf16[512,256]{1,0:T(8,128)(2,1)S(1)}, bf16[512,256]{1,0:T(8,128)(2,1)}, u32[]{:S(2)}, u32[]{:S(2)}) collective-permute-start(bf16[512,256]{1,0:T(8,128)(2,1)S(1)} %get-tuple-element.30), channel_id=1, source_target_pairs={{6,0},{7,1},{0,2},{1,3},{2,4},{3,5},{4,6},{5,7},{14,8},{15,9},{8,1... | collective-permute-start | bytes 786440 | tf_op jit(solution)/shard_map/ppermute | solution.py:241
  23.6 20.9 %collective-permute-start.3 = (bf16[512,256]{1,0:T(8,128)(2,1)}, bf16[512,256]{1,0:T(8,128)(2,1)}, u32[]{:S(2)}, u32[]{:S(2)}) collective-permute-start(bf16[512,256]{1,0:T(8,128)(2,1)} %collective-permute-done.2.block), channel_id=1, source_target_pairs={{6,0},{7,1},{0,2},{1,3},{2,4},{3,5},{4,6},{5,7},{14,8},{15,9},{8,1... | collective-permute-start | bytes 786440 | tf_op jit(solution)/shard_map/ppermute | solution.py:241
  23.6 23.5 %collective-permute-start.1 = (bf16[512,256]{1,0:T(8,128)(2,1)}, bf16[512,256]{1,0:T(8,128)(2,1)}, u32[]{:S(2)}, u32[]{:S(2)}) collective-permute-start(bf16[512,256]{1,0:T(8,128)(2,1)} %collective-permute-done.block), channel_id=1, source_target_pairs={{6,0},{7,1},{0,2},{1,3},{2,4},{3,5},{4,6},{5,7},{14,8},{15,9},{8,1... | collective-permute-start | bytes 786440 | tf_op jit(solution)/shard_map/ppermute | solution.py:241
  30.0 8.0 %copy-start.16 = (s32[4,128]{1,0:T(4,128)S(1)}, s32[4,128]{1,0:T(4,128)}, u32[]{:S(2)}) copy-start(s32[4,128]{1,0:T(4,128)} %requests.1) | copy-start | bytes 6148
  32.6 5.4 %copy-start.10 = (bf16[1,512,256]{2,1,0:T(8,128)(2,1)S(1)}, bf16[1,512,256]{2,1,0:T(8,128)(2,1)}, u32[]{:S(2)}) copy-start(bf16[1,512,256]{2,1,0:T(8,128)(2,1)} %copy-done.9) | copy-start | bytes 786436
  37.9 9.2 %copy-start.3 = (bf16[512,1024]{1,0:T(8,128)(2,1)S(1)}, bf16[512,1024]{1,0:T(8,128)(2,1)}, u32[]{:S(2)}) copy-start(bf16[512,1024]{1,0:T(8,128)(2,1)} %copy-done.1) | copy-start | bytes 3145732
  38.0 9.2 %copy-start.12 = (bf16[1024,512]{1,0:T(8,128)(2,1)S(1)}, bf16[1024,512]{1,0:T(8,128)(2,1)}, u32[]{:S(2)}) copy-start(bf16[1024,512]{1,0:T(8,128)(2,1)} %copy-done.11) | copy-start | bytes 3145732
  38.0 9.2 %copy-start.14 = (bf16[1024,512]{1,0:T(8,128)(2,1)S(1)}, bf16[1024,512]{1,0:T(8,128)(2,1)}, u32[]{:S(2)}) copy-start(bf16[1024,512]{1,0:T(8,128)(2,1)} %copy-done.13) | copy-start | bytes 3145732
  52.8 3.3 %collective-permute-start.6 = (s16[2,256,1408]{2,1,0:T(8,128)(2,1)S(1)}, s16[2,256,1408]{2,1,0:T(8,128)(2,1)S(1)}, u32[]{:S(2)}, u32[]{:S(2)}) collective-permute-start(s16[2,256,1408]{2,1,0:T(8,128)(2,1)S(1)} %get-tuple-element.19), channel_id=1, source_target_pairs={{0,8},{8,0},{16,24},{24,16},{1,9},{9,1},{17,25},{25,17},{2,10},{10... | collective-permute-start | bytes 4325384 | tf_op jit(solution)/shard_map/ppermute | solution.py:245
  57.6 18.5 %collective-permute-start.7 = (s16[1,256,1408]{2,1,0:T(8,128)(2,1)}, s16[1,256,1408]{2,1,0:T(8,128)(2,1)}, u32[]{:S(2)}, u32[]{:S(2)}) collective-permute-start(s16[1,256,1408]{2,1,0:T(8,128)(2,1)} %get-tuple-element.21), channel_id=1, source_target_pairs={{0,16},{8,24},{16,0},{24,8},{1,17},{9,25},{17,1},{25,9},{2,18},{10... | collective-permute-start | bytes 2162696 | tf_op jit(solution)/shard_map/ppermute | solution.py:245
  77.9 10.7 %collective-permute-start.8 = (s16[32,1408]{1,0:T(8,128)(2,1)S(1)}, s16[32,1408]{1,0:T(8,128)(2,1)S(1)}, u32[]{:S(2)}, u32[]{:S(2)}) collective-permute-start(s16[32,1408]{1,0:T(8,128)(2,1)S(1)} %get-tuple-element.23), channel_id=1, source_target_pairs={{0,1},{1,0},{2,3},{3,2},{4,5},{5,4},{6,7},{7,6},{8,9},{9,8},{10,11... | collective-permute-start | bytes 270344 | tf_op jit(solution)/shard_map/ppermute | solution.py:245
  82.8 9.7 %collective-permute-start.9 = (s16[32,1408]{1,0:T(8,128)(2,1)S(1)}, s16[32,1408]{1,0:T(8,128)(2,1)S(1)}, u32[]{:S(2)}, u32[]{:S(2)}) collective-permute-start(s16[32,1408]{1,0:T(8,128)(2,1)S(1)} %get-tuple-element.24), channel_id=1, source_target_pairs={{0,2},{1,3},{2,0},{3,1},{4,6},{5,7},{6,4},{7,5},{8,10},{9,11},{10,... | collective-permute-start | bytes 270344 | tf_op jit(solution)/shard_map/ppermute | solution.py:245
  84.2 8.3 %collective-permute-start.10 = (s16[32,1408]{1,0:T(8,128)(2,1)S(1)}, s16[32,1408]{1,0:T(8,128)(2,1)S(1)}, u32[]{:S(2)}, u32[]{:S(2)}) collective-permute-start(s16[32,1408]{1,0:T(8,128)(2,1)S(1)} %get-tuple-element.25), channel_id=1, source_target_pairs={{0,3},{1,2},{2,1},{3,0},{4,7},{5,6},{6,5},{7,4},{8,11},{9,10},{10,... | collective-permute-start | bytes 270344 | tf_op jit(solution)/shard_map/ppermute | solution.py:245
  84.3 8.2 %collective-permute-start.11 = (s16[32,1408]{1,0:T(8,128)(2,1)S(1)}, s16[32,1408]{1,0:T(8,128)(2,1)S(1)}, u32[]{:S(2)}, u32[]{:S(2)}) collective-permute-start(s16[32,1408]{1,0:T(8,128)(2,1)S(1)} %get-tuple-element.26), channel_id=1, source_target_pairs={{0,4},{1,5},{2,6},{3,7},{4,0},{5,1},{6,2},{7,3},{8,12},{9,13},{10,... | collective-permute-start | bytes 270344 | tf_op jit(solution)/shard_map/ppermute | solution.py:245
  87.2 14.2 %collective-permute-start.12 = (s16[32,1408]{1,0:T(8,128)(2,1)S(1)}, s16[32,1408]{1,0:T(8,128)(2,1)S(1)}, u32[]{:S(2)}, u32[]{:S(2)}) collective-permute-start(s16[32,1408]{1,0:T(8,128)(2,1)S(1)} %get-tuple-element.27), channel_id=1, source_target_pairs={{0,5},{1,4},{2,7},{3,6},{4,1},{5,0},{6,3},{7,2},{8,13},{9,12},{10,... | collective-permute-start | bytes 270344 | tf_op jit(solution)/shard_map/ppermute | solution.py:245
  88.7 12.7 %collective-permute-start.13 = (s16[32,1408]{1,0:T(8,128)(2,1)S(1)}, s16[32,1408]{1,0:T(8,128)(2,1)S(1)}, u32[]{:S(2)}, u32[]{:S(2)}) collective-permute-start(s16[32,1408]{1,0:T(8,128)(2,1)S(1)} %get-tuple-element.28), channel_id=1, source_target_pairs={{0,6},{1,7},{2,4},{3,5},{4,2},{5,3},{6,0},{7,1},{8,14},{9,15},{10,... | collective-permute-start | bytes 270344 | tf_op jit(solution)/shard_map/ppermute | solution.py:245
  92.5 8.9 %collective-permute-start.14 = (s16[32,1408]{1,0:T(8,128)(2,1)S(1)}, s16[32,1408]{1,0:T(8,128)(2,1)S(1)}, u32[]{:S(2)}, u32[]{:S(2)}) collective-permute-start(s16[32,1408]{1,0:T(8,128)(2,1)S(1)} %get-tuple-element.29), channel_id=1, source_target_pairs={{0,7},{1,6},{2,5},{3,4},{4,3},{5,2},{6,1},{7,0},{8,15},{9,14},{10,... | collective-permute-start | bytes 270344 | tf_op jit(solution)/shard_map/ppermute | solution.py:245
  101.7 9.3 %collective-permute-start.21 = (s16[32,1408]{1,0:T(8,128)(2,1)S(1)}, s16[32,1408]{1,0:T(8,128)(2,1)S(1)}, u32[]{:S(2)}, u32[]{:S(2)}) collective-permute-start(s16[32,1408]{1,0:T(8,128)(2,1)S(1)} %shard_map.103.refs_0_), channel_id=1, source_target_pairs={{0,7},{1,6},{2,5},{3,4},{4,3},{5,2},{6,1},{7,0},{8,15},{9,14},{10,... | collective-permute-start | bytes 270344 | tf_op jit(solution)/shard_map/ppermute | solution.py:245
  104.3 13.0 %collective-permute-start.20 = (s16[32,1408]{1,0:T(8,128)(2,1)S(1)}, s16[32,1408]{1,0:T(8,128)(2,1)S(1)}, u32[]{:S(2)}, u32[]{:S(2)}) collective-permute-start(s16[32,1408]{1,0:T(8,128)(2,1)S(1)} %shard_map.103.refs_0_), channel_id=1, source_target_pairs={{0,6},{1,7},{2,4},{3,5},{4,2},{5,3},{6,0},{7,1},{8,14},{9,15},{10,... | collective-permute-start | bytes 270344 | tf_op jit(solution)/shard_map/ppermute | solution.py:245
  105.5 15.0 %collective-permute-start.19 = (s16[32,1408]{1,0:T(8,128)(2,1)S(1)}, s16[32,1408]{1,0:T(8,128)(2,1)S(1)}, u32[]{:S(2)}, u32[]{:S(2)}) collective-permute-start(s16[32,1408]{1,0:T(8,128)(2,1)S(1)} %shard_map.103.refs_0_), channel_id=1, source_target_pairs={{0,5},{1,4},{2,7},{3,6},{4,1},{5,0},{6,3},{7,2},{8,13},{9,12},{10,... | collective-permute-start | bytes 270344 | tf_op jit(solution)/shard_map/ppermute | solution.py:245
  109.2 11.4 %collective-permute-start.18 = (s16[32,1408]{1,0:T(8,128)(2,1)S(1)}, s16[32,1408]{1,0:T(8,128)(2,1)S(1)}, u32[]{:S(2)}, u32[]{:S(2)}) collective-permute-start(s16[32,1408]{1,0:T(8,128)(2,1)S(1)} %shard_map.103.refs_0_), channel_id=1, source_target_pairs={{0,4},{1,5},{2,6},{3,7},{4,0},{5,1},{6,2},{7,3},{8,12},{9,13},{10,... | collective-permute-start | bytes 270344 | tf_op jit(solution)/shard_map/ppermute | solution.py:245
  109.4 11.2 %collective-permute-start.17 = (s16[32,1408]{1,0:T(8,128)(2,1)S(1)}, s16[32,1408]{1,0:T(8,128)(2,1)S(1)}, u32[]{:S(2)}, u32[]{:S(2)}) collective-permute-start(s16[32,1408]{1,0:T(8,128)(2,1)S(1)} %shard_map.103.refs_0_), channel_id=1, source_target_pairs={{0,3},{1,2},{2,1},{3,0},{4,7},{5,6},{6,5},{7,4},{8,11},{9,10},{10,... | collective-permute-start | bytes 270344 | tf_op jit(solution)/shard_map/ppermute | solution.py:245
  111.0 10.5 %collective-permute-start.16 = (s16[32,1408]{1,0:T(8,128)(2,1)S(1)}, s16[32,1408]{1,0:T(8,128)(2,1)S(1)}, u32[]{:S(2)}, u32[]{:S(2)}) collective-permute-start(s16[32,1408]{1,0:T(8,128)(2,1)S(1)} %shard_map.103.refs_0_), channel_id=1, source_target_pairs={{0,2},{1,3},{2,0},{3,1},{4,6},{5,7},{6,4},{7,5},{8,10},{9,11},{10,... | collective-permute-start | bytes 270344 | tf_op jit(solution)/shard_map/ppermute | solution.py:245
  117.3 4.5 %collective-permute-start.15 = (s16[32,1408]{1,0:T(8,128)(2,1)S(1)}, s16[32,1408]{1,0:T(8,128)(2,1)S(1)}, u32[]{:S(2)}, u32[]{:S(2)}) collective-permute-start(s16[32,1408]{1,0:T(8,128)(2,1)S(1)} %shard_map.103.refs_0_), channel_id=1, source_target_pairs={{0,1},{1,0},{2,3},{3,2},{4,5},{5,4},{6,7},{7,6},{8,9},{9,8},{10,11... | collective-permute-start | bytes 270344 | tf_op jit(solution)/shard_map/ppermute | solution.py:245
  (10 other events, 27.3 us)

commit v3 on v2

--- a/solution.py
+++ b/solution.py
@@ -7,6 +7,7 @@
 from jax.experimental import pallas as pl
 from jax.experimental.pallas import tpu as pltpu
 from jax.sharding import PartitionSpec as P
+
 
 NEGW = 8
 TILE = 128
@@ -53,22 +54,32 @@
     return out
 
 
-def norms(z):
+def distances(y, z):
+    rows = y.shape[0]
+    gram = dot_nt(jnp.concatenate(parts(y, 3), axis=0), z)
+    gram = gram[:rows] + gram[rows : 2 * rows] + gram[2 * rows :]
     zf = z.astype(F32)
-    ones = jnp.ones((8, z.shape[1]), BF16)
-    return sum(dot_nt(ones, part) for part in parts(zf * zf, 2))[0:1]
-
-
-def distances(y, z, z_norm):
-    gram = sum(dot_nt(part, z) for part in parts(y, 3))
+    z_norm = jnp.broadcast_to(jnp.sum(zf * zf, axis=1, keepdims=True), (z.shape[0], rows)).T
     y_norm = jnp.sum(y * y, axis=1, keepdims=True)
     return jnp.maximum(y_norm + z_norm - 2.0 * gram, 0.0) * (1.0 / z.shape[1])
 
 
 def pull(y, z, coef):
+    rows = y.shape[0]
     high, low = parts(coef, 2)
     total = jnp.sum(high.astype(F32) + low.astype(F32), axis=1, keepdims=True)
-    return y * total - (dot(high, z) + dot(low, z))
+    mixed = dot(jnp.concatenate([high, low], axis=0), z)
+    return y * total - (mixed[:rows] + mixed[rows:])
+
+
+def forward_body(inputs, w_first, w_second, hidden, codes, sent):
+    tile = min(inputs.shape[0], 2 * TILE)
+    for at in range(0, inputs.shape[0], tile):
+        rows_of = slice(at, at + tile)
+        hidden[rows_of, :] = jnp.maximum(dot(inputs[rows_of, :], w_first[...]), 0.0).astype(BF16)
+        value = dot(hidden[rows_of, :], w_second[...])
+        codes[rows_of, :] = value
+        sent[rows_of, :] = value.astype(BF16)
 
 
 def flip_body(inputs, hidden, inputs_t, hidden_t):
@@ -76,32 +87,39 @@
     hidden_t[...] = hidden[...].T
 
 
-def near_body(me, codes, requests, slots, counts, edges, grad, *rest):
+def weight_body(slots, counts, edges, out, total):
+    tile = 32
+    rows = slots.shape[1]
+    for at in range(0, out.shape[1], tile):
+        place = at + lax.broadcasted_iota(jnp.int32, (tile, rows), 0)
+        weight = jnp.zeros((tile, rows), F32)
+        for k in range(slots.shape[0]):
+            live = jnp.where(k < counts[...], edges[k : k + 1, :].astype(F32), 0.0)
+            weight = weight + jnp.where(place == slots[k : k + 1, :], live, 0.0)
+        total[at : at + tile, :] = weight.astype(BF16)
+    out[...] = total[...].T
+
+
+def near_body(me, codes, requests, weight, grad, *rest):
     out, table = rest[-2:]
     cap = requests.shape[1]
-    place = 0
-    for ref in rest[:-2]:
-        for j in range(ref.shape[0]):
-            rows = ref.shape[1]
-            asked = requests[pl.ds(me[0] ^ place, 1), :]
-            hot = lax.broadcasted_iota(jnp.int32, (rows, cap), 0) == asked
-            hot = jnp.where(hot, 1.0, 0.0).astype(BF16).T
-            at = pl.ds(pl.multiple_of((me[0] ^ place) * cap, cap), cap)
-            table[at, :] = dot(hot, ref[j]).astype(BF16)
-            place += 1
-    z = table[...]
-    z_norm = norms(z)
+    for place, block in enumerate(rest[:-2]):
+        asked = requests[pl.ds(me[0] ^ place, 1), :]
+        hot = lax.broadcasted_iota(jnp.int32, (block.shape[0], cap), 0) == asked
+        hot = jnp.where(hot, 1.0, 0.0).astype(BF16).T
+        at = pl.ds(pl.multiple_of((me[0] ^ place) * cap, cap), cap)
+        table[at, :] = dot(hot, block[...]).astype(BF16)
     tile = min(codes.shape[0], TILE)
-    column = lax.broadcasted_iota(jnp.int32, (tile, z.shape[0]), 1)
+    part = 2 * tile
     for at in range(0, codes.shape[0], tile):
         rows_of = slice(at, at + tile)
         y = codes[rows_of, :]
-        weight = jnp.zeros((tile, z.shape[0]), F32)
-        live = lax.broadcasted_iota(jnp.int32, (tile, edges.shape[1]), 1) < counts[rows_of, :]
-        live = jnp.where(live, edges[rows_of, :].astype(F32), 0.0)
-        for k in range(slots.shape[1]):
-            weight = weight + jnp.where(column == slots[rows_of, k : k + 1], live[:, k : k + 1], 0.0)
-        out[rows_of, :] = grad[rows_of, :] + pull(y, z, weight / (1.0 + distances(y, z, z_norm)))
+        total = grad[rows_of, :]
+        for low in range(0, table.shape[0], part):
+            z = table[low : low + part, :]
+            strength = weight[rows_of, low : low + part].astype(F32)
+            total = total + pull(y, z, strength / (1.0 + distances(y, z)))
+        out[rows_of, :] = total
 
 
 def repulsion(codes, block, offset, twice, put):
@@ -119,7 +137,7 @@
     for at in range(0, rows, tile):
         y = codes[at : at + tile, :]
         z = twice[pl.ds(pl.multiple_of(start + at, PACK), window), :]
-        dist = distances(y, z, norms(z))
+        dist = distances(y, z)
         onep = 1.0 + dist
         coef = jnp.where(band, 1.0 / (onep * (dist + 0.1 * onep)), 0.0)
         put(slice(at, at + tile), pull(y, z, coef))
@@ -144,7 +162,7 @@
     for piece in (one, two):
         top = jnp.maximum(jnp.max(jnp.abs(piece), axis=1, keepdims=True), TINY)
         code = jnp.ceil(jnp.log2(top) * STEPS)
-        unit = FULL / jnp.exp2(code * (1.0 / STEPS))
+        unit = FULL * jnp.exp2(code * (-1.0 / STEPS))
         quanta.append(jnp.round(piece * unit))
         codes.append(code)
     lane = lax.broadcasted_iota(jnp.int32, (one.shape[0], LANES), 1)
@@ -260,24 +278,38 @@
     assert powers, "axis sizes"
     wide, narrow = lax.axis_index("wide"), lax.axis_index("narrow")
     w_id, n_id = (index.reshape(1).astype(jnp.int32) for index in (wide, narrow))
-    pre = jnp.dot(inputs, w_first, preferred_element_type=F32)
-    hidden = jnp.maximum(pre, 0.0).astype(BF16)
-    codes = jnp.dot(hidden, w_second, preferred_element_type=F32)
-    sent = codes.astype(BF16)
+    hidden, codes, sent = call(
+        forward_body,
+        (
+            jax.ShapeDtypeStruct((rows, hid), BF16),
+            jax.ShapeDtypeStruct((rows, width), F32),
+            jax.ShapeDtypeStruct((rows, width), BF16),
+        ),
+        0,
+        3,
+    )(inputs, w_first, w_second)
     steps = offsets.shape[0]
     blocks = []
     for step in range(steps):
-        blocks.append(from_behind(sent if step < 2 else blocks[step - 2], "narrow", min(step, 1) + 1))
-    near = [sent[None]]
+        source = sent if step < 2 else blocks[step - 2]
+        blocks.append(from_behind(source, "narrow", min(step, 1) + 1))
+    near = [sent]
     for bit in bits(peers):
-        moved = near[0] if bit == 1 else jnp.concatenate(near)
-        near.append(swapped(moved, "wide", bit))
+        near += [swapped(block, "wide", bit) for block in near]
     inputs_t, hidden_t = call(
         flip_body,
         (jax.ShapeDtypeStruct((din, rows), BF16), jax.ShapeDtypeStruct((hid, rows), BF16)),
         0,
         2,
     )(inputs, hidden)
+    size = peers * requests.shape[1]
+    weight = call(
+        weight_body,
+        jax.ShapeDtypeStruct((rows, size), BF16),
+        0,
+        3,
+        [pltpu.VMEM((size, rows), BF16)],
+    )(slots.T, counts[None], edge_weight.T)
     like = jax.ShapeDtypeStruct(codes.shape, F32)
     twice = twice_of(rows, width)
 
@@ -290,9 +322,8 @@
     early = max(steps - 2, 1)
     for step in range(early):
         grad = far(step, grad)
-    table = pltpu.VMEM((peers * requests.shape[1], width), BF16)
-    grad = call(near_body, like, 1, 6 + len(near), [table])(
-        w_id, codes, requests, slots, counts[:, None], edge_weight, grad, *near
+    grad = call(near_body, like, 1, 4 + len(near), [pltpu.VMEM((size, width), BF16)])(
+        w_id, codes, requests, weight, grad, *near
     )
     for step in range(early, steps - 1):
         grad = far(step, grad)

time: 123 us -> 107 us (0.87)
  local copies, waits for them, and re-layouts: 9.62 us -> 3.89 us
  Pallas kernels: 25.4 us -> 21.8 us
  matrix products: 2.93 us -> 0 us
  waiting for transfers between devices: 44.6 us -> 41.7 us
    unnamed x42 -> x20, local copies, waits for them, and re-layouts: 8.75 us -> 3.89 us
    dot_general x2 -> x0, matrix products: 2.93 us -> none  [the longest x1 2.47 us: shards(): pre = jnp.dot(inputs, w_first, preferred_element_type=F32)]
    ppermute x18 -> x19, waiting for transfers between devices: 35.7 us -> 33.5 us  [swapped(): lax.ppermute(block, axis, [(i, i ^ bit) for i in range(lax.axis_size(axis...]
    pallas_call x3, Pallas kernels: 7.9 us -> 6.16 us  [far(): call(body, like, 1, 2 + len(given), [twice])]
    ppermute x18 -> x19, starting transfers between devices: 34.2 us -> 32.7 us  [swapped(): lax.ppermute(block, axis, [(i, i ^ bit) for i in range(lax.axis_size(axis...]
    pallas_call x1 -> x3, Pallas kernels: 6.48 us -> 7.09 us  [the longest x1 3.62 us: shards(): call(near_body, like, 1, 4 + len(near), [pltpu.VMEM((size, width), BF16)])]
  transfers between devices with their start and end apart: 22 -> 23, of which waited for: 9 -> 10; matrix products, arithmetic and copies ran while one was open for 2% -> 0% of each run, Pallas kernels for 12% -> 11%
where the time goes in v3:
time: 107 us; the launch traced here: 106 us
  waiting for transfers between devices  41.7 us (39%)
  starting transfers between devices  38.2 us (36%)
  Pallas kernels  21.8 us (20%)
  local copies, waits for them, and re-layouts  3.89 us (4%)
    ppermute x19, waiting for transfers between devices, swapped(): lax.ppermute(block, axis, [(i, i ^ bit) for i in range(lax.axis_size(axis...  33.5 us
    ppermute x19, starting transfers between devices, swapped(): lax.ppermute(block, axis, [(i, i ^ bit) for i in range(lax.axis_size(axis...  32.7 us
    ppermute x4, waiting for transfers between devices, from_behind(): return lax.ppermute(block, axis, route)  8.21 us
    pallas_call x3, Pallas kernels, far(): call(body, like, 1, 2 + len(given), [twice])  6.16 us
    ppermute x4, starting transfers between devices, from_behind(): return lax.ppermute(block, axis, route)  5.52 us
    pallas_call x1, Pallas kernels, shards(): call(body, halves, 2, 7, scratch)  5.05 us
    unnamed x20, local copies, waits for them, and re-layouts  3.89 us
    pallas_call x1, Pallas kernels, shards(): call(near_body, like, 1, 4 + len(near), [pltpu.VMEM((size, width), BF16)])  3.62 us
  transfers between devices with their start and end apart: 23, of which 10 were waited for; matrix products, arithmetic and copies ran while one was open for 0% of the time, Pallas kernels for 11%

profile of v3, /device:TPU:0, one launch (start us, length us, event | category | flops | bytes accessed | tf_op | source)
XLA Modules:
  0.0 106.5 jit_solution(5420910910616981841)
XLA Ops:
  0.6 1.2 %copy-done = bf16[512,1024]{1,0:T(8,128)(2,1)S(1)} copy-done((bf16[512,1024]{1,0:T(8,128)(2,1)S(1)}, bf16[512,1024]{1,0:T(8,128)(2,1)}, u32[]{:S(2)}) %copy-start) | copy-done | bytes 1048600
  1.9 1.6 %copy-done.2 = bf16[1024,1024]{1,0:T(8,128)(2,1)S(1)} copy-done((bf16[1024,1024]{1,0:T(8,128)(2,1)S(1)}, bf16[1024,1024]{1,0:T(8,128)(2,1)}, u32[]{:S(2)}) %copy-start.2) | copy-done | bytes 2097176
  3.4 1.0 copy-done.3
  4.5 1.6 %shard_map.95 = (bf16[512,1024]{1,0:T(8,128)(2,1)S(1)}, f32[512,256]{1,0:T(8,128)S(1)}, bf16[512,256]{1,0:T(8,128)(2,1)S(1)}) custom-call(bf16[512,1024]{1,0:T(8,128)(2,1)S(1)} %copy-done, bf16[1024,1024]{1,0:T(8,128)(2,1)S(1)} %copy-done.2, bf16[1024,256]{1,0:T(8,128)(2,1)S(1)} %copy-done.3), custom_call_target="tpu_custom_call" | custom-call | tf_op jit(solution)/shard_map/pallas_call | solution.py:281
  6.7 2.6 %collective-permute-start.2 = (bf16[512,256]{1,0:T(8,128)(2,1)S(1)}, bf16[512,256]{1,0:T(8,128)(2,1)S(1)}, u32[]{:S(2)}, u32[]{:S(2)}) collective-permute-start(bf16[512,256]{1,0:T(8,128)(2,1)S(1)} %get-tuple-element.20.rest_0_), channel_id=1, source_target_pairs={{7,0},{0,1},{1,2},{2,3},{3,4},{4,5},{5,6},{6,7},{15,8},{8,9},{9,10... | collective-permute-start | bytes 786440 | tf_op jit(solution)/shard_map/ppermute | solution.py:259
  9.3 1.6 %collective-permute-start = (bf16[512,256]{1,0:T(8,128)(2,1)S(1)}, bf16[512,256]{1,0:T(8,128)(2,1)}, u32[]{:S(2)}, u32[]{:S(2)}) collective-permute-start(bf16[512,256]{1,0:T(8,128)(2,1)S(1)} %get-tuple-element.20.rest_0_), channel_id=1, source_target_pairs={{6,0},{7,1},{0,2},{1,3},{2,4},{3,5},{4,6},{5,7},{14,8},{15,9},{8,1... | collective-permute-start | bytes 786440 | tf_op jit(solution)/shard_map/ppermute | solution.py:259
  10.9 1.5 %collective-permute-start.5 = (bf16[512,256]{1,0:T(8,128)(2,1)S(1)}, bf16[512,256]{1,0:T(8,128)(2,1)}, u32[]{:S(2)}, u32[]{:S(2)}) collective-permute-start(bf16[512,256]{1,0:T(8,128)(2,1)S(1)} %get-tuple-element.20.rest_0_), channel_id=1, source_target_pairs={{0,16},{8,24},{16,0},{24,8},{1,17},{9,25},{17,1},{25,9},{2,18},{10... | collective-permute-start | bytes 786440 | tf_op jit(solution)/shard_map/ppermute | solution.py:263
  12.9 6.6 %collective-permute-done.2.block = bf16[512,256]{1,0:T(8,128)(2,1)S(1)} collective-permute-done((bf16[512,256]{1,0:T(8,128)(2,1)S(1)}, bf16[512,256]{1,0:T(8,128)(2,1)S(1)}, u32[]{:S(2)}, u32[]{:S(2)}) %collective-permute-start.2) | collective-permute-done | bytes 262176 | tf_op jit(solution)/shard_map/ppermute | solution.py:259
  19.7 1.4 %collective-permute-start.1 = (bf16[512,256]{1,0:T(8,128)(2,1)}, bf16[512,256]{1,0:T(8,128)(2,1)}, u32[]{:S(2)}, u32[]{:S(2)}) collective-permute-start(bf16[512,256]{1,0:T(8,128)(2,1)} %collective-permute-done.block), channel_id=1, source_target_pairs={{6,0},{7,1},{0,2},{1,3},{2,4},{3,5},{4,6},{5,7},{14,8},{15,9},{8,1... | collective-permute-start | bytes 786440 | tf_op jit(solution)/shard_map/ppermute | solution.py:259
  21.7 1.8 %shard_map.96.weight = bf16[512,512]{1,0:T(8,128)(2,1)S(1)} custom-call(s32[15,512]{1,0:T(8,128)S(1)} %bitcast.13, s32[1,512]{1,0:T(1,128)S(1)} %bitcast.15, s32[15,512]{1,0:T(8,128)S(1)} %bitcast.14), custom_call_target="tpu_custom_call" | custom-call | tf_op jit(solution)/shard_map/pallas_call | solution.py:306
  23.5 1.8 %shard_map.97.rest_0_ = f32[512,256]{1,0:T(8,128)S(1)} custom-call(s32[4]{0:T(128)S(1)} %copy-done.7, f32[512,256]{1,0:T(8,128)S(1)} %get-tuple-element.19.codes, bf16[512,256]{1,0:T(8,128)(2,1)S(1)} %collective-permute-done.2.block), custom_call_target="tpu_custom_call" | custom-call | tf_op jit(solution)/shard_map/pallas_call | solution.py:319
  25.3 2.2 %shard_map.98.grad = f32[512,256]{1,0:T(8,128)S(1)} custom-call(s32[4]{0:T(128)S(1)} %copy-done.7, f32[512,256]{1,0:T(8,128)S(1)} %get-tuple-element.19.codes, bf16[512,256]{1,0:T(8,128)(2,1)} %collective-permute-done.block, f32[512,256]{1,0:T(8,128)S(1)} %shard_map.97.rest_0_), custom_call_target="tpu_custom_call" | custom-call | tf_op jit(solution)/shard_map/pallas_call | solution.py:319
  27.5 3.6 %shard_map.99.rest_0_ = f32[512,256]{1,0:T(8,128)S(1)} custom-call(s32[1]{0:T(128)} %bitcast.1.me, f32[512,256]{1,0:T(8,128)S(1)} %get-tuple-element.19.codes, s32[4,128]{1,0:T(4,128)S(1)} %copy-done.9, bf16[512,512]{1,0:T(8,128)(2,1)S(1)} %shard_map.96.weight, f32[512,256]{1,0:T(8,128)S(1)} %shard_map.98.grad, ...), custom_call_target="tpu_custom_call" | custom-call | tf_op jit(solution)/shard_map/pallas_call | solution.py:325
  31.1 2.2 %shard_map.100.grad = f32[512,256]{1,0:T(8,128)S(1)} custom-call(s32[4]{0:T(128)S(1)} %copy-done.7, f32[512,256]{1,0:T(8,128)S(1)} %get-tuple-element.19.codes, bf16[512,256]{1,0:T(8,128)(2,1)} %collective-permute-done.3.block, f32[512,256]{1,0:T(8,128)S(1)} %shard_map.99.rest_0_), custom_call_target="tpu_custom_call" | custom-call | tf_op jit(solution)/shard_map/pallas_call | solution.py:319
  33.4 1.5 %collective-permute-done.1.block = bf16[512,256]{1,0:T(8,128)(2,1)} collective-permute-done((bf16[512,256]{1,0:T(8,128)(2,1)}, bf16[512,256]{1,0:T(8,128)(2,1)}, u32[]{:S(2)}, u32[]{:S(2)}) %collective-permute-start.1) | collective-permute-done | bytes 262176 | tf_op jit(solution)/shard_map/ppermute | solution.py:259
  34.9 5.1 %shard_map.102 = (f32[2,256,1280]{2,1,0:T(8,128)S(1)}, s16[2,256,1408]{2,1,0:T(8,128)(2,1)S(1)}) custom-call(s32[4]{0:T(128)S(1)} %copy-done.7, s32[1]{0:T(128)S(6)} %select_n.19.bit, f32[512,256]{1,0:T(8,128)S(1)} %get-tuple-element.19.codes, bf16[512,256]{1,0:T(8,128)(2,1)} %collective-permute-done.1.block, f32[512,256]{1,0:T(8,128)S(1)} %shard_map.100.grad, ...), custom_call_target="tpu_custom_call" | custom-call | tf_op jit(solution)/shard_map/pallas_call | solution.py:362
  40.0 3.2 %collective-permute-done.7 = s16[2,256,1408]{2,1,0:T(8,128)(2,1)S(1)} collective-permute-done((s16[2,256,1408]{2,1,0:T(8,128)(2,1)S(1)}, s16[2,256,1408]{2,1,0:T(8,128)(2,1)S(1)}, u32[]{:S(2)}, u32[]{:S(2)}) %collective-permute-start.7) | collective-permute-done | bytes 1441824 | tf_op jit(solution)/shard_map/ppermute | solution.py:263
  43.9 1.4 %collective-permute-start.8 = (s16[1,256,1408]{2,1,0:T(8,128)(2,1)S(1)}, s16[1,256,1408]{2,1,0:T(8,128)(2,1)S(1)}, u32[]{:S(2)}, u32[]{:S(2)}) collective-permute-start(s16[1,256,1408]{2,1,0:T(8,128)(2,1)S(1)} %get-tuple-element.27), channel_id=1, source_target_pairs={{0,16},{8,24},{16,0},{24,8},{1,17},{9,25},{17,1},{25,9},{2,18},{10... | collective-permute-start | bytes 2162696 | tf_op jit(solution)/shard_map/ppermute | solution.py:263
  45.3 16.9 %collective-permute-done.8 = s16[1,256,1408]{2,1,0:T(8,128)(2,1)S(1)} collective-permute-done((s16[1,256,1408]{2,1,0:T(8,128)(2,1)S(1)}, s16[1,256,1408]{2,1,0:T(8,128)(2,1)S(1)}, u32[]{:S(2)}, u32[]{:S(2)}) %collective-permute-start.8) | collective-permute-done | bytes 720928 | tf_op jit(solution)/shard_map/ppermute | solution.py:263
  62.8 3.4 %collective-permute-start.9 = (s16[32,1408]{1,0:T(8,128)(2,1)S(1)}, s16[32,1408]{1,0:T(8,128)(2,1)S(1)}, u32[]{:S(2)}, u32[]{:S(2)}) collective-permute-start(s16[32,1408]{1,0:T(8,128)(2,1)S(1)} %get-tuple-element.29), channel_id=1, source_target_pairs={{0,1},{1,0},{2,3},{3,2},{4,5},{5,4},{6,7},{7,6},{8,9},{9,8},{10,11... | collective-permute-start | bytes 270344 | tf_op jit(solution)/shard_map/ppermute | solution.py:263
  66.2 1.5 %collective-permute-start.10 = (s16[32,1408]{1,0:T(8,128)(2,1)S(1)}, s16[32,1408]{1,0:T(8,128)(2,1)S(1)}, u32[]{:S(2)}, u32[]{:S(2)}) collective-permute-start(s16[32,1408]{1,0:T(8,128)(2,1)S(1)} %get-tuple-element.30), channel_id=1, source_target_pairs={{0,2},{1,3},{2,0},{3,1},{4,6},{5,7},{6,4},{7,5},{8,10},{9,11},{10,... | collective-permute-start | bytes 270344 | tf_op jit(solution)/shard_map/ppermute | solution.py:263
  67.8 2.8 %collective-permute-start.12 = (s16[32,1408]{1,0:T(8,128)(2,1)S(1)}, s16[32,1408]{1,0:T(8,128)(2,1)S(1)}, u32[]{:S(2)}, u32[]{:S(2)}) collective-permute-start(s16[32,1408]{1,0:T(8,128)(2,1)S(1)} %get-tuple-element.32), channel_id=1, source_target_pairs={{0,4},{1,5},{2,6},{3,7},{4,0},{5,1},{6,2},{7,3},{8,12},{9,13},{10,... | collective-permute-start | bytes 270344 | tf_op jit(solution)/shard_map/ppermute | solution.py:263
  70.6 1.5 %collective-permute-start.13 = (s16[32,1408]{1,0:T(8,128)(2,1)S(1)}, s16[32,1408]{1,0:T(8,128)(2,1)S(1)}, u32[]{:S(2)}, u32[]{:S(2)}) collective-permute-start(s16[32,1408]{1,0:T(8,128)(2,1)S(1)} %get-tuple-element.33), channel_id=1, source_target_pairs={{0,5},{1,4},{2,7},{3,6},{4,1},{5,0},{6,3},{7,2},{8,13},{9,12},{10,... | collective-permute-start | bytes 270344 | tf_op jit(solution)/shard_map/ppermute | solution.py:263
  72.1 3.8 %collective-permute-start.14 = (s16[32,1408]{1,0:T(8,128)(2,1)S(1)}, s16[32,1408]{1,0:T(8,128)(2,1)S(1)}, u32[]{:S(2)}, u32[]{:S(2)}) collective-permute-start(s16[32,1408]{1,0:T(8,128)(2,1)S(1)} %get-tuple-element.34), channel_id=1, source_target_pairs={{0,6},{1,7},{2,4},{3,5},{4,2},{5,3},{6,0},{7,1},{8,14},{9,15},{10,... | collective-permute-start | bytes 270344 | tf_op jit(solution)/shard_map/ppermute | solution.py:263
  75.9 8.9 %collective-permute-done.13.refs_4_ = s16[32,1408]{1,0:T(8,128)(2,1)S(1)} collective-permute-done((s16[32,1408]{1,0:T(8,128)(2,1)S(1)}, s16[32,1408]{1,0:T(8,128)(2,1)S(1)}, u32[]{:S(2)}, u32[]{:S(2)}) %collective-permute-start.13) | collective-permute-done | bytes 90144 | tf_op jit(solution)/shard_map/ppermute | solution.py:263
  85.1 2.6 %collective-permute-start.22 = (s16[32,1408]{1,0:T(8,128)(2,1)S(1)}, s16[32,1408]{1,0:T(8,128)(2,1)S(1)}, u32[]{:S(2)}, u32[]{:S(2)}) collective-permute-start(s16[32,1408]{1,0:T(8,128)(2,1)S(1)} %shard_map.105.refs_0_), channel_id=1, source_target_pairs={{0,7},{1,6},{2,5},{3,4},{4,3},{5,2},{6,1},{7,0},{8,15},{9,14},{10,... | collective-permute-start | bytes 270344 | tf_op jit(solution)/shard_map/ppermute | solution.py:263
  87.7 1.2 %collective-permute-start.21 = (s16[32,1408]{1,0:T(8,128)(2,1)S(1)}, s16[32,1408]{1,0:T(8,128)(2,1)S(1)}, u32[]{:S(2)}, u32[]{:S(2)}) collective-permute-start(s16[32,1408]{1,0:T(8,128)(2,1)S(1)} %shard_map.105.refs_0_), channel_id=1, source_target_pairs={{0,6},{1,7},{2,4},{3,5},{4,2},{5,3},{6,0},{7,1},{8,14},{9,15},{10,... | collective-permute-start | bytes 270344 | tf_op jit(solution)/shard_map/ppermute | solution.py:263
  88.9 3.7 %collective-permute-start.20 = (s16[32,1408]{1,0:T(8,128)(2,1)S(1)}, s16[32,1408]{1,0:T(8,128)(2,1)S(1)}, u32[]{:S(2)}, u32[]{:S(2)}) collective-permute-start(s16[32,1408]{1,0:T(8,128)(2,1)S(1)} %shard_map.105.refs_0_), channel_id=1, source_target_pairs={{0,5},{1,4},{2,7},{3,6},{4,1},{5,0},{6,3},{7,2},{8,13},{9,12},{10,... | collective-permute-start | bytes 270344 | tf_op jit(solution)/shard_map/ppermute | solution.py:263
  92.8 1.5 %collective-permute-start.18 = (s16[32,1408]{1,0:T(8,128)(2,1)S(1)}, s16[32,1408]{1,0:T(8,128)(2,1)S(1)}, u32[]{:S(2)}, u32[]{:S(2)}) collective-permute-start(s16[32,1408]{1,0:T(8,128)(2,1)S(1)} %shard_map.105.refs_0_), channel_id=1, source_target_pairs={{0,3},{1,2},{2,1},{3,0},{4,7},{5,6},{6,5},{7,4},{8,11},{9,10},{10,... | collective-permute-start | bytes 270344 | tf_op jit(solution)/shard_map/ppermute | solution.py:263
  94.4 6.3 %collective-permute-start.17 = (s16[32,1408]{1,0:T(8,128)(2,1)S(1)}, s16[32,1408]{1,0:T(8,128)(2,1)S(1)}, u32[]{:S(2)}, u32[]{:S(2)}) collective-permute-start(s16[32,1408]{1,0:T(8,128)(2,1)S(1)} %shard_map.105.refs_0_), channel_id=1, source_target_pairs={{0,2},{1,3},{2,0},{3,1},{4,6},{5,7},{6,4},{7,5},{8,10},{9,11},{10,... | collective-permute-start | bytes 270344 | tf_op jit(solution)/shard_map/ppermute | solution.py:263
  100.7 3.2 %collective-permute-done.20.refs_5_ = s16[32,1408]{1,0:T(8,128)(2,1)S(1)} collective-permute-done((s16[32,1408]{1,0:T(8,128)(2,1)S(1)}, s16[32,1408]{1,0:T(8,128)(2,1)S(1)}, u32[]{:S(2)}, u32[]{:S(2)}) %collective-permute-start.20) | collective-permute-done | bytes 90144 | tf_op jit(solution)/shard_map/ppermute | solution.py:263
  105.3 1.2 %shard_map.106 = (f32[256,1024]{1,0:T(8,128)}, f32[256,256]{1,0:T(8,128)}) custom-call(s32[1]{0:T(128)} %bitcast.me, s16[32,1408]{1,0:T(8,128)(2,1)S(1)} %shard_map.105.refs_0_, s16[32,1408]{1,0:T(8,128)(2,1)S(1)} %collective-permute-done.16.refs_1_, s16[32,1408]{1,0:T(8,128)(2,1)S(1)} %collective-permute-done.17.refs_2_, ...), custom_call_target="tpu_custom_call" | custom-call | tf_op jit(solution)/shard_map/pallas_call | solution.py:376
  (46 shorter events, 5.3 us)
Async XLA Ops:
  0.6 1.2 %copy-start = (bf16[512,1024]{1,0:T(8,128)(2,1)S(1)}, bf16[512,1024]{1,0:T(8,128)(2,1)}, u32[]{:S(2)}) copy-start(bf16[512,1024]{1,0:T(8,128)(2,1)} %inputs.3) | copy-start | bytes 3145732
  1.9 1.6 %copy-start.2 = (bf16[1024,1024]{1,0:T(8,128)(2,1)S(1)}, bf16[1024,1024]{1,0:T(8,128)(2,1)}, u32[]{:S(2)}) copy-start(bf16[1024,1024]{1,0:T(8,128)(2,1)} %w_first.1) | copy-start | bytes 6291460
  4.5 16.5 %copy-start.1 = (bf16[512,1024]{1,0:T(8,128)(2,1)S(1)}, bf16[512,1024]{1,0:T(8,128)(2,1)}, u32[]{:S(2)}) copy-start(bf16[512,1024]{1,0:T(8,128)(2,1)} %inputs.3) | copy-start | bytes 3145732
  6.1 15.5 %copy-start.5 = (s32[512,15]{0,1:T(8,128)S(1)}, s32[512,15]{0,1:T(8,128)}, u32[]{:S(2)}) copy-start(s32[512,15]{0,1:T(8,128)} %param.12) | copy-start | bytes 92164
  6.2 15.5 %copy-start.6 = (s32[512,15]{0,1:T(8,128)S(1)}, s32[512,15]{0,1:T(8,128)}, u32[]{:S(2)}) copy-start(s32[512,15]{0,1:T(8,128)} %param.14) | copy-start | bytes 92164
  6.2 15.5 %copy-start.8 = (s32[512]{0:T(512)S(1)}, s32[512]{0:T(512)}, u32[]{:S(2)}) copy-start(s32[512]{0:T(512)} %param.13) | copy-start | bytes 6148
  6.2 17.3 %copy-start.7 = (s32[4]{0:T(128)S(1)}, s32[4]{0:T(128)}, u32[]{:S(2)}) copy-start(s32[4]{0:T(128)} %offsets.7) | copy-start | bytes 52
  6.2 6.2 %collective-permute-start.4 = (bf16[512,256]{1,0:T(8,128)(2,1)S(1)}, bf16[512,256]{1,0:T(8,128)(2,1)S(1)}, u32[]{:S(2)}, u32[]{:S(2)}) collective-permute-start(bf16[512,256]{1,0:T(8,128)(2,1)S(1)} %get-tuple-element.20.rest_0_), channel_id=1, source_target_pairs={{0,8},{8,0},{16,24},{24,16},{1,9},{9,1},{17,25},{25,17},{2,10},{10... | collective-permute-start | bytes 786440 | tf_op jit(solution)/shard_map/ppermute | solution.py:263
  6.7 12.8 %collective-permute-start.2 = (bf16[512,256]{1,0:T(8,128)(2,1)S(1)}, bf16[512,256]{1,0:T(8,128)(2,1)S(1)}, u32[]{:S(2)}, u32[]{:S(2)}) collective-permute-start(bf16[512,256]{1,0:T(8,128)(2,1)S(1)} %get-tuple-element.20.rest_0_), channel_id=1, source_target_pairs={{7,0},{0,1},{1,2},{2,3},{3,4},{4,5},{5,6},{6,7},{15,8},{8,9},{9,10... | collective-permute-start | bytes 786440 | tf_op jit(solution)/shard_map/ppermute | solution.py:259
  9.3 10.3 %collective-permute-start = (bf16[512,256]{1,0:T(8,128)(2,1)S(1)}, bf16[512,256]{1,0:T(8,128)(2,1)}, u32[]{:S(2)}, u32[]{:S(2)}) collective-permute-start(bf16[512,256]{1,0:T(8,128)(2,1)S(1)} %get-tuple-element.20.rest_0_), channel_id=1, source_target_pairs={{6,0},{7,1},{0,2},{1,3},{2,4},{3,5},{4,6},{5,7},{14,8},{15,9},{8,1... | collective-permute-start | bytes 786440 | tf_op jit(solution)/shard_map/ppermute | solution.py:259
  10.9 16.6 %collective-permute-start.5 = (bf16[512,256]{1,0:T(8,128)(2,1)S(1)}, bf16[512,256]{1,0:T(8,128)(2,1)}, u32[]{:S(2)}, u32[]{:S(2)}) collective-permute-start(bf16[512,256]{1,0:T(8,128)(2,1)S(1)} %get-tuple-element.20.rest_0_), channel_id=1, source_target_pairs={{0,16},{8,24},{16,0},{24,8},{1,17},{9,25},{17,1},{25,9},{2,18},{10... | collective-permute-start | bytes 786440 | tf_op jit(solution)/shard_map/ppermute | solution.py:263
  12.4 15.1 %collective-permute-start.6 = (bf16[512,256]{1,0:T(8,128)(2,1)S(1)}, bf16[512,256]{1,0:T(8,128)(2,1)}, u32[]{:S(2)}, u32[]{:S(2)}) collective-permute-start(bf16[512,256]{1,0:T(8,128)(2,1)S(1)} %collective-permute-done.4.rest_1_), channel_id=1, source_target_pairs={{0,16},{8,24},{16,0},{24,8},{1,17},{9,25},{17,1},{25,9},{2,18},{10... | collective-permute-start | bytes 786440 | tf_op jit(solution)/shard_map/ppermute | solution.py:263
  19.5 11.6 %collective-permute-start.3 = (bf16[512,256]{1,0:T(8,128)(2,1)S(1)}, bf16[512,256]{1,0:T(8,128)(2,1)}, u32[]{:S(2)}, u32[]{:S(2)}) collective-permute-start(bf16[512,256]{1,0:T(8,128)(2,1)S(1)} %collective-permute-done.2.block), channel_id=1, source_target_pairs={{6,0},{7,1},{0,2},{1,3},{2,4},{3,5},{4,6},{5,7},{14,8},{15,9},{8,1... | collective-permute-start | bytes 786440 | tf_op jit(solution)/shard_map/ppermute | solution.py:259
  19.7 15.2 %collective-permute-start.1 = (bf16[512,256]{1,0:T(8,128)(2,1)}, bf16[512,256]{1,0:T(8,128)(2,1)}, u32[]{:S(2)}, u32[]{:S(2)}) collective-permute-start(bf16[512,256]{1,0:T(8,128)(2,1)} %collective-permute-done.block), channel_id=1, source_target_pairs={{6,0},{7,1},{0,2},{1,3},{2,4},{3,5},{4,6},{5,7},{14,8},{15,9},{8,1... | collective-permute-start | bytes 786440 | tf_op jit(solution)/shard_map/ppermute | solution.py:259
  23.5 4.0 %copy-start.9 = (s32[4,128]{1,0:T(4,128)S(1)}, s32[4,128]{1,0:T(4,128)}, u32[]{:S(2)}) copy-start(s32[4,128]{1,0:T(4,128)} %requests.1) | copy-start | bytes 6148
  31.1 3.7 %copy-start.4 = (bf16[1024,256]{1,0:T(8,128)(2,1)S(1)}, bf16[1024,256]{1,0:T(8,128)(2,1)}, u32[]{:S(2)}) copy-start(bf16[1024,256]{1,0:T(8,128)(2,1)} %w_second.3) | copy-start | bytes 1572868
  39.9 3.3 %collective-permute-start.7 = (s16[2,256,1408]{2,1,0:T(8,128)(2,1)S(1)}, s16[2,256,1408]{2,1,0:T(8,128)(2,1)S(1)}, u32[]{:S(2)}, u32[]{:S(2)}) collective-permute-start(s16[2,256,1408]{2,1,0:T(8,128)(2,1)S(1)} %get-tuple-element.25), channel_id=1, source_target_pairs={{0,8},{8,0},{16,24},{24,16},{1,9},{9,1},{17,25},{25,17},{2,10},{10... | collective-permute-start | bytes 4325384 | tf_op jit(solution)/shard_map/ppermute | solution.py:263
  43.9 18.2 %collective-permute-start.8 = (s16[1,256,1408]{2,1,0:T(8,128)(2,1)S(1)}, s16[1,256,1408]{2,1,0:T(8,128)(2,1)S(1)}, u32[]{:S(2)}, u32[]{:S(2)}) collective-permute-start(s16[1,256,1408]{2,1,0:T(8,128)(2,1)S(1)} %get-tuple-element.27), channel_id=1, source_target_pairs={{0,16},{8,24},{16,0},{24,8},{1,17},{9,25},{17,1},{25,9},{2,18},{10... | collective-permute-start | bytes 2162696 | tf_op jit(solution)/shard_map/ppermute | solution.py:263
  62.8 9.2 %collective-permute-start.9 = (s16[32,1408]{1,0:T(8,128)(2,1)S(1)}, s16[32,1408]{1,0:T(8,128)(2,1)S(1)}, u32[]{:S(2)}, u32[]{:S(2)}) collective-permute-start(s16[32,1408]{1,0:T(8,128)(2,1)S(1)} %get-tuple-element.29), channel_id=1, source_target_pairs={{0,1},{1,0},{2,3},{3,2},{4,5},{5,4},{6,7},{7,6},{8,9},{9,8},{10,11... | collective-permute-start | bytes 270344 | tf_op jit(solution)/shard_map/ppermute | solution.py:263
  66.2 9.7 %collective-permute-start.10 = (s16[32,1408]{1,0:T(8,128)(2,1)S(1)}, s16[32,1408]{1,0:T(8,128)(2,1)S(1)}, u32[]{:S(2)}, u32[]{:S(2)}) collective-permute-start(s16[32,1408]{1,0:T(8,128)(2,1)S(1)} %get-tuple-element.30), channel_id=1, source_target_pairs={{0,2},{1,3},{2,0},{3,1},{4,6},{5,7},{6,4},{7,5},{8,10},{9,11},{10,... | collective-permute-start | bytes 270344 | tf_op jit(solution)/shard_map/ppermute | solution.py:263
  67.7 8.2 %collective-permute-start.11 = (s16[32,1408]{1,0:T(8,128)(2,1)S(1)}, s16[32,1408]{1,0:T(8,128)(2,1)S(1)}, u32[]{:S(2)}, u32[]{:S(2)}) collective-permute-start(s16[32,1408]{1,0:T(8,128)(2,1)S(1)} %get-tuple-element.31), channel_id=1, source_target_pairs={{0,3},{1,2},{2,1},{3,0},{4,7},{5,6},{6,5},{7,4},{8,11},{9,10},{10,... | collective-permute-start | bytes 270344 | tf_op jit(solution)/shard_map/ppermute | solution.py:263
  67.8 8.2 %collective-permute-start.12 = (s16[32,1408]{1,0:T(8,128)(2,1)S(1)}, s16[32,1408]{1,0:T(8,128)(2,1)S(1)}, u32[]{:S(2)}, u32[]{:S(2)}) collective-permute-start(s16[32,1408]{1,0:T(8,128)(2,1)S(1)} %get-tuple-element.32), channel_id=1, source_target_pairs={{0,4},{1,5},{2,6},{3,7},{4,0},{5,1},{6,2},{7,3},{8,12},{9,13},{10,... | collective-permute-start | bytes 270344 | tf_op jit(solution)/shard_map/ppermute | solution.py:263
  70.6 14.2 %collective-permute-start.13 = (s16[32,1408]{1,0:T(8,128)(2,1)S(1)}, s16[32,1408]{1,0:T(8,128)(2,1)S(1)}, u32[]{:S(2)}, u32[]{:S(2)}) collective-permute-start(s16[32,1408]{1,0:T(8,128)(2,1)S(1)} %get-tuple-element.33), channel_id=1, source_target_pairs={{0,5},{1,4},{2,7},{3,6},{4,1},{5,0},{6,3},{7,2},{8,13},{9,12},{10,... | collective-permute-start | bytes 270344 | tf_op jit(solution)/shard_map/ppermute | solution.py:263
  72.1 12.7 %collective-permute-start.14 = (s16[32,1408]{1,0:T(8,128)(2,1)S(1)}, s16[32,1408]{1,0:T(8,128)(2,1)S(1)}, u32[]{:S(2)}, u32[]{:S(2)}) collective-permute-start(s16[32,1408]{1,0:T(8,128)(2,1)S(1)} %get-tuple-element.34), channel_id=1, source_target_pairs={{0,6},{1,7},{2,4},{3,5},{4,2},{5,3},{6,0},{7,1},{8,14},{9,15},{10,... | collective-permute-start | bytes 270344 | tf_op jit(solution)/shard_map/ppermute | solution.py:263
  75.9 8.9 %collective-permute-start.15 = (s16[32,1408]{1,0:T(8,128)(2,1)S(1)}, s16[32,1408]{1,0:T(8,128)(2,1)S(1)}, u32[]{:S(2)}, u32[]{:S(2)}) collective-permute-start(s16[32,1408]{1,0:T(8,128)(2,1)S(1)} %get-tuple-element.35), channel_id=1, source_target_pairs={{0,7},{1,6},{2,5},{3,4},{4,3},{5,2},{6,1},{7,0},{8,15},{9,14},{10,... | collective-permute-start | bytes 270344 | tf_op jit(solution)/shard_map/ppermute | solution.py:263
  85.1 9.3 %collective-permute-start.22 = (s16[32,1408]{1,0:T(8,128)(2,1)S(1)}, s16[32,1408]{1,0:T(8,128)(2,1)S(1)}, u32[]{:S(2)}, u32[]{:S(2)}) collective-permute-start(s16[32,1408]{1,0:T(8,128)(2,1)S(1)} %shard_map.105.refs_0_), channel_id=1, source_target_pairs={{0,7},{1,6},{2,5},{3,4},{4,3},{5,2},{6,1},{7,0},{8,15},{9,14},{10,... | collective-permute-start | bytes 270344 | tf_op jit(solution)/shard_map/ppermute | solution.py:263
  87.7 13.0 %collective-permute-start.21 = (s16[32,1408]{1,0:T(8,128)(2,1)S(1)}, s16[32,1408]{1,0:T(8,128)(2,1)S(1)}, u32[]{:S(2)}, u32[]{:S(2)}) collective-permute-start(s16[32,1408]{1,0:T(8,128)(2,1)S(1)} %shard_map.105.refs_0_), channel_id=1, source_target_pairs={{0,6},{1,7},{2,4},{3,5},{4,2},{5,3},{6,0},{7,1},{8,14},{9,15},{10,... | collective-permute-start | bytes 270344 | tf_op jit(solution)/shard_map/ppermute | solution.py:263
  88.9 15.0 %collective-permute-start.20 = (s16[32,1408]{1,0:T(8,128)(2,1)S(1)}, s16[32,1408]{1,0:T(8,128)(2,1)S(1)}, u32[]{:S(2)}, u32[]{:S(2)}) collective-permute-start(s16[32,1408]{1,0:T(8,128)(2,1)S(1)} %shard_map.105.refs_0_), channel_id=1, source_target_pairs={{0,5},{1,4},{2,7},{3,6},{4,1},{5,0},{6,3},{7,2},{8,13},{9,12},{10,... | collective-permute-start | bytes 270344 | tf_op jit(solution)/shard_map/ppermute | solution.py:263
  92.6 11.4 %collective-permute-start.19 = (s16[32,1408]{1,0:T(8,128)(2,1)S(1)}, s16[32,1408]{1,0:T(8,128)(2,1)S(1)}, u32[]{:S(2)}, u32[]{:S(2)}) collective-permute-start(s16[32,1408]{1,0:T(8,128)(2,1)S(1)} %shard_map.105.refs_0_), channel_id=1, source_target_pairs={{0,4},{1,5},{2,6},{3,7},{4,0},{5,1},{6,2},{7,3},{8,12},{9,13},{10,... | collective-permute-start | bytes 270344 | tf_op jit(solution)/shard_map/ppermute | solution.py:263
  92.8 11.2 %collective-permute-start.18 = (s16[32,1408]{1,0:T(8,128)(2,1)S(1)}, s16[32,1408]{1,0:T(8,128)(2,1)S(1)}, u32[]{:S(2)}, u32[]{:S(2)}) collective-permute-start(s16[32,1408]{1,0:T(8,128)(2,1)S(1)} %shard_map.105.refs_0_), channel_id=1, source_target_pairs={{0,3},{1,2},{2,1},{3,0},{4,7},{5,6},{6,5},{7,4},{8,11},{9,10},{10,... | collective-permute-start | bytes 270344 | tf_op jit(solution)/shard_map/ppermute | solution.py:263
  94.4 10.5 %collective-permute-start.17 = (s16[32,1408]{1,0:T(8,128)(2,1)S(1)}, s16[32,1408]{1,0:T(8,128)(2,1)S(1)}, u32[]{:S(2)}, u32[]{:S(2)}) collective-permute-start(s16[32,1408]{1,0:T(8,128)(2,1)S(1)} %shard_map.105.refs_0_), channel_id=1, source_target_pairs={{0,2},{1,3},{2,0},{3,1},{4,6},{5,7},{6,4},{7,5},{8,10},{9,11},{10,... | collective-permute-start | bytes 270344 | tf_op jit(solution)/shard_map/ppermute | solution.py:263
  100.7 4.5 %collective-permute-start.16 = (s16[32,1408]{1,0:T(8,128)(2,1)S(1)}, s16[32,1408]{1,0:T(8,128)(2,1)S(1)}, u32[]{:S(2)}, u32[]{:S(2)}) collective-permute-start(s16[32,1408]{1,0:T(8,128)(2,1)S(1)} %shard_map.105.refs_0_), channel_id=1, source_target_pairs={{0,1},{1,0},{2,3},{3,2},{4,5},{5,4},{6,7},{7,6},{8,9},{9,8},{10,11... | collective-permute-start | bytes 270344 | tf_op jit(solution)/shard_map/ppermute | solution.py:263
  (1 other events, 1.0 us)

commit v4 on v3

--- a/solution.py
+++ b/solution.py
@@ -23,6 +23,10 @@
 I16 = jnp.int16
 VMEM = pl.BlockSpec(memory_space=pltpu.VMEM)
 SMEM = pl.BlockSpec(memory_space=pltpu.SMEM)
+
+
+def digit(me, below, count):
+    return lax.rem(lax.div(me[0], below), count)
 
 
 def call(body, out_shape, n_scalars, n_arrays, scratch=(), mib=16):
@@ -72,14 +76,26 @@
     return y * total - (mixed[:rows] + mixed[rows:])
 
 
-def forward_body(inputs, w_first, w_second, hidden, codes, sent):
-    tile = min(inputs.shape[0], 2 * TILE)
-    for at in range(0, inputs.shape[0], tile):
-        rows_of = slice(at, at + tile)
-        hidden[rows_of, :] = jnp.maximum(dot(inputs[rows_of, :], w_first[...]), 0.0).astype(BF16)
-        value = dot(hidden[rows_of, :], w_second[...])
-        codes[rows_of, :] = value
-        sent[rows_of, :] = value.astype(BF16)
+def forward_body(me, inputs, w_first, w_second, hidden, codes, sent, block, first, second, sems):
+    del me
+    count = first.shape[0]
+    size = first.shape[2]
+    copies = [pltpu.make_async_copy(inputs, block, sems.at[0])]
+    for c in range(count):
+        columns = w_first.at[:, c * size : (c + 1) * size]
+        copies.append(pltpu.make_async_copy(columns, first.at[c], sems.at[c + 1]))
+    copies.append(pltpu.make_async_copy(w_second, second, sems.at[count + 1]))
+    for copy in copies:
+        copy.start()
+    copies[0].wait()
+    for c in range(count):
+        copies[c + 1].wait()
+        columns = slice(c * size, (c + 1) * size)
+        hidden[:, columns] = jnp.maximum(dot(block[...], first[c]), 0.0).astype(BF16)
+    copies[-1].wait()
+    value = dot(hidden[...], second[...])
+    codes[...] = value
+    sent[...] = value.astype(BF16)
 
 
 def flip_body(inputs, hidden, inputs_t, hidden_t):
@@ -100,14 +116,15 @@
     out[...] = total[...].T
 
 
-def near_body(me, codes, requests, weight, grad, *rest):
+def near_body(group, me, codes, requests, weight, grad, *rest):
     out, table = rest[-2:]
     cap = requests.shape[1]
+    wide = digit(me, group, len(rest[:-2]))
     for place, block in enumerate(rest[:-2]):
-        asked = requests[pl.ds(me[0] ^ place, 1), :]
+        asked = requests[pl.ds(wide ^ place, 1), :]
         hot = lax.broadcasted_iota(jnp.int32, (block.shape[0], cap), 0) == asked
         hot = jnp.where(hot, 1.0, 0.0).astype(BF16).T
-        at = pl.ds(pl.multiple_of((me[0] ^ place) * cap, cap), cap)
+        at = pl.ds(pl.multiple_of((wide ^ place) * cap, cap), cap)
         table[at, :] = dot(hot, block[...]).astype(BF16)
     tile = min(codes.shape[0], TILE)
     part = 2 * tile
@@ -186,28 +203,40 @@
 
 def gradients(step, scale, offsets, codes, block, grad, w_second, hidden, twice, dcodes, dpre):
     def put(at, value):
-        small = (scale * (grad[at, :] - value)).astype(BF16)
-        dcodes[at, :] = small
-        wide = dot_nt(small, w_second[...])
-        dpre[at, :] = jnp.where(hidden[at, :] > 0, wide, 0.0).astype(BF16)
+        dcodes[at, :] = (scale * (grad[at, :] - value)).astype(BF16)
 
     repulsion(codes, block, offsets[step], twice, put)
-
-
-def last_body(step, scale, offsets, bit, codes, block, grad, w_second, hidden, inputs_t, hidden_t, keep, send, *scratch):
-    gradients(step, scale, offsets, codes, block, grad, w_second, hidden, *scratch)
-    dcodes, dpre = scratch[1:]
+    size = 2 * LANES
+    for at in range(0, hidden.shape[1], size):
+        columns = slice(at, at + size)
+        wide = dot_nt(dcodes[...], w_second[columns, :])
+        dpre[:, columns] = jnp.where(hidden[:, columns] > 0, wide, 0.0).astype(BF16)
+
+
+def give_body(step, scale, below, offsets, me, codes, block, grad, w_second, hidden, inputs_t, hidden_t, send, dcodes, dpre, twice):
+    gradients(step, scale, offsets, codes, block, grad, w_second, hidden, twice, dcodes, dpre)
+    groups, rows = send.shape[:2]
+    one, two = halves(1 - digit(me, below, 2), groups, rows, dcodes, dpre, inputs_t, hidden_t)
+    for a in range(groups):
+        at = slice(a * rows, (a + 1) * rows)
+        put_encoded(send.at[a], one[at], two[at])
+
+
+def hold_body(below, me, dcodes, dpre, inputs_t, hidden_t, keep):
+    groups, rows = keep.shape[:2]
     first = dpre.shape[1]
-    rows = keep.shape[1]
-    mine = bit[0]
-    for a in range(keep.shape[0]):
-        rows_of = pl.ds(pl.multiple_of((2 * a + 1 - mine) * rows, rows), rows)
-        one, two = dot(inputs_t[rows_of, :], dpre[...]), dot(hidden_t[rows_of, :], dcodes[...])
-        put_encoded(send.at[a], one, two)
-    for a in range(keep.shape[0]):
-        rows_of = pl.ds(pl.multiple_of((2 * a + mine) * rows, rows), rows)
-        keep[a, :, :first] = dot(inputs_t[rows_of, :], dpre[...])
-        keep[a, :, first:] = dot(hidden_t[rows_of, :], dcodes[...])
+    one, two = halves(digit(me, below, 2), groups, rows, dcodes, dpre, inputs_t, hidden_t)
+    for a in range(groups):
+        at = slice(a * rows, (a + 1) * rows)
+        keep[a, :, :first], keep[a, :, first:] = one[at], two[at]
+
+
+def halves(side, groups, rows, dcodes, dpre, inputs_t, hidden_t):
+    def taken(ref):
+        at = [pl.ds(pl.multiple_of((2 * a + side) * rows, rows), rows) for a in range(groups)]
+        return jnp.concatenate([ref[rows_of, :] for rows_of in at], axis=0)
+
+    return dot(taken(inputs_t), dpre[...]), dot(taken(hidden_t), dcodes[...])
 
 
 def last_plain_body(step, scale, offsets, codes, block, grad, w_second, hidden, inputs_t, hidden_t, one, two, *scratch):
@@ -222,35 +251,74 @@
     return held[:, :first] + one, held[:, first:] + two
 
 
-def stage_body(first, bit, held, got, keep, send):
-    mine = bit[0]
+def stage_body(first, below, me, held, got, keep, send):
+    mine = digit(me, below, 2)
     for a in range(held.shape[0]):
         put_encoded(send.at[a], *summed(held.at[a, 1 - mine], got.at[a, 1 - mine], first))
     for a in range(held.shape[0]):
         keep[a, :, :first], keep[a, :, first:] = summed(held.at[a, mine], got.at[a, mine], first)
 
 
-def deal_body(first, me, held, got, keep, *sends):
-    for k in range(1, held.shape[0]):
-        put_encoded(sends[k - 1], *summed(held.at[me[0] ^ k], got.at[me[0] ^ k], first))
-    keep[:, :first], keep[:, first:] = summed(held.at[me[0]], got.at[me[0]], first)
+def part_body(first, belows, me, held, got, p_keep, p_send, q_keep, q_send):
+    mine, here = (digit(me, below, 2) for below in belows)
+    other, there = 1 - mine, 1 - here
+    for j in range(held.shape[2]):
+        for bit in range(2):
+            at = (other, 0, j, bit)
+            put_encoded(p_send.at[j, bit], *summed(held.at[at], got.at[at], first))
+        for block in range(2):
+            at = (block, 1, j, there)
+            put_encoded(q_send.at[block, j], *summed(held.at[at], got.at[at], first))
+    for j in range(held.shape[2]):
+        for bit in range(2):
+            at = (mine, 0, j, bit)
+            p_keep[j, bit, :, :first], p_keep[j, bit, :, first:] = summed(held.at[at], got.at[at], first)
+        for block in range(2):
+            at = (block, 1, j, here)
+            q_keep[block, j, :, :first], q_keep[block, j, :, first:] = summed(held.at[at], got.at[at], first)
+
+
+def cross_body(first, belows, me, p_held, q_held, p_got, q_got, p_keep, q_keep, p_send, q_send):
+    mine, here = (digit(me, below, 2) for below in belows)
+    other, there = 1 - mine, 1 - here
+    for j in range(p_send.shape[0]):
+        put_encoded(p_send.at[j], *summed(p_held.at[j, there], p_got.at[j, there], first))
+        put_encoded(q_send.at[j], *summed(q_held.at[other, j], q_got.at[other, j], first))
+    for j in range(p_send.shape[0]):
+        p_keep[j, :, :first], p_keep[j, :, first:] = summed(p_held.at[j, here], p_got.at[j, here], first)
+        q_keep[j, :, :first], q_keep[j, :, first:] = summed(q_held.at[mine, j], q_got.at[mine, j], first)
+
+
+def deal_body(first, me, p_held, q_held, p_got, q_got, keep, *sends):
+    pairs = ((p_held, p_got), (q_held, q_got))
+    mine = digit(me, 2, p_held.shape[0])
+    for k in range(1, p_held.shape[0]):
+        for half, (held, got) in enumerate(pairs):
+            piece = summed(held.at[mine ^ k], got.at[mine ^ k], first)
+            put_encoded(sends[k - 1].at[half], *piece)
+    for half, (held, got) in enumerate(pairs):
+        keep[half, :, :first], keep[half, :, first:] = summed(held.at[mine], got.at[mine], first)
 
 
 def close_body(first, held, *refs):
-    one, two = held[:, :first], held[:, first:]
-    for got in refs[:-1]:
-        more = decode(got, first, held.shape[1])
-        one, two = one + more[0], two + more[1]
-    put_encoded(refs[-1], one, two)
+    for half in range(held.shape[0]):
+        one, two = held[half, :, :first], held[half, :, first:]
+        for got in refs[:-1]:
+            more = decode(got.at[half], first, held.shape[2])
+            one, two = one + more[0], two + more[1]
+        put_encoded(refs[-1].at[half], one, two)
 
 
 def spread_body(first, me, *refs):
     one, two = refs[-2:]
     width = first + two.shape[1]
+    narrow = digit(me, 1, len(refs[:-2]))
     for place, ref in enumerate(refs[:-2]):
-        rows = ref.shape[0]
-        at = pl.ds(pl.multiple_of((me[0] ^ place) * rows, rows), rows)
-        one[at, :], two[at, :] = decode(ref, first, width)
+        rows = ref.shape[1]
+        for half in range(ref.shape[0]):
+            at = half * (one.shape[0] // 2) + (narrow ^ place) * rows
+            at = pl.ds(pl.multiple_of(at, rows), rows)
+            one[at, :], two[at, :] = decode(ref.at[half], first, width)
 
 
 def from_behind(block, axis, distance):
@@ -276,18 +344,25 @@
     total_rows = rows * peers * group
     powers = peers & (peers - 1) == 0 and group & (group - 1) == 0 and peers > 1 and group > 1
     assert powers, "axis sizes"
-    wide, narrow = lax.axis_index("wide"), lax.axis_index("narrow")
-    w_id, n_id = (index.reshape(1).astype(jnp.int32) for index in (wide, narrow))
-    hidden, codes, sent = call(
+    me = lax.axis_index(("wide", "narrow")).reshape(1).astype(jnp.int32)
+    count = 4 if hid % (4 * LANES) == 0 else 1
+    hidden, codes, sent = pl.pallas_call(
         forward_body,
-        (
+        out_shape=(
             jax.ShapeDtypeStruct((rows, hid), BF16),
             jax.ShapeDtypeStruct((rows, width), F32),
             jax.ShapeDtypeStruct((rows, width), BF16),
         ),
-        0,
-        3,
-    )(inputs, w_first, w_second)
+        in_specs=[SMEM] + [pl.BlockSpec(memory_space=pltpu.HBM)] * 3,
+        out_specs=[VMEM] * 3,
+        scratch_shapes=[
+            pltpu.VMEM(inputs.shape, BF16),
+            pltpu.VMEM((count, din, hid // count), BF16),
+            pltpu.VMEM(w_second.shape, BF16),
+            pltpu.SemaphoreType.DMA((count + 2,)),
+        ],
+        compiler_params=pltpu.CompilerParams(vmem_limit_bytes=16 * 1024 * 1024),
+    )(me, *(pltpu.with_memory_space_constraint(a, pltpu.HBM) for a in (inputs, w_first, w_second)))
     steps = offsets.shape[0]
     blocks = []
     for step in range(steps):
@@ -322,15 +397,15 @@
     early = max(steps - 2, 1)
     for step in range(early):
         grad = far(step, grad)
-    grad = call(near_body, like, 1, 4 + len(near), [pltpu.VMEM((size, width), BF16)])(
-        w_id, codes, requests, weight, grad, *near
+    grad = call(functools.partial(near_body, group), like, 1, 4 + len(near), [pltpu.VMEM((size, width), BF16)])(
+        me, codes, requests, weight, grad, *near
     )
     for step in range(early, steps - 1):
         grad = far(step, grad)
     scale = 2.0 / (slots.shape[1] * math.sqrt(total_rows))
     chunk = din // (peers * group)
     scratch = [twice, pltpu.VMEM((rows, width), BF16), pltpu.VMEM((rows, hid), BF16)]
-    if din != hid or chunk % 16 or din % (peers * group):
+    if din != hid or chunk % 32 or din % (peers * group) or peers < 4 or group < 4:
         one, two = call(
             functools.partial(last_plain_body, steps - 1, scale),
             (jax.ShapeDtypeStruct((din, hid), F32), jax.ShapeDtypeStruct((hid, width), F32)),
@@ -352,26 +427,61 @@
     def coded(*shape):
         return jax.ShapeDtypeStruct((*shape, full + LANES), I16)
 
-    plan = [(bit, peers // (2 * bit), din // peers) for bit in bits(peers)]
     keep = got = None
-    for bit, groups, lines in plan:
-        side = (w_id // bit) % 2
-        halves = (plain(groups, lines), coded(groups, lines))
+    for bit in bits(peers)[:-1]:
+        below = bit * group
+        groups, lines = peers // (2 * bit), din // peers
         if keep is None:
-            body = functools.partial(last_body, steps - 1, scale)
-            keep, send = call(body, halves, 2, 7, scratch)(
-                offsets, side, codes, blocks[-1], grad, w_second, hidden, inputs_t, hidden_t
-            )
+            send, dcodes, dpre = call(
+                functools.partial(give_body, steps - 1, scale, below),
+                (
+                    coded(groups, lines),
+                    jax.ShapeDtypeStruct((rows, width), BF16),
+                    jax.ShapeDtypeStruct((rows, hid), BF16),
+                ),
+                2,
+                7,
+                [twice],
+            )(offsets, me, codes, blocks[-1], grad, w_second, hidden, inputs_t, hidden_t)
+            keep = call(functools.partial(hold_body, below), plain(groups, lines), 1, 4)(me, dcodes, dpre, inputs_t, hidden_t)
         else:
-            keep, send = call(functools.partial(stage_body, first), halves, 1, 2)(
-                side, keep.reshape(groups, 2, lines, full), got.reshape(groups, 2, lines, full + LANES)
-            )
+            keep, send = call(
+                functools.partial(stage_body, first, below), (plain(groups, lines), coded(groups, lines)), 1, 2
+            )(me, keep.reshape(groups, 2, lines, full), got.reshape(groups, 2, lines, full + LANES))
         got = swapped(send, "wide", bit)
+    last, lines, others = peers // 2, chunk // 2, group // 2
+    belows = (last * group, 1)
+    p_keep, p_send, q_keep, q_send = call(
+        functools.partial(part_body, first, belows),
+        (
+            plain(others, 2, lines),
+            coded(others, 2, lines),
+            plain(2, others, lines),
+            coded(2, others, lines),
+        ),
+        1,
+        2,
+    )(
+        me,
+        keep.reshape(2, 2, others, 2, lines, full),
+        got.reshape(2, 2, others, 2, lines, full + LANES),
+    )
+    p_got, q_got = swapped(p_send, "wide", last), swapped(q_send, "narrow", 1)
+    p_keep, q_keep, p_send, q_send = call(
+        functools.partial(cross_body, first, belows),
+        (plain(others, lines),) * 2 + (coded(others, lines),) * 2,
+        1,
+        4,
+    )(me, p_keep, q_keep, p_got, q_got)
+    p_got, q_got = swapped(p_send, "narrow", 1), swapped(q_send, "wide", last)
     keep, *sends = call(
-        functools.partial(deal_body, first), (plain(chunk),) + (coded(chunk),) * (group - 1), 1, 2
-    )(n_id, keep.reshape(group, chunk, full), got.reshape(group, chunk, full + LANES))
-    gots = [swapped(send, "narrow", k + 1) for k, send in enumerate(sends)]
-    mine = call(functools.partial(close_body, first), coded(chunk), 0, group)(keep, *gots)
+        functools.partial(deal_body, first),
+        (plain(2, lines),) + (coded(2, lines),) * (others - 1),
+        1,
+        4,
+    )(me, p_keep, q_keep, p_got, q_got)
+    gots = [swapped(send, "narrow", 2 * (k + 1)) for k, send in enumerate(sends)]
+    mine = call(functools.partial(close_body, first), coded(2, lines), 0, others)(keep, *gots)
     pieces = [mine] + [swapped(mine, "narrow", k) for k in range(1, group)]
     return call(
         functools.partial(spread_body, first),
@@ -381,7 +491,7 @@
         ),
         1,
         group,
-    )(n_id, *pieces)
+    )(me, *pieces)
 
 
 def solution(mesh):

time: 107 us -> 90.6 us (0.85)
  starting transfers between devices: 38.2 us -> 31.3 us
  waiting for transfers between devices: 41.7 us -> 35.1 us
  local copies, waits for them, and re-layouts: 3.89 us -> 0.04 us
  Pallas kernels: 21.8 us -> 23.1 us
    ppermute x19 -> x18, waiting for transfers between devices: 33.5 us -> 25.2 us  [swapped(): lax.ppermute(block, axis, [(i, i ^ bit) for i in range(lax.axis_size(axis...]
    ppermute x19 -> x18, starting transfers between devices: 32.7 us -> 25.7 us  [swapped(): lax.ppermute(block, axis, [(i, i ^ bit) for i in range(lax.axis_size(axis...]
    unnamed x20 -> x14, local copies, waits for them, and re-layouts: 3.89 us -> 0.04 us
    pallas_call x6 -> x8, Pallas kernels: 12 us -> 14.2 us  [the longest x1 4.71 us: shards(): pl.pallas_call(forward_body, out_shape=(jax.ShapeDtypeStruct((rows, hid),...]
    ppermute x4, waiting for transfers between devices: 8.21 us -> 9.86 us  [from_behind(): return lax.ppermute(block, axis, route)]
  transfers between devices with their start and end apart: 23 -> 22, of which waited for: 10 -> 16; matrix products, arithmetic and copies ran while one was open for 0% -> 0% of each run, Pallas kernels for 11% -> 12%
where the time goes in v4:
time: 90.6 us; the launch traced here: 90.4 us
  waiting for transfers between devices  35.1 us (39%)
  starting transfers between devices  31.3 us (35%)
  Pallas kernels  23.1 us (25%)
    ppermute x18, starting transfers between devices, swapped(): lax.ppermute(block, axis, [(i, i ^ bit) for i in range(lax.axis_size(axis...  25.7 us
    ppermute x18, waiting for transfers between devices, swapped(): lax.ppermute(block, axis, [(i, i ^ bit) for i in range(lax.axis_size(axis...  25.2 us
    ppermute x4, waiting for transfers between devices, from_behind(): return lax.ppermute(block, axis, route)  9.86 us
    ppermute x4, starting transfers between devices, from_behind(): return lax.ppermute(block, axis, route)  5.62 us
    pallas_call x3, Pallas kernels, far(): call(body, like, 1, 2 + len(given), [twice])  5.28 us
    pallas_call x1, Pallas kernels, shards(): pl.pallas_call(forward_body, out_shape=(jax.ShapeDtypeStruct((rows, hid),...  4.71 us
    pallas_call x1, Pallas kernels, shards(): call(functools.partial(give_body, steps - 1, scale, below), (coded(groups...  3.12 us
    pallas_call x1, Pallas kernels, shards(): call(functools.partial(near_body, group), like, 1, 4 + len(near), [pltpu....  2.63 us
  transfers between devices with their start and end apart: 22, of which 16 were waited for; matrix products, arithmetic and copies ran while one was open for 0% of the time, Pallas kernels for 12%

profile of v4, /device:TPU:0, one launch (start us, length us, event | category | flops | bytes accessed | tf_op | source)
XLA Modules:
  0.0 90.4 jit_solution(199716964209497455)
XLA Ops:
  0.7 4.7 %shard_map.95 = (bf16[512,1024]{1,0:T(8,128)(2,1)S(1)}, f32[512,256]{1,0:T(8,128)S(1)}, bf16[512,256]{1,0:T(8,128)(2,1)S(1)}) custom-call(s32[1]{0:T(128)} %bitcast.me, bf16[512,1024]{1,0:T(8,128)(2,1)} %inputs.3, bf16[1024,1024]{1,0:T(8,128)(2,1)} %w_first.1, bf16[1024,256]{1,0:T(8,128)(2,1)} %w_second.3), custom_call_target="tpu_custom_call" | custom-call | tf_op jit(solution)/shard_map/pallas_call | solution.py:349
  6.0 2.6 %collective-permute-start.2 = (bf16[512,256]{1,0:T(8,128)(2,1)S(1)}, bf16[512,256]{1,0:T(8,128)(2,1)S(1)}, u32[]{:S(2)}, u32[]{:S(2)}) collective-permute-start(bf16[512,256]{1,0:T(8,128)(2,1)S(1)} %get-tuple-element.23.rest_0_), channel_id=1, source_target_pairs={{7,0},{0,1},{1,2},{2,3},{3,4},{4,5},{5,6},{6,7},{15,8},{8,9},{9,10... | collective-permute-start | bytes 786440 | tf_op jit(solution)/shard_map/ppermute | solution.py:327
  8.5 1.6 %collective-permute-start = (bf16[512,256]{1,0:T(8,128)(2,1)S(1)}, bf16[512,256]{1,0:T(8,128)(2,1)S(1)}, u32[]{:S(2)}, u32[]{:S(2)}) collective-permute-start(bf16[512,256]{1,0:T(8,128)(2,1)S(1)} %get-tuple-element.23.rest_0_), channel_id=1, source_target_pairs={{6,0},{7,1},{0,2},{1,3},{2,4},{3,5},{4,6},{5,7},{14,8},{15,9},{8,1... | collective-permute-start | bytes 786440 | tf_op jit(solution)/shard_map/ppermute | solution.py:327
  10.1 1.5 %collective-permute-start.5 = (bf16[512,256]{1,0:T(8,128)(2,1)S(1)}, bf16[512,256]{1,0:T(8,128)(2,1)S(1)}, u32[]{:S(2)}, u32[]{:S(2)}) collective-permute-start(bf16[512,256]{1,0:T(8,128)(2,1)S(1)} %get-tuple-element.23.rest_0_), channel_id=1, source_target_pairs={{0,16},{8,24},{16,0},{24,8},{1,17},{9,25},{17,1},{25,9},{2,18},{10... | collective-permute-start | bytes 786440 | tf_op jit(solution)/shard_map/ppermute | solution.py:331
  12.1 6.6 %collective-permute-done.2.block = bf16[512,256]{1,0:T(8,128)(2,1)S(1)} collective-permute-done((bf16[512,256]{1,0:T(8,128)(2,1)S(1)}, bf16[512,256]{1,0:T(8,128)(2,1)S(1)}, u32[]{:S(2)}, u32[]{:S(2)}) %collective-permute-start.2) | collective-permute-done | bytes 262176 | tf_op jit(solution)/shard_map/ppermute | solution.py:327
  18.8 1.5 %collective-permute-start.1 = (bf16[512,256]{1,0:T(8,128)(2,1)S(1)}, bf16[512,256]{1,0:T(8,128)(2,1)S(1)}, u32[]{:S(2)}, u32[]{:S(2)}) collective-permute-start(bf16[512,256]{1,0:T(8,128)(2,1)S(1)} %collective-permute-done.block), channel_id=1, source_target_pairs={{6,0},{7,1},{0,2},{1,3},{2,4},{3,5},{4,6},{5,7},{14,8},{15,9},{8,1... | collective-permute-start | bytes 786440 | tf_op jit(solution)/shard_map/ppermute | solution.py:327
  20.9 1.8 %shard_map.96.weight = bf16[512,512]{1,0:T(8,128)(2,1)S(1)} custom-call(s32[15,512]{1,0:T(8,128)S(1)} %bitcast.8, s32[1,512]{1,0:T(1,128)S(1)} %bitcast.10, s32[15,512]{1,0:T(8,128)S(1)} %bitcast.9), custom_call_target="tpu_custom_call" | custom-call | tf_op jit(solution)/shard_map/pallas_call | solution.py:381
  22.7 1.8 %shard_map.97.rest_0_ = f32[512,256]{1,0:T(8,128)S(1)} custom-call(s32[4]{0:T(128)S(1)} %copy-done.4, f32[512,256]{1,0:T(8,128)S(1)} %get-tuple-element.22.codes, bf16[512,256]{1,0:T(8,128)(2,1)S(1)} %collective-permute-done.2.block), custom_call_target="tpu_custom_call" | custom-call | tf_op jit(solution)/shard_map/pallas_call | solution.py:394
  24.5 1.8 %shard_map.98.grad = f32[512,256]{1,0:T(8,128)S(1)} custom-call(s32[4]{0:T(128)S(1)} %copy-done.4, f32[512,256]{1,0:T(8,128)S(1)} %get-tuple-element.22.codes, bf16[512,256]{1,0:T(8,128)(2,1)S(1)} %collective-permute-done.block, f32[512,256]{1,0:T(8,128)S(1)} %shard_map.97.rest_0_), custom_call_target="tpu_custom_call" | custom-call | tf_op jit(solution)/shard_map/pallas_call | solution.py:394
  26.3 2.6 %shard_map.99.rest_0_ = f32[512,256]{1,0:T(8,128)S(1)} custom-call(s32[1]{0:T(128)} %bitcast.me, f32[512,256]{1,0:T(8,128)S(1)} %get-tuple-element.22.codes, s32[4,128]{1,0:T(4,128)S(1)} %copy-done.6, bf16[512,512]{1,0:T(8,128)(2,1)S(1)} %shard_map.96.weight, f32[512,256]{1,0:T(8,128)S(1)} %shard_map.98.grad, ...), custom_call_target="tpu_custom_call" | custom-call | tf_op jit(solution)/shard_map/pallas_call | solution.py:400
  29.7 1.8 %shard_map.100.grad = f32[512,256]{1,0:T(8,128)S(1)} custom-call(s32[4]{0:T(128)S(1)} %copy-done.4, f32[512,256]{1,0:T(8,128)S(1)} %get-tuple-element.22.codes, bf16[512,256]{1,0:T(8,128)(2,1)S(1)} %collective-permute-done.3.block, f32[512,256]{1,0:T(8,128)S(1)} %shard_map.99.rest_0_), custom_call_target="tpu_custom_call" | custom-call | tf_op jit(solution)/shard_map/pallas_call | solution.py:394
  31.5 2.5 %collective-permute-done.1.block = bf16[512,256]{1,0:T(8,128)(2,1)S(1)} collective-permute-done((bf16[512,256]{1,0:T(8,128)(2,1)S(1)}, bf16[512,256]{1,0:T(8,128)(2,1)S(1)}, u32[]{:S(2)}, u32[]{:S(2)}) %collective-permute-start.1) | collective-permute-done | bytes 262176 | tf_op jit(solution)/shard_map/ppermute | solution.py:327
  34.0 3.1 %shard_map.102 = (s16[2,256,1408]{2,1,0:T(8,128)(2,1)S(1)}, bf16[512,256]{1,0:T(8,128)(2,1)S(1)}, bf16[512,1024]{1,0:T(8,128)(2,1)S(1)}) custom-call(s32[4]{0:T(128)S(1)} %copy-done.4, s32[1]{0:T(128)} %bitcast.me, f32[512,256]{1,0:T(8,128)S(1)} %get-tuple-element.22.codes, bf16[512,256]{1,0:T(8,128)(2,1)S(1)} %collective-permute-done.1.block, ...), custom_call_target="tpu_custom_call" | custom-call | tf_op jit(solution)/shard_map/pallas_call | solution.py:435
  38.0 2.3 %collective-permute-done.7 = s16[2,256,1408]{2,1,0:T(8,128)(2,1)S(1)} collective-permute-done((s16[2,256,1408]{2,1,0:T(8,128)(2,1)S(1)}, s16[2,256,1408]{2,1,0:T(8,128)(2,1)S(1)}, u32[]{:S(2)}, u32[]{:S(2)}) %collective-permute-start.7) | collective-permute-done | bytes 1441824 | tf_op jit(solution)/shard_map/ppermute | solution.py:331
  40.4 1.6 %shard_map.104 = (f32[4,2,16,1280]{3,2,1,0:T(8,128)S(1)}, s16[4,2,16,1408]{3,2,1,0:T(8,128)(2,1)S(1)}, f32[2,4,16,1280]{3,2,1,0:T(8,128)S(1)}, s16[2,4,16,1408]{3,2,1,0:T(8,128)(2,1)S(1)}) custom-call(s32[1]{0:T(128)} %bitcast.me, f32[2,2,4,2,16,1280]{5,4,3,2,1,0:T(8,128)S(1)} %bitcast.6, s16[2,2,4,2,16,1408]{5,4,3,2,1,0:T(8,128)(2,1)S(1)} %bitcast.7), custom_call_target="tpu_custom_call" | custom-call | tf_op jit(solution)/shard_map/pallas_call | solution.py:454
  42.0 1.4 %collective-permute-start.8 = (s16[4,2,16,1408]{3,2,1,0:T(8,128)(2,1)S(1)}, s16[4,2,16,1408]{3,2,1,0:T(8,128)(2,1)S(1)}, u32[]{:S(2)}, u32[]{:S(2)}) collective-permute-start(s16[4,2,16,1408]{3,2,1,0:T(8,128)(2,1)S(1)} %get-tuple-element.32), channel_id=1, source_target_pairs={{0,16},{8,24},{16,0},{24,8},{1,17},{9,25},{17,1},{25,9},{2,18},{10... | collective-permute-start | bytes 1081352 | tf_op jit(solution)/shard_map/ppermute | solution.py:331
  43.4 2.1 %collective-permute-start.9 = (s16[2,4,16,1408]{3,2,1,0:T(8,128)(2,1)S(1)}, s16[2,4,16,1408]{3,2,1,0:T(8,128)(2,1)S(1)}, u32[]{:S(2)}, u32[]{:S(2)}) collective-permute-start(s16[2,4,16,1408]{3,2,1,0:T(8,128)(2,1)S(1)} %get-tuple-element.33), channel_id=1, source_target_pairs={{0,1},{1,0},{2,3},{3,2},{4,5},{5,4},{6,7},{7,6},{8,9},{9,8},{10,11... | collective-permute-start | bytes 1081352 | tf_op jit(solution)/shard_map/ppermute | solution.py:331
  45.4 7.0 %collective-permute-done.8.p_got = s16[4,2,16,1408]{3,2,1,0:T(8,128)(2,1)S(1)} collective-permute-done((s16[4,2,16,1408]{3,2,1,0:T(8,128)(2,1)S(1)}, s16[4,2,16,1408]{3,2,1,0:T(8,128)(2,1)S(1)}, u32[]{:S(2)}, u32[]{:S(2)}) %collective-permute-start.8) | collective-permute-done | bytes 360480 | tf_op jit(solution)/shard_map/ppermute | solution.py:331
  52.5 1.4 %collective-permute-done.9.q_got = s16[2,4,16,1408]{3,2,1,0:T(8,128)(2,1)S(1)} collective-permute-done((s16[2,4,16,1408]{3,2,1,0:T(8,128)(2,1)S(1)}, s16[2,4,16,1408]{3,2,1,0:T(8,128)(2,1)S(1)}, u32[]{:S(2)}, u32[]{:S(2)}) %collective-permute-start.9) | collective-permute-done | bytes 360480 | tf_op jit(solution)/shard_map/ppermute | solution.py:331
  54.6 1.8 %collective-permute-start.10 = (s16[4,16,1408]{2,1,0:T(8,128)(2,1)S(1)}, s16[4,16,1408]{2,1,0:T(8,128)(2,1)S(1)}, u32[]{:S(2)}, u32[]{:S(2)}) collective-permute-start(s16[4,16,1408]{2,1,0:T(8,128)(2,1)S(1)} %get-tuple-element.36), channel_id=1, source_target_pairs={{0,1},{1,0},{2,3},{3,2},{4,5},{5,4},{6,7},{7,6},{8,9},{9,8},{10,11... | collective-permute-start | bytes 540680 | tf_op jit(solution)/shard_map/ppermute | solution.py:331
  57.0 3.5 %collective-permute-done.10.p_got = s16[4,16,1408]{2,1,0:T(8,128)(2,1)S(1)} collective-permute-done((s16[4,16,1408]{2,1,0:T(8,128)(2,1)S(1)}, s16[4,16,1408]{2,1,0:T(8,128)(2,1)S(1)}, u32[]{:S(2)}, u32[]{:S(2)}) %collective-permute-start.10) | collective-permute-done | bytes 180256 | tf_op jit(solution)/shard_map/ppermute | solution.py:331
  60.4 1.5 %collective-permute-done.11.q_got = s16[4,16,1408]{2,1,0:T(8,128)(2,1)S(1)} collective-permute-done((s16[4,16,1408]{2,1,0:T(8,128)(2,1)S(1)}, s16[4,16,1408]{2,1,0:T(8,128)(2,1)S(1)}, u32[]{:S(2)}, u32[]{:S(2)}) %collective-permute-start.11) | collective-permute-done | bytes 180256 | tf_op jit(solution)/shard_map/ppermute | solution.py:331
  63.4 3.0 %collective-permute-start.13 = (s16[2,16,1408]{2,1,0:T(8,128)(2,1)S(1)}, s16[2,16,1408]{2,1,0:T(8,128)(2,1)S(1)}, u32[]{:S(2)}, u32[]{:S(2)}) collective-permute-start(s16[2,16,1408]{2,1,0:T(8,128)(2,1)S(1)} %get-tuple-element.40), channel_id=1, source_target_pairs={{0,4},{1,5},{2,6},{3,7},{4,0},{5,1},{6,2},{7,3},{8,12},{9,13},{10,... | collective-permute-start | bytes 270344 | tf_op jit(solution)/shard_map/ppermute | solution.py:331
  67.1 3.8 %collective-permute-done.13.refs_1_ = s16[2,16,1408]{2,1,0:T(8,128)(2,1)S(1)} collective-permute-done((s16[2,16,1408]{2,1,0:T(8,128)(2,1)S(1)}, s16[2,16,1408]{2,1,0:T(8,128)(2,1)S(1)}, u32[]{:S(2)}, u32[]{:S(2)}) %collective-permute-start.13) | collective-permute-done | bytes 90144 | tf_op jit(solution)/shard_map/ppermute | solution.py:331
  70.9 2.0 %collective-permute-done.14.refs_2_ = s16[2,16,1408]{2,1,0:T(8,128)(2,1)S(1)} collective-permute-done((s16[2,16,1408]{2,1,0:T(8,128)(2,1)S(1)}, s16[2,16,1408]{2,1,0:T(8,128)(2,1)S(1)}, u32[]{:S(2)}, u32[]{:S(2)}) %collective-permute-start.14) | collective-permute-done | bytes 90144 | tf_op jit(solution)/shard_map/ppermute | solution.py:331
  73.1 1.3 %collective-permute-start.21 = (s16[2,16,1408]{2,1,0:T(8,128)(2,1)S(1)}, s16[2,16,1408]{2,1,0:T(8,128)(2,1)S(1)}, u32[]{:S(2)}, u32[]{:S(2)}) collective-permute-start(s16[2,16,1408]{2,1,0:T(8,128)(2,1)S(1)} %shard_map.107.refs_0_), channel_id=1, source_target_pairs={{0,7},{1,6},{2,5},{3,4},{4,3},{5,2},{6,1},{7,0},{8,15},{9,14},{10,... | collective-permute-start | bytes 270344 | tf_op jit(solution)/shard_map/ppermute | solution.py:331
  74.4 2.3 %collective-permute-start.20 = (s16[2,16,1408]{2,1,0:T(8,128)(2,1)S(1)}, s16[2,16,1408]{2,1,0:T(8,128)(2,1)S(1)}, u32[]{:S(2)}, u32[]{:S(2)}) collective-permute-start(s16[2,16,1408]{2,1,0:T(8,128)(2,1)S(1)} %shard_map.107.refs_0_), channel_id=1, source_target_pairs={{0,6},{1,7},{2,4},{3,5},{4,2},{5,3},{6,0},{7,1},{8,14},{9,15},{10,... | collective-permute-start | bytes 270344 | tf_op jit(solution)/shard_map/ppermute | solution.py:331
  76.7 2.9 %collective-permute-start.19 = (s16[2,16,1408]{2,1,0:T(8,128)(2,1)S(1)}, s16[2,16,1408]{2,1,0:T(8,128)(2,1)S(1)}, u32[]{:S(2)}, u32[]{:S(2)}) collective-permute-start(s16[2,16,1408]{2,1,0:T(8,128)(2,1)S(1)} %shard_map.107.refs_0_), channel_id=1, source_target_pairs={{0,5},{1,4},{2,7},{3,6},{4,1},{5,0},{6,3},{7,2},{8,13},{9,12},{10,... | collective-permute-start | bytes 270344 | tf_op jit(solution)/shard_map/ppermute | solution.py:331
  81.4 2.6 %collective-permute-start.16 = (s16[2,16,1408]{2,1,0:T(8,128)(2,1)S(1)}, s16[2,16,1408]{2,1,0:T(8,128)(2,1)S(1)}, u32[]{:S(2)}, u32[]{:S(2)}) collective-permute-start(s16[2,16,1408]{2,1,0:T(8,128)(2,1)S(1)} %shard_map.107.refs_0_), channel_id=1, source_target_pairs={{0,2},{1,3},{2,0},{3,1},{4,6},{5,7},{6,4},{7,5},{8,10},{9,11},{10,... | collective-permute-start | bytes 270344 | tf_op jit(solution)/shard_map/ppermute | solution.py:331
  84.0 2.0 %collective-permute-start.15 = (s16[2,16,1408]{2,1,0:T(8,128)(2,1)S(1)}, s16[2,16,1408]{2,1,0:T(8,128)(2,1)S(1)}, u32[]{:S(2)}, u32[]{:S(2)}) collective-permute-start(s16[2,16,1408]{2,1,0:T(8,128)(2,1)S(1)} %shard_map.107.refs_0_), channel_id=1, source_target_pairs={{0,1},{1,0},{2,3},{3,2},{4,5},{5,4},{6,7},{7,6},{8,9},{9,8},{10,11... | collective-permute-start | bytes 270344 | tf_op jit(solution)/shard_map/ppermute | solution.py:331
  86.1 2.2 %collective-permute-done.19.refs_5_ = s16[2,16,1408]{2,1,0:T(8,128)(2,1)S(1)} collective-permute-done((s16[2,16,1408]{2,1,0:T(8,128)(2,1)S(1)}, s16[2,16,1408]{2,1,0:T(8,128)(2,1)S(1)}, u32[]{:S(2)}, u32[]{:S(2)}) %collective-permute-start.19) | collective-permute-done | bytes 90144 | tf_op jit(solution)/shard_map/ppermute | solution.py:331
  89.2 1.2 %shard_map.108 = (f32[256,1024]{1,0:T(8,128)}, f32[256,256]{1,0:T(8,128)}) custom-call(s32[1]{0:T(128)} %bitcast.me, s16[2,16,1408]{2,1,0:T(8,128)(2,1)S(1)} %shard_map.107.refs_0_, s16[2,16,1408]{2,1,0:T(8,128)(2,1)S(1)} %collective-permute-done.15.refs_1_, s16[2,16,1408]{2,1,0:T(8,128)(2,1)S(1)} %collective-permute-done.16.refs_2_, ...), custom_call_target="tpu_custom_call" | custom-call | tf_op jit(solution)/shard_map/pallas_call | solution.py:486
  (40 shorter events, 9.7 us)
Async XLA Ops:
  0.6 19.6 %copy-start = (bf16[512,1024]{1,0:T(8,128)(2,1)S(1)}, bf16[512,1024]{1,0:T(8,128)(2,1)}, u32[]{:S(2)}) copy-start(bf16[512,1024]{1,0:T(8,128)(2,1)} %inputs.3) | copy-start | bytes 3145732
  0.6 20.2 %copy-start.2 = (s32[512,15]{0,1:T(8,128)S(1)}, s32[512,15]{0,1:T(8,128)}, u32[]{:S(2)}) copy-start(s32[512,15]{0,1:T(8,128)} %param.12) | copy-start | bytes 92164
  0.7 20.2 %copy-start.3 = (s32[512,15]{0,1:T(8,128)S(1)}, s32[512,15]{0,1:T(8,128)}, u32[]{:S(2)}) copy-start(s32[512,15]{0,1:T(8,128)} %param.14) | copy-start | bytes 92164
  0.7 20.2 %copy-start.5 = (s32[512]{0:T(512)S(1)}, s32[512]{0:T(512)}, u32[]{:S(2)}) copy-start(s32[512]{0:T(512)} %param.13) | copy-start | bytes 6148
  5.4 17.3 %copy-start.4 = (s32[4]{0:T(128)S(1)}, s32[4]{0:T(128)}, u32[]{:S(2)}) copy-start(s32[4]{0:T(128)} %offsets.7) | copy-start | bytes 52
  5.4 6.2 %collective-permute-start.4 = (bf16[512,256]{1,0:T(8,128)(2,1)S(1)}, bf16[512,256]{1,0:T(8,128)(2,1)S(1)}, u32[]{:S(2)}, u32[]{:S(2)}) collective-permute-start(bf16[512,256]{1,0:T(8,128)(2,1)S(1)} %get-tuple-element.23.rest_0_), channel_id=1, source_target_pairs={{0,8},{8,0},{16,24},{24,16},{1,9},{9,1},{17,25},{25,17},{2,10},{10... | collective-permute-start | bytes 786440 | tf_op jit(solution)/shard_map/ppermute | solution.py:331
  6.0 12.8 %collective-permute-start.2 = (bf16[512,256]{1,0:T(8,128)(2,1)S(1)}, bf16[512,256]{1,0:T(8,128)(2,1)S(1)}, u32[]{:S(2)}, u32[]{:S(2)}) collective-permute-start(bf16[512,256]{1,0:T(8,128)(2,1)S(1)} %get-tuple-element.23.rest_0_), channel_id=1, source_target_pairs={{7,0},{0,1},{1,2},{2,3},{3,4},{4,5},{5,6},{6,7},{15,8},{8,9},{9,10... | collective-permute-start | bytes 786440 | tf_op jit(solution)/shard_map/ppermute | solution.py:327
  8.5 10.2 %collective-permute-start = (bf16[512,256]{1,0:T(8,128)(2,1)S(1)}, bf16[512,256]{1,0:T(8,128)(2,1)S(1)}, u32[]{:S(2)}, u32[]{:S(2)}) collective-permute-start(bf16[512,256]{1,0:T(8,128)(2,1)S(1)} %get-tuple-element.23.rest_0_), channel_id=1, source_target_pairs={{6,0},{7,1},{0,2},{1,3},{2,4},{3,5},{4,6},{5,7},{14,8},{15,9},{8,1... | collective-permute-start | bytes 786440 | tf_op jit(solution)/shard_map/ppermute | solution.py:327
  10.1 16.2 %collective-permute-start.5 = (bf16[512,256]{1,0:T(8,128)(2,1)S(1)}, bf16[512,256]{1,0:T(8,128)(2,1)S(1)}, u32[]{:S(2)}, u32[]{:S(2)}) collective-permute-start(bf16[512,256]{1,0:T(8,128)(2,1)S(1)} %get-tuple-element.23.rest_0_), channel_id=1, source_target_pairs={{0,16},{8,24},{16,0},{24,8},{1,17},{9,25},{17,1},{25,9},{2,18},{10... | collective-permute-start | bytes 786440 | tf_op jit(solution)/shard_map/ppermute | solution.py:331
  11.6 14.7 %collective-permute-start.6 = (bf16[512,256]{1,0:T(8,128)(2,1)S(1)}, bf16[512,256]{1,0:T(8,128)(2,1)S(1)}, u32[]{:S(2)}, u32[]{:S(2)}) collective-permute-start(bf16[512,256]{1,0:T(8,128)(2,1)S(1)} %collective-permute-done.4.rest_1_), channel_id=1, source_target_pairs={{0,16},{8,24},{16,0},{24,8},{1,17},{9,25},{17,1},{25,9},{2,18},{10... | collective-permute-start | bytes 786440 | tf_op jit(solution)/shard_map/ppermute | solution.py:331
  18.7 11.0 %collective-permute-start.3 = (bf16[512,256]{1,0:T(8,128)(2,1)S(1)}, bf16[512,256]{1,0:T(8,128)(2,1)S(1)}, u32[]{:S(2)}, u32[]{:S(2)}) collective-permute-start(bf16[512,256]{1,0:T(8,128)(2,1)S(1)} %collective-permute-done.2.block), channel_id=1, source_target_pairs={{6,0},{7,1},{0,2},{1,3},{2,4},{3,5},{4,6},{5,7},{14,8},{15,9},{8,1... | collective-permute-start | bytes 786440 | tf_op jit(solution)/shard_map/ppermute | solution.py:327
  18.8 15.2 %collective-permute-start.1 = (bf16[512,256]{1,0:T(8,128)(2,1)S(1)}, bf16[512,256]{1,0:T(8,128)(2,1)S(1)}, u32[]{:S(2)}, u32[]{:S(2)}) collective-permute-start(bf16[512,256]{1,0:T(8,128)(2,1)S(1)} %collective-permute-done.block), channel_id=1, source_target_pairs={{6,0},{7,1},{0,2},{1,3},{2,4},{3,5},{4,6},{5,7},{14,8},{15,9},{8,1... | collective-permute-start | bytes 786440 | tf_op jit(solution)/shard_map/ppermute | solution.py:327
  20.8 5.5 %copy-start.6 = (s32[4,128]{1,0:T(4,128)S(1)}, s32[4,128]{1,0:T(4,128)}, u32[]{:S(2)}) copy-start(s32[4,128]{1,0:T(4,128)} %requests.1) | copy-start | bytes 6148
  26.3 7.7 %copy-start.1 = (bf16[1024,256]{1,0:T(8,128)(2,1)S(1)}, bf16[1024,256]{1,0:T(8,128)(2,1)}, u32[]{:S(2)}) copy-start(bf16[1024,256]{1,0:T(8,128)(2,1)} %w_second.3) | copy-start | bytes 1572868
  37.1 3.3 %collective-permute-start.7 = (s16[2,256,1408]{2,1,0:T(8,128)(2,1)S(1)}, s16[2,256,1408]{2,1,0:T(8,128)(2,1)S(1)}, u32[]{:S(2)}, u32[]{:S(2)}) collective-permute-start(s16[2,256,1408]{2,1,0:T(8,128)(2,1)S(1)} %get-tuple-element.29), channel_id=1, source_target_pairs={{0,8},{8,0},{16,24},{24,16},{1,9},{9,1},{17,25},{25,17},{2,10},{10... | collective-permute-start | bytes 4325384 | tf_op jit(solution)/shard_map/ppermute | solution.py:331
  42.0 10.5 %collective-permute-start.8 = (s16[4,2,16,1408]{3,2,1,0:T(8,128)(2,1)S(1)}, s16[4,2,16,1408]{3,2,1,0:T(8,128)(2,1)S(1)}, u32[]{:S(2)}, u32[]{:S(2)}) collective-permute-start(s16[4,2,16,1408]{3,2,1,0:T(8,128)(2,1)S(1)} %get-tuple-element.32), channel_id=1, source_target_pairs={{0,16},{8,24},{16,0},{24,8},{1,17},{9,25},{17,1},{25,9},{2,18},{10... | collective-permute-start | bytes 1081352 | tf_op jit(solution)/shard_map/ppermute | solution.py:331
  43.4 10.5 %collective-permute-start.9 = (s16[2,4,16,1408]{3,2,1,0:T(8,128)(2,1)S(1)}, s16[2,4,16,1408]{3,2,1,0:T(8,128)(2,1)S(1)}, u32[]{:S(2)}, u32[]{:S(2)}) collective-permute-start(s16[2,4,16,1408]{3,2,1,0:T(8,128)(2,1)S(1)} %get-tuple-element.33), channel_id=1, source_target_pairs={{0,1},{1,0},{2,3},{3,2},{4,5},{5,4},{6,7},{7,6},{8,9},{9,8},{10,11... | collective-permute-start | bytes 1081352 | tf_op jit(solution)/shard_map/ppermute | solution.py:331
  54.6 5.8 %collective-permute-start.10 = (s16[4,16,1408]{2,1,0:T(8,128)(2,1)S(1)}, s16[4,16,1408]{2,1,0:T(8,128)(2,1)S(1)}, u32[]{:S(2)}, u32[]{:S(2)}) collective-permute-start(s16[4,16,1408]{2,1,0:T(8,128)(2,1)S(1)} %get-tuple-element.36), channel_id=1, source_target_pairs={{0,1},{1,0},{2,3},{3,2},{4,5},{5,4},{6,7},{7,6},{8,9},{9,8},{10,11... | collective-permute-start | bytes 540680 | tf_op jit(solution)/shard_map/ppermute | solution.py:331
  56.4 5.5 %collective-permute-start.11 = (s16[4,16,1408]{2,1,0:T(8,128)(2,1)S(1)}, s16[4,16,1408]{2,1,0:T(8,128)(2,1)S(1)}, u32[]{:S(2)}, u32[]{:S(2)}) collective-permute-start(s16[4,16,1408]{2,1,0:T(8,128)(2,1)S(1)} %get-tuple-element.37), channel_id=1, source_target_pairs={{0,16},{8,24},{16,0},{24,8},{1,17},{9,25},{17,1},{25,9},{2,18},{10... | collective-permute-start | bytes 540680 | tf_op jit(solution)/shard_map/ppermute | solution.py:331
  62.3 4.8 %collective-permute-start.12 = (s16[2,16,1408]{2,1,0:T(8,128)(2,1)S(1)}, s16[2,16,1408]{2,1,0:T(8,128)(2,1)S(1)}, u32[]{:S(2)}, u32[]{:S(2)}) collective-permute-start(s16[2,16,1408]{2,1,0:T(8,128)(2,1)S(1)} %get-tuple-element.39), channel_id=1, source_target_pairs={{0,2},{1,3},{2,0},{3,1},{4,6},{5,7},{6,4},{7,5},{8,10},{9,11},{10,... | collective-permute-start | bytes 270344 | tf_op jit(solution)/shard_map/ppermute | solution.py:331
  63.4 7.5 %collective-permute-start.13 = (s16[2,16,1408]{2,1,0:T(8,128)(2,1)S(1)}, s16[2,16,1408]{2,1,0:T(8,128)(2,1)S(1)}, u32[]{:S(2)}, u32[]{:S(2)}) collective-permute-start(s16[2,16,1408]{2,1,0:T(8,128)(2,1)S(1)} %get-tuple-element.40), channel_id=1, source_target_pairs={{0,4},{1,5},{2,6},{3,7},{4,0},{5,1},{6,2},{7,3},{8,12},{9,13},{10,... | collective-permute-start | bytes 270344 | tf_op jit(solution)/shard_map/ppermute | solution.py:331
  66.4 6.4 %collective-permute-start.14 = (s16[2,16,1408]{2,1,0:T(8,128)(2,1)S(1)}, s16[2,16,1408]{2,1,0:T(8,128)(2,1)S(1)}, u32[]{:S(2)}, u32[]{:S(2)}) collective-permute-start(s16[2,16,1408]{2,1,0:T(8,128)(2,1)S(1)} %get-tuple-element.41), channel_id=1, source_target_pairs={{0,6},{1,7},{2,4},{3,5},{4,2},{5,3},{6,0},{7,1},{8,14},{9,15},{10,... | collective-permute-start | bytes 270344 | tf_op jit(solution)/shard_map/ppermute | solution.py:331
  73.1 8.3 %collective-permute-start.21 = (s16[2,16,1408]{2,1,0:T(8,128)(2,1)S(1)}, s16[2,16,1408]{2,1,0:T(8,128)(2,1)S(1)}, u32[]{:S(2)}, u32[]{:S(2)}) collective-permute-start(s16[2,16,1408]{2,1,0:T(8,128)(2,1)S(1)} %shard_map.107.refs_0_), channel_id=1, source_target_pairs={{0,7},{1,6},{2,5},{3,4},{4,3},{5,2},{6,1},{7,0},{8,15},{9,14},{10,... | collective-permute-start | bytes 270344 | tf_op jit(solution)/shard_map/ppermute | solution.py:331
  74.4 9.6 %collective-permute-start.20 = (s16[2,16,1408]{2,1,0:T(8,128)(2,1)S(1)}, s16[2,16,1408]{2,1,0:T(8,128)(2,1)S(1)}, u32[]{:S(2)}, u32[]{:S(2)}) collective-permute-start(s16[2,16,1408]{2,1,0:T(8,128)(2,1)S(1)} %shard_map.107.refs_0_), channel_id=1, source_target_pairs={{0,6},{1,7},{2,4},{3,5},{4,2},{5,3},{6,0},{7,1},{8,14},{9,15},{10,... | collective-permute-start | bytes 270344 | tf_op jit(solution)/shard_map/ppermute | solution.py:331
  76.7 11.6 %collective-permute-start.19 = (s16[2,16,1408]{2,1,0:T(8,128)(2,1)S(1)}, s16[2,16,1408]{2,1,0:T(8,128)(2,1)S(1)}, u32[]{:S(2)}, u32[]{:S(2)}) collective-permute-start(s16[2,16,1408]{2,1,0:T(8,128)(2,1)S(1)} %shard_map.107.refs_0_), channel_id=1, source_target_pairs={{0,5},{1,4},{2,7},{3,6},{4,1},{5,0},{6,3},{7,2},{8,13},{9,12},{10,... | collective-permute-start | bytes 270344 | tf_op jit(solution)/shard_map/ppermute | solution.py:331
  79.6 9.0 %collective-permute-start.18 = (s16[2,16,1408]{2,1,0:T(8,128)(2,1)S(1)}, s16[2,16,1408]{2,1,0:T(8,128)(2,1)S(1)}, u32[]{:S(2)}, u32[]{:S(2)}) collective-permute-start(s16[2,16,1408]{2,1,0:T(8,128)(2,1)S(1)} %shard_map.107.refs_0_), channel_id=1, source_target_pairs={{0,4},{1,5},{2,6},{3,7},{4,0},{5,1},{6,2},{7,3},{8,12},{9,13},{10,... | collective-permute-start | bytes 270344 | tf_op jit(solution)/shard_map/ppermute | solution.py:331
  80.8 7.8 %collective-permute-start.17 = (s16[2,16,1408]{2,1,0:T(8,128)(2,1)S(1)}, s16[2,16,1408]{2,1,0:T(8,128)(2,1)S(1)}, u32[]{:S(2)}, u32[]{:S(2)}) collective-permute-start(s16[2,16,1408]{2,1,0:T(8,128)(2,1)S(1)} %shard_map.107.refs_0_), channel_id=1, source_target_pairs={{0,3},{1,2},{2,1},{3,0},{4,7},{5,6},{6,5},{7,4},{8,11},{9,10},{10,... | collective-permute-start | bytes 270344 | tf_op jit(solution)/shard_map/ppermute | solution.py:331
  81.4 7.5 %collective-permute-start.16 = (s16[2,16,1408]{2,1,0:T(8,128)(2,1)S(1)}, s16[2,16,1408]{2,1,0:T(8,128)(2,1)S(1)}, u32[]{:S(2)}, u32[]{:S(2)}) collective-permute-start(s16[2,16,1408]{2,1,0:T(8,128)(2,1)S(1)} %shard_map.107.refs_0_), channel_id=1, source_target_pairs={{0,2},{1,3},{2,0},{3,1},{4,6},{5,7},{6,4},{7,5},{8,10},{9,11},{10,... | collective-permute-start | bytes 270344 | tf_op jit(solution)/shard_map/ppermute | solution.py:331
  84.0 5.1 %collective-permute-start.15 = (s16[2,16,1408]{2,1,0:T(8,128)(2,1)S(1)}, s16[2,16,1408]{2,1,0:T(8,128)(2,1)S(1)}, u32[]{:S(2)}, u32[]{:S(2)}) collective-permute-start(s16[2,16,1408]{2,1,0:T(8,128)(2,1)S(1)} %shard_map.107.refs_0_), channel_id=1, source_target_pairs={{0,1},{1,0},{2,3},{3,2},{4,5},{5,4},{6,7},{7,6},{8,9},{9,8},{10,11... | collective-permute-start | bytes 270344 | tf_op jit(solution)/shard_map/ppermute | solution.py:331

commit v5 on v4

--- a/solution.py
+++ b/solution.py
@@ -12,6 +12,7 @@
 NEGW = 8
 TILE = 128
 PACK = 16
+SHARE = 16
 LANES = 128
 HALF = LANES // 2
 FULL = 32000.0
@@ -139,8 +140,11 @@
         out[rows_of, :] = total
 
 
-def repulsion(codes, block, offset, twice, put):
-    rows = block.shape[0]
+def repulsion(me, codes, choices, offset, twice, put):
+    rows = codes.shape[0]
+    block = choices[0][...]
+    if len(choices) > 1:
+        block = jnp.where(digit(me, 1, 2) > 0, choices[1][...], block)
     tile = min(rows, TILE)
     window = tile + max(tile, LANES)
     for at in range(0, twice.shape[0], rows):
@@ -165,13 +169,15 @@
     return pltpu.VMEM((2 * rows + max(tile, LANES), width), BF16)
 
 
-def far_body(step, started, offsets, codes, block, *rest):
-    grad, out, twice = rest if started else (None,) + rest
+def far_body(step, count, me, offsets, codes, *rest):
+    choices, rest = rest[:count], rest[count:]
+    out, twice = rest[-2:]
+    grad = rest[0] if len(rest) > 2 else None
 
     def put(at, value):
-        out[at, :] = grad[at, :] - value if started else -value
-
-    repulsion(codes, block, offsets[step], twice, put)
+        out[at, :] = -value if grad is None else grad[at, :] - value
+
+    repulsion(me, codes, choices, offsets[step], twice, put)
 
 
 def encode(one, two):
@@ -179,33 +185,68 @@
     for piece in (one, two):
         top = jnp.maximum(jnp.max(jnp.abs(piece), axis=1, keepdims=True), TINY)
         code = jnp.ceil(jnp.log2(top) * STEPS)
-        unit = FULL * jnp.exp2(code * (-1.0 / STEPS))
-        quanta.append(jnp.round(piece * unit))
+        quanta.append(short(jnp.round(piece * (FULL * jnp.exp2(code * (-1.0 / STEPS))))))
         codes.append(code)
-    lane = lax.broadcasted_iota(jnp.int32, (one.shape[0], LANES), 1)
-    quanta.append(jnp.where(lane < HALF, codes[0], codes[1]))
-    return [q.astype(jnp.int32).astype(I16) for q in quanta]
+    return quanta, codes
+
+
+def short(value):
+    return value.astype(jnp.int32).astype(I16)
+
+
+def unit_of(code):
+    return jnp.exp2(code * (1.0 / STEPS)) * (1.0 / FULL)
+
+
+def pack(ref, pieces):
+    rows = ref.shape[1]
+    lane = lax.broadcasted_iota(jnp.int32, (rows, LANES), 1)
+    header = jnp.zeros((rows, LANES), F32)
+    at = 0
+    for k, piece in enumerate(pieces):
+        quanta, codes = encode(*piece)
+        for quantum in quanta:
+            for column in range(0, quantum.shape[1], LANES):
+                ref[at] = quantum[:, column : column + LANES]
+                at += 1
+        for j, code in enumerate(codes):
+            header = jnp.where(lane >= SHARE * k + SHARE // 2 * j, code, header)
+    ref[at] = short(header)
+
+
+def unpack(ref, k, first, width):
+    tiles = width // LANES
+    header = ref[ref.shape[0] - 1].astype(jnp.int32).astype(F32)
+    out = []
+    for j, (low, high) in enumerate(((0, first // LANES), (first // LANES, tiles))):
+        lane = SHARE * k + SHARE // 2 * j
+        unit = unit_of(header[:, lane : lane + 1])
+        value = [ref[k * tiles + g].astype(jnp.int32).astype(F32) for g in range(low, high)]
+        out.append(jnp.concatenate(value, axis=1) * unit)
+    return out
 
 
 def decode(packed, first, width):
     code = packed[:, width:].astype(jnp.int32).astype(F32)
     out = []
     for lane, low, high in ((0, 0, first), (HALF, first, width)):
-        unit = jnp.exp2(code[:, lane : lane + 1] * (1.0 / STEPS)) * (1.0 / FULL)
+        unit = unit_of(code[:, lane : lane + 1])
         out.append(packed[:, low:high].astype(jnp.int32).astype(F32) * unit)
     return out
 
 
 def put_encoded(ref, one, two):
     first, width = one.shape[1], one.shape[1] + two.shape[1]
-    ref[:, :first], ref[:, first:width], ref[:, width:] = encode(one, two)
-
-
-def gradients(step, scale, offsets, codes, block, grad, w_second, hidden, twice, dcodes, dpre):
+    (ref[:, :first], ref[:, first:width]), codes = encode(one, two)
+    lane = lax.broadcasted_iota(jnp.int32, (one.shape[0], LANES), 1)
+    ref[:, width:] = short(jnp.where(lane < HALF, codes[0], codes[1]))
+
+
+def gradients(step, scale, me, offsets, codes, choices, grad, w_second, hidden, twice, dcodes, dpre):
     def put(at, value):
         dcodes[at, :] = (scale * (grad[at, :] - value)).astype(BF16)
 
-    repulsion(codes, block, offsets[step], twice, put)
+    repulsion(me, codes, choices, offsets[step], twice, put)
     size = 2 * LANES
     for at in range(0, hidden.shape[1], size):
         columns = slice(at, at + size)
@@ -213,8 +254,9 @@
         dpre[:, columns] = jnp.where(hidden[:, columns] > 0, wide, 0.0).astype(BF16)
 
 
-def give_body(step, scale, below, offsets, me, codes, block, grad, w_second, hidden, inputs_t, hidden_t, send, dcodes, dpre, twice):
-    gradients(step, scale, offsets, codes, block, grad, w_second, hidden, twice, dcodes, dpre)
+def give_body(step, scale, below, me, offsets, codes, *rest):
+    *choices, grad, w_second, hidden, inputs_t, hidden_t, send, dcodes, dpre, twice = rest
+    gradients(step, scale, me, offsets, codes, choices, grad, w_second, hidden, twice, dcodes, dpre)
     groups, rows = send.shape[:2]
     one, two = halves(1 - digit(me, below, 2), groups, rows, dcodes, dpre, inputs_t, hidden_t)
     for a in range(groups):
@@ -239,9 +281,9 @@
     return dot(taken(inputs_t), dpre[...]), dot(taken(hidden_t), dcodes[...])
 
 
-def last_plain_body(step, scale, offsets, codes, block, grad, w_second, hidden, inputs_t, hidden_t, one, two, *scratch):
-    gradients(step, scale, offsets, codes, block, grad, w_second, hidden, *scratch)
-    dcodes, dpre = scratch[1:]
+def last_plain_body(step, scale, me, offsets, codes, *rest):
+    *choices, grad, w_second, hidden, inputs_t, hidden_t, one, two, twice, dcodes, dpre = rest
+    gradients(step, scale, me, offsets, codes, choices, grad, w_second, hidden, twice, dcodes, dpre)
     one[...] = dot(inputs_t[...], dpre[...])
     two[...] = dot(hidden_t[...], dcodes[...])
 
@@ -259,54 +301,74 @@
         keep[a, :, :first], keep[a, :, first:] = summed(held.at[a, mine], got.at[a, mine], first)
 
 
-def part_body(first, belows, me, held, got, p_keep, p_send, q_keep, q_send):
-    mine, here = (digit(me, below, 2) for below in belows)
-    other, there = 1 - mine, 1 - here
-    for j in range(held.shape[2]):
-        for bit in range(2):
-            at = (other, 0, j, bit)
-            put_encoded(p_send.at[j, bit], *summed(held.at[at], got.at[at], first))
-        for block in range(2):
-            at = (block, 1, j, there)
-            put_encoded(q_send.at[block, j], *summed(held.at[at], got.at[at], first))
-    for j in range(held.shape[2]):
-        for bit in range(2):
-            at = (mine, 0, j, bit)
-            p_keep[j, bit, :, :first], p_keep[j, bit, :, first:] = summed(held.at[at], got.at[at], first)
-        for block in range(2):
-            at = (block, 1, j, here)
-            q_keep[block, j, :, :first], q_keep[block, j, :, first:] = summed(held.at[at], got.at[at], first)
-
-
-def cross_body(first, belows, me, p_held, q_held, p_got, q_got, p_keep, q_keep, p_send, q_send):
-    mine, here = (digit(me, below, 2) for below in belows)
-    other, there = 1 - mine, 1 - here
-    for j in range(p_send.shape[0]):
-        put_encoded(p_send.at[j], *summed(p_held.at[j, there], p_got.at[j, there], first))
-        put_encoded(q_send.at[j], *summed(q_held.at[other, j], q_got.at[other, j], first))
-    for j in range(p_send.shape[0]):
-        p_keep[j, :, :first], p_keep[j, :, first:] = summed(p_held.at[j, here], p_got.at[j, here], first)
-        q_keep[j, :, :first], q_keep[j, :, first:] = summed(q_held.at[mine, j], q_got.at[mine, j], first)
-
-
-def deal_body(first, me, p_held, q_held, p_got, q_got, keep, *sends):
+def part_index(below, me, others):
+    mine, here, place = digit(me, below, 2), digit(me, 1, 2), digit(me, 2, others)
+
+    def p_at(side, k, r):
+        return (mine ^ side, 0, place ^ k, here ^ r)
+
+    def q_at(side, r, k):
+        return (mine ^ r, 1, place ^ k, here ^ side)
+
+    return p_at, q_at
+
+
+def part_send_body(first, below, half, me, held, got, send):
+    others = held.shape[2]
+    index = part_index(below, me, others)[half]
+    pairs = [(i, j) for i in range((others, 2)[half]) for j in range((2, others)[half])]
+    pack(send, [summed(held.at[index(1, *pair)], got.at[index(1, *pair)], first) for pair in pairs])
+
+
+def part_keep_body(first, below, me, held, got, p_keep, q_keep):
+    others = held.shape[2]
+    p_at, q_at = part_index(below, me, others)
+    for k in range(others):
+        for r in range(2):
+            at = p_at(0, k, r)
+            p_keep[k, r, :, :first], p_keep[k, r, :, first:] = summed(held.at[at], got.at[at], first)
+            at = q_at(0, r, k)
+            q_keep[r, k, :, :first], q_keep[r, k, :, first:] = summed(held.at[at], got.at[at], first)
+
+
+def joined(held, got, k, first):
+    one, two = unpack(got, k, first, held.shape[-1])
+    return held[:, :first] + one, held[:, first:] + two
+
+
+def cross_send_body(first, p_held, q_held, p_got, q_got, p_send, q_send):
+    others = p_held.shape[0]
+    pack(p_send, [joined(p_held.at[k, 1], p_got, 2 * k + 1, first) for k in range(others)])
+    pack(q_send, [joined(q_held.at[1, k], q_got, others + k, first) for k in range(others)])
+
+
+def cross_keep_body(first, p_held, q_held, p_got, q_got, p_keep, q_keep):
+    for k in range(p_held.shape[0]):
+        p_keep[k, :, :first], p_keep[k, :, first:] = joined(p_held.at[k, 0], p_got, 2 * k, first)
+        q_keep[k, :, :first], q_keep[k, :, first:] = joined(q_held.at[0, k], q_got, k, first)
+
+
+def deal_send_body(first, p_held, q_held, p_got, q_got, *sends):
     pairs = ((p_held, p_got), (q_held, q_got))
-    mine = digit(me, 2, p_held.shape[0])
-    for k in range(1, p_held.shape[0]):
-        for half, (held, got) in enumerate(pairs):
-            piece = summed(held.at[mine ^ k], got.at[mine ^ k], first)
-            put_encoded(sends[k - 1].at[half], *piece)
+    for k, send in enumerate(sends, 1):
+        pack(send, [joined(held.at[k], got, k, first) for held, got in pairs])
+
+
+def deal_keep_body(first, p_held, q_held, p_got, q_got, keep):
+    pairs = ((p_held, p_got), (q_held, q_got))
     for half, (held, got) in enumerate(pairs):
-        keep[half, :, :first], keep[half, :, first:] = summed(held.at[mine], got.at[mine], first)
+        keep[half, :, :first], keep[half, :, first:] = joined(held.at[0], got, 0, first)
 
 
 def close_body(first, held, *refs):
+    pieces = []
     for half in range(held.shape[0]):
         one, two = held[half, :, :first], held[half, :, first:]
         for got in refs[:-1]:
-            more = decode(got.at[half], first, held.shape[2])
+            more = unpack(got, half, first, held.shape[2])
             one, two = one + more[0], two + more[1]
-        put_encoded(refs[-1].at[half], one, two)
+        pieces.append((one, two))
+    pack(refs[-1], pieces)
 
 
 def spread_body(first, me, *refs):
@@ -315,10 +377,10 @@
     narrow = digit(me, 1, len(refs[:-2]))
     for place, ref in enumerate(refs[:-2]):
         rows = ref.shape[1]
-        for half in range(ref.shape[0]):
+        for half in range(2):
             at = half * (one.shape[0] // 2) + (narrow ^ place) * rows
             at = pl.ds(pl.multiple_of(at, rows), rows)
-            one[at, :], two[at, :] = decode(ref.at[half], first, width)
+            one[at, :], two[at, :] = unpack(ref, half, first, width)
 
 
 def from_behind(block, axis, distance):
@@ -364,10 +426,21 @@
         compiler_params=pltpu.CompilerParams(vmem_limit_bytes=16 * 1024 * 1024),
     )(me, *(pltpu.with_memory_space_constraint(a, pltpu.HBM) for a in (inputs, w_first, w_second)))
     steps = offsets.shape[0]
-    blocks = []
-    for step in range(steps):
-        source = sent if step < 2 else blocks[step - 2]
-        blocks.append(from_behind(source, "narrow", min(step, 1) + 1))
+    paired = steps == 4
+    if paired:
+        two = from_behind(sent, "narrow", 2)
+        own = swapped(sent, "narrow", 1)
+        four = from_behind(two, "narrow", 2)
+        pair = swapped(two, "narrow", 1)
+        three = lax.ppermute(two, "narrow", [((n - 1) % group, n) for n in range(0, group, 2)])
+        blocks = [(pair, own), (two,), (three, pair), (four,)]
+        order = [1, 0, 3, 2]
+    else:
+        blocks = []
+        for step in range(steps):
+            source = sent if step < 2 else blocks[step - 2][0]
+            blocks.append((from_behind(source, "narrow", min(step, 1) + 1),))
+        order = list(range(steps))
     near = [sent]
     for bit in bits(peers):
         near += [swapped(block, "wide", bit) for block in near]
@@ -389,30 +462,29 @@
     twice = twice_of(rows, width)
 
     def far(step, grad):
-        given = () if grad is None else (grad,)
-        body = functools.partial(far_body, step, bool(given))
-        return call(body, like, 1, 2 + len(given), [twice])(offsets, codes, blocks[step], *given)
-
-    grad = None
-    early = max(steps - 2, 1)
-    for step in range(early):
-        grad = far(step, grad)
+        given = blocks[step] + (() if grad is None else (grad,))
+        body = functools.partial(far_body, step, len(blocks[step]))
+        return call(body, like, 2, 1 + len(given), [twice])(me, offsets, codes, *given)
+
+    grad = far(order[0], None)
     grad = call(functools.partial(near_body, group), like, 1, 4 + len(near), [pltpu.VMEM((size, width), BF16)])(
         me, codes, requests, weight, grad, *near
     )
-    for step in range(early, steps - 1):
+    for step in order[1:-1]:
         grad = far(step, grad)
+    step = order[-1]
+    last_inputs = (me, offsets, codes, *blocks[step], grad, w_second, hidden, inputs_t, hidden_t)
     scale = 2.0 / (slots.shape[1] * math.sqrt(total_rows))
     chunk = din // (peers * group)
     scratch = [twice, pltpu.VMEM((rows, width), BF16), pltpu.VMEM((rows, hid), BF16)]
-    if din != hid or chunk % 32 or din % (peers * group) or peers < 4 or group < 4:
+    if din != hid or chunk % 32 or din % (peers * group) or peers < 4 or not 4 <= group <= LANES // SHARE or width % LANES:
         one, two = call(
-            functools.partial(last_plain_body, steps - 1, scale),
+            functools.partial(last_plain_body, step, scale),
             (jax.ShapeDtypeStruct((din, hid), F32), jax.ShapeDtypeStruct((hid, width), F32)),
-            1,
-            7,
+            2,
+            len(last_inputs) - 2,
             scratch,
-        )(offsets, codes, blocks[-1], grad, w_second, hidden, inputs_t, hidden_t)
+        )(*last_inputs)
         owned = (
             lax.psum_scatter(one, "wide", scatter_dimension=0, tiled=True),
             lax.psum_scatter(two, "wide", scatter_dimension=0, tiled=True),
@@ -433,16 +505,16 @@
         groups, lines = peers // (2 * bit), din // peers
         if keep is None:
             send, dcodes, dpre = call(
-                functools.partial(give_body, steps - 1, scale, below),
+                functools.partial(give_body, step, scale, below),
                 (
                     coded(groups, lines),
                     jax.ShapeDtypeStruct((rows, width), BF16),
                     jax.ShapeDtypeStruct((rows, hid), BF16),
                 ),
                 2,
-                7,
+                len(last_inputs) - 2,
                 [twice],
-            )(offsets, me, codes, blocks[-1], grad, w_second, hidden, inputs_t, hidden_t)
+            )(*last_inputs)
             keep = call(functools.partial(hold_body, below), plain(groups, lines), 1, 4)(me, dcodes, dpre, inputs_t, hidden_t)
         else:
             keep, send = call(
@@ -450,48 +522,45 @@
             )(me, keep.reshape(groups, 2, lines, full), got.reshape(groups, 2, lines, full + LANES))
         got = swapped(send, "wide", bit)
     last, lines, others = peers // 2, chunk // 2, group // 2
-    belows = (last * group, 1)
-    p_keep, p_send, q_keep, q_send = call(
-        functools.partial(part_body, first, belows),
-        (
-            plain(others, 2, lines),
-            coded(others, 2, lines),
-            plain(2, others, lines),
-            coded(2, others, lines),
-        ),
-        1,
-        2,
-    )(
-        me,
+    below = last * group
+
+    def message(count):
+        return jax.ShapeDtypeStruct((count * (full // LANES) + 1, lines, LANES), I16)
+
+    def do(body, shapes, scalars, arrays):
+        return call(body, shapes, len(scalars), len(arrays))(*scalars, *arrays)
+
+    rest = (
         keep.reshape(2, 2, others, 2, lines, full),
         got.reshape(2, 2, others, 2, lines, full + LANES),
     )
-    p_got, q_got = swapped(p_send, "wide", last), swapped(q_send, "narrow", 1)
-    p_keep, q_keep, p_send, q_send = call(
-        functools.partial(cross_body, first, belows),
-        (plain(others, lines),) * 2 + (coded(others, lines),) * 2,
-        1,
-        4,
-    )(me, p_keep, q_keep, p_got, q_got)
+    sends = [
+        do(functools.partial(part_send_body, first, below, half), message(2 * others), (me,), rest)
+        for half in range(2)
+    ]
+    p_keep, q_keep = do(
+        functools.partial(part_keep_body, first, below), (plain(others, 2, lines), plain(2, others, lines)), (me,), rest
+    )
+    p_got, q_got = swapped(sends[0], "wide", last), swapped(sends[1], "narrow", 1)
+    rest = (p_keep, q_keep, p_got, q_got)
+    p_send, q_send = do(functools.partial(cross_send_body, first), (message(others),) * 2, (), rest)
+    p_keep, q_keep = do(functools.partial(cross_keep_body, first), (plain(others, lines),) * 2, (), rest)
     p_got, q_got = swapped(p_send, "narrow", 1), swapped(q_send, "wide", last)
-    keep, *sends = call(
-        functools.partial(deal_body, first),
-        (plain(2, lines),) + (coded(2, lines),) * (others - 1),
-        1,
-        4,
-    )(me, p_keep, q_keep, p_got, q_got)
-    gots = [swapped(send, "narrow", 2 * (k + 1)) for k, send in enumerate(sends)]
-    mine = call(functools.partial(close_body, first), coded(2, lines), 0, others)(keep, *gots)
+    rest = (p_keep, q_keep, p_got, q_got)
+    sends = do(functools.partial(deal_send_body, first), (message(2),) * (others - 1), (), rest)
+    keep = do(functools.partial(deal_keep_body, first), plain(2, lines), (), rest)
+    gots = [swapped(send, "narrow", 2 * k) for k, send in enumerate(sends, 1)]
+    mine = do(functools.partial(close_body, first), message(2), (), (keep, *gots))
     pieces = [mine] + [swapped(mine, "narrow", k) for k in range(1, group)]
-    return call(
+    return do(
         functools.partial(spread_body, first),
         (
             jax.ShapeDtypeStruct((din // peers, hid), F32),
             jax.ShapeDtypeStruct((hid // peers, width), F32),
         ),
-        1,
-        group,
-    )(me, *pieces)
+        (me,),
+        pieces,
+    )
 
 
 def solution(mesh):

time: 90.6 us -> 86.5 us (0.955)
  waiting for transfers between devices: 35.1 us -> 32.9 us
  starting transfers between devices: 31.3 us -> 30.3 us
    ppermute x4 -> x2, waiting for transfers between devices: 9.86 us -> 5.39 us  [from_behind(): return lax.ppermute(block, axis, route)]
    ppermute x0 -> x1, waiting for transfers between devices: none -> 3.16 us  [shards(): lax.ppermute(two, 'narrow', [((n - 1) % group, n) for n in range(0, group...]
    ppermute x4 -> x2, starting transfers between devices: 5.62 us -> 2.63 us  [from_behind(): return lax.ppermute(block, axis, route)]
    ppermute x0 -> x1, starting transfers between devices: none -> 1.46 us  [shards(): lax.ppermute(two, 'narrow', [((n - 1) % group, n) for n in range(0, group...]
    pallas_call x9 -> x13, Pallas kernels: 12.5 us -> 11.5 us  [the longest x3 5.3 us: far(): call(body, like, 2, 1 + len(given), [twice])(me, offsets, codes, *given)]
    ppermute x18 -> x20, waiting for transfers between devices: 25.2 us -> 24.4 us  [swapped(): lax.ppermute(block, axis, [(i, i ^ bit) for i in range(lax.axis_size(axis...]
    ppermute x18 -> x20, starting transfers between devices: 25.7 us -> 26.2 us  [swapped(): lax.ppermute(block, axis, [(i, i ^ bit) for i in range(lax.axis_size(axis...]
  transfers between devices with their start and end apart: 22 -> 23, of which waited for: 16 -> 14; matrix products, arithmetic and copies ran while one was open for 0% -> 0% of each run, Pallas kernels for 12% -> 14%
where the time goes in v5:
time: 86.5 us; the launch traced here: 86.3 us
  waiting for transfers between devices  32.9 us (38%)
  starting transfers between devices  30.3 us (35%)
  Pallas kernels  22.2 us (26%)
  between operations  0.93 us (1%)
    ppermute x20, starting transfers between devices, swapped(): lax.ppermute(block, axis, [(i, i ^ bit) for i in range(lax.axis_size(axis...  26.2 us
    ppermute x20, waiting for transfers between devices, swapped(): lax.ppermute(block, axis, [(i, i ^ bit) for i in range(lax.axis_size(axis...  24.4 us
    ppermute x2, waiting for transfers between devices, from_behind(): return lax.ppermute(block, axis, route)  5.39 us
    pallas_call x3, Pallas kernels, far(): call(body, like, 2, 1 + len(given), [twice])(me, offsets, codes, *given)  5.3 us
    pallas_call x1, Pallas kernels, shards(): pl.pallas_call(forward_body, out_shape=(jax.ShapeDtypeStruct((rows, hid),...  4.71 us
    ppermute x1, waiting for transfers between devices, shards(): lax.ppermute(two, 'narrow', [((n - 1) % group, n) for n in range(0, group...  3.16 us
    pallas_call x9, Pallas kernels, do(): return call(body, shapes, len(scalars), len(arrays))(*scalars, *arrays)  3.12 us
    pallas_call x1, Pallas kernels, shards(): call(functools.partial(give_body, step, scale, below), (coded(groups, lin...  3.1 us
  transfers between devices with their start and end apart: 23, of which 14 were waited for; matrix products, arithmetic and copies ran while one was open for 0% of the time, Pallas kernels for 14%

profile of v5, /device:TPU:0, one launch (start us, length us, event | category | flops | bytes accessed | tf_op | source)
XLA Modules:
  0.0 86.3 jit_solution(9894921425420001533)
XLA Ops:
  0.7 4.7 %shard_map.95 = (bf16[512,1024]{1,0:T(8,128)(2,1)S(1)}, f32[512,256]{1,0:T(8,128)S(1)}, bf16[512,256]{1,0:T(8,128)(2,1)S(1)}) custom-call(s32[1]{0:T(128)} %bitcast.me, bf16[512,1024]{1,0:T(8,128)(2,1)} %inputs.3, bf16[1024,1024]{1,0:T(8,128)(2,1)} %w_first.1, bf16[1024,256]{1,0:T(8,128)(2,1)} %rest_3_.1), custom_call_target="tpu_custom_call" | custom-call | tf_op jit(solution)/shard_map/pallas_call | solution.py:411
  6.0 2.6 %collective-permute-start = (bf16[512,256]{1,0:T(8,128)(2,1)S(1)}, bf16[512,256]{1,0:T(8,128)(2,1)S(1)}, u32[]{:S(2)}, u32[]{:S(2)}) collective-permute-start(bf16[512,256]{1,0:T(8,128)(2,1)S(1)} %get-tuple-element.20.rest_0_), channel_id=1, source_target_pairs={{6,0},{7,1},{0,2},{1,3},{2,4},{3,5},{4,6},{5,7},{14,8},{15,9},{8,1... | collective-permute-start | bytes 786440 | tf_op jit(solution)/shard_map/ppermute | solution.py:389
  8.6 1.5 %collective-permute-start.6 = (bf16[512,256]{1,0:T(8,128)(2,1)S(1)}, bf16[512,256]{1,0:T(8,128)(2,1)S(1)}, u32[]{:S(2)}, u32[]{:S(2)}) collective-permute-start(bf16[512,256]{1,0:T(8,128)(2,1)S(1)} %get-tuple-element.20.rest_0_), channel_id=1, source_target_pairs={{0,16},{8,24},{16,0},{24,8},{1,17},{9,25},{17,1},{25,9},{2,18},{10... | collective-permute-start | bytes 786440 | tf_op jit(solution)/shard_map/ppermute | solution.py:393
  10.6 1.5 %collective-permute-start.4 = (bf16[512,256]{1,0:T(8,128)(2,1)S(1)}, bf16[512,256]{1,0:T(8,128)(2,1)S(1)}, u32[]{:S(2)}, u32[]{:S(2)}) collective-permute-start(bf16[512,256]{1,0:T(8,128)(2,1)S(1)} %get-tuple-element.20.rest_0_), channel_id=1, source_target_pairs={{0,1},{1,0},{2,3},{3,2},{4,5},{5,4},{6,7},{7,6},{8,9},{9,8},{10,11... | collective-permute-start | bytes 786440 | tf_op jit(solution)/shard_map/ppermute | solution.py:393
  12.2 5.4 %collective-permute-done.rest_0_ = bf16[512,256]{1,0:T(8,128)(2,1)S(1)} collective-permute-done((bf16[512,256]{1,0:T(8,128)(2,1)S(1)}, bf16[512,256]{1,0:T(8,128)(2,1)S(1)}, u32[]{:S(2)}, u32[]{:S(2)}) %collective-permute-start) | collective-permute-done | bytes 262176 | tf_op jit(solution)/shard_map/ppermute | solution.py:389
  17.5 1.5 %collective-permute-start.2 = (bf16[512,256]{1,0:T(8,128)(2,1)S(1)}, bf16[512,256]{1,0:T(8,128)(2,1)S(1)}, u32[]{:S(2)}, u32[]{:S(2)}) collective-permute-start(bf16[512,256]{1,0:T(8,128)(2,1)S(1)} %collective-permute-done.rest_0_), channel_id=1, source_target_pairs={{0,1},{1,0},{2,3},{3,2},{4,5},{5,4},{6,7},{7,6},{8,9},{9,8},{10,11... | collective-permute-start | bytes 786440 | tf_op jit(solution)/shard_map/ppermute | solution.py:393
  19.1 1.5 %collective-permute-start.1 = (bf16[512,256]{1,0:T(8,128)(2,1)S(1)}, bf16[512,256]{1,0:T(8,128)(2,1)S(1)}, u32[]{:S(2)}, u32[]{:S(2)}) collective-permute-start(bf16[512,256]{1,0:T(8,128)(2,1)S(1)} %collective-permute-done.rest_0_), channel_id=1, source_target_pairs={{7,0},{1,2},{3,4},{5,6},{15,8},{9,10},{11,12},{13,14},{23,16},{17,... | collective-permute-start | bytes 786440 | tf_op jit(solution)/shard_map/ppermute | solution.py:435
  21.2 1.8 %shard_map.96.weight = bf16[512,512]{1,0:T(8,128)(2,1)S(1)} custom-call(s32[15,512]{1,0:T(8,128)S(1)} %bitcast.12, s32[1,512]{1,0:T(1,128)S(1)} %bitcast.14, s32[15,512]{1,0:T(8,128)S(1)} %bitcast.13), custom_call_target="tpu_custom_call" | custom-call | tf_op jit(solution)/shard_map/pallas_call | solution.py:454
  23.0 1.8 %shard_map.97.grad = f32[512,256]{1,0:T(8,128)S(1)} custom-call(s32[1]{0:T(128)} %bitcast.me, s32[4]{0:T(128)S(1)} %copy-done.4, f32[512,256]{1,0:T(8,128)S(1)} %get-tuple-element.19.codes, bf16[512,256]{1,0:T(8,128)(2,1)S(1)} %collective-permute-done.rest_0_), custom_call_target="tpu_custom_call" | custom-call | tf_op jit(solution)/shard_map/pallas_call | solution.py:467
  24.8 2.6 %shard_map.98.rest_2_ = f32[512,256]{1,0:T(8,128)S(1)} custom-call(s32[1]{0:T(128)} %bitcast.me, f32[512,256]{1,0:T(8,128)S(1)} %get-tuple-element.19.codes, s32[4,128]{1,0:T(4,128)S(1)} %copy-done.6, bf16[512,512]{1,0:T(8,128)(2,1)S(1)} %shard_map.96.weight, f32[512,256]{1,0:T(8,128)S(1)} %shard_map.97.grad, ...), custom_call_target="tpu_custom_call" | custom-call | tf_op jit(solution)/shard_map/pallas_call | solution.py:470
  27.5 1.8 %shard_map.99.rest_1_ = f32[512,256]{1,0:T(8,128)S(1)} custom-call(s32[1]{0:T(128)} %bitcast.me, s32[4]{0:T(128)S(1)} %copy-done.4, f32[512,256]{1,0:T(8,128)S(1)} %get-tuple-element.19.codes, bf16[512,256]{1,0:T(8,128)(2,1)S(1)} %collective-permute-done.2.rest_0_.rest_1_, bf16[512,256]{1,0:T(8,128)(2,1)S(1)} %collective-permute-done.4.rest_1_, ...), custom_call_target="tpu_custom_call" | custom-call | tf_op jit(solution)/shard_map/pallas_call | solution.py:467
  29.3 1.8 %shard_map.100.rest_2_ = f32[512,256]{1,0:T(8,128)S(1)} custom-call(s32[1]{0:T(128)} %bitcast.me, s32[4]{0:T(128)S(1)} %copy-done.4, f32[512,256]{1,0:T(8,128)S(1)} %get-tuple-element.19.codes, bf16[512,256]{1,0:T(8,128)(2,1)S(1)} %collective-permute-done.3.rest_0_, f32[512,256]{1,0:T(8,128)S(1)} %shard_map.99.rest_1_), custom_call_target="tpu_custom_call" | custom-call | tf_op jit(solution)/shard_map/pallas_call | solution.py:467
  31.1 3.2 %collective-permute-done.1.rest_0_ = bf16[512,256]{1,0:T(8,128)(2,1)S(1)} collective-permute-done((bf16[512,256]{1,0:T(8,128)(2,1)S(1)}, bf16[512,256]{1,0:T(8,128)(2,1)S(1)}, u32[]{:S(2)}, u32[]{:S(2)}) %collective-permute-start.1) | collective-permute-done | bytes 262176 | tf_op jit(solution)/shard_map/ppermute | solution.py:435
  34.2 3.1 %shard_map.102 = (s16[2,256,1408]{2,1,0:T(8,128)(2,1)S(1)}, bf16[512,256]{1,0:T(8,128)(2,1)S(1)}, bf16[512,1024]{1,0:T(8,128)(2,1)S(1)}) custom-call(s32[1]{0:T(128)} %bitcast.me, s32[4]{0:T(128)S(1)} %copy-done.4, f32[512,256]{1,0:T(8,128)S(1)} %get-tuple-element.19.codes, bf16[512,256]{1,0:T(8,128)(2,1)S(1)} %collective-permute-done.1.rest_0_, ...), custom_call_target="tpu_custom_call" | custom-call | tf_op jit(solution)/shard_map/pallas_call | solution.py:507
  38.3 2.3 %collective-permute-done.8 = s16[2,256,1408]{2,1,0:T(8,128)(2,1)S(1)} collective-permute-done((s16[2,256,1408]{2,1,0:T(8,128)(2,1)S(1)}, s16[2,256,1408]{2,1,0:T(8,128)(2,1)S(1)}, u32[]{:S(2)}, u32[]{:S(2)}) %collective-permute-start.8) | collective-permute-done | bytes 1441824 | tf_op jit(solution)/shard_map/ppermute | solution.py:393
  41.2 1.3 %collective-permute-start.9 = (s16[81,16,128]{2,1,0:T(8,128)(2,1)S(1)}, s16[81,16,128]{2,1,0:T(8,128)(2,1)S(1)}, u32[]{:S(2)}, u32[]{:S(2)}) collective-permute-start(s16[81,16,128]{2,1,0:T(8,128)(2,1)S(1)} %shard_map.105), channel_id=1, source_target_pairs={{0,16},{8,24},{16,0},{24,8},{1,17},{9,25},{17,1},{25,9},{2,18},{10... | collective-permute-start | bytes 995336 | tf_op jit(solution)/shard_map/ppermute | solution.py:393
  43.3 7.9 %collective-permute-done.9.p_got = s16[81,16,128]{2,1,0:T(8,128)(2,1)S(1)} collective-permute-done((s16[81,16,128]{2,1,0:T(8,128)(2,1)S(1)}, s16[81,16,128]{2,1,0:T(8,128)(2,1)S(1)}, u32[]{:S(2)}, u32[]{:S(2)}) %collective-permute-start.9) | collective-permute-done | bytes 331808 | tf_op jit(solution)/shard_map/ppermute | solution.py:393
  51.1 1.0 %collective-permute-done.10.q_got = s16[81,16,128]{2,1,0:T(8,128)(2,1)S(1)} collective-permute-done((s16[81,16,128]{2,1,0:T(8,128)(2,1)S(1)}, s16[81,16,128]{2,1,0:T(8,128)(2,1)S(1)}, u32[]{:S(2)}, u32[]{:S(2)}) %collective-permute-start.10) | collective-permute-done | bytes 331808 | tf_op jit(solution)/shard_map/ppermute | solution.py:393
  53.7 4.2 %collective-permute-done.11.p_got = s16[41,16,128]{2,1,0:T(8,128)(2,1)S(1)} collective-permute-done((s16[41,16,128]{2,1,0:T(8,128)(2,1)S(1)}, s16[41,16,128]{2,1,0:T(8,128)(2,1)S(1)}, u32[]{:S(2)}, u32[]{:S(2)}) %collective-permute-start.11) | collective-permute-done | bytes 167968 | tf_op jit(solution)/shard_map/ppermute | solution.py:393
  58.6 1.6 %collective-permute-start.13 = (s16[21,16,128]{2,1,0:T(8,128)(2,1)S(1)}, s16[21,16,128]{2,1,0:T(8,128)(2,1)S(1)}, u32[]{:S(2)}, u32[]{:S(2)}) collective-permute-start(s16[21,16,128]{2,1,0:T(8,128)(2,1)S(1)} %get-tuple-element.33), channel_id=1, source_target_pairs={{0,2},{1,3},{2,0},{3,1},{4,6},{5,7},{6,4},{7,5},{8,10},{9,11},{10,... | collective-permute-start | bytes 258056 | tf_op jit(solution)/shard_map/ppermute | solution.py:393
  60.3 1.6 %collective-permute-start.14 = (s16[21,16,128]{2,1,0:T(8,128)(2,1)S(1)}, s16[21,16,128]{2,1,0:T(8,128)(2,1)S(1)}, u32[]{:S(2)}, u32[]{:S(2)}) collective-permute-start(s16[21,16,128]{2,1,0:T(8,128)(2,1)S(1)} %get-tuple-element.34), channel_id=1, source_target_pairs={{0,4},{1,5},{2,6},{3,7},{4,0},{5,1},{6,2},{7,3},{8,12},{9,13},{10,... | collective-permute-start | bytes 258056 | tf_op jit(solution)/shard_map/ppermute | solution.py:393
  61.8 1.4 %collective-permute-start.15 = (s16[21,16,128]{2,1,0:T(8,128)(2,1)S(1)}, s16[21,16,128]{2,1,0:T(8,128)(2,1)S(1)}, u32[]{:S(2)}, u32[]{:S(2)}) collective-permute-start(s16[21,16,128]{2,1,0:T(8,128)(2,1)S(1)} %get-tuple-element.35), channel_id=1, source_target_pairs={{0,6},{1,7},{2,4},{3,5},{4,2},{5,3},{6,0},{7,1},{8,14},{9,15},{10,... | collective-permute-start | bytes 258056 | tf_op jit(solution)/shard_map/ppermute | solution.py:393
  63.3 3.8 %collective-permute-done.14.refs_1_ = s16[21,16,128]{2,1,0:T(8,128)(2,1)S(1)} collective-permute-done((s16[21,16,128]{2,1,0:T(8,128)(2,1)S(1)}, s16[21,16,128]{2,1,0:T(8,128)(2,1)S(1)}, u32[]{:S(2)}, u32[]{:S(2)}) %collective-permute-start.14) | collective-permute-done | bytes 86048 | tf_op jit(solution)/shard_map/ppermute | solution.py:393
  67.2 1.0 %collective-permute-done.15.refs_2_ = s16[21,16,128]{2,1,0:T(8,128)(2,1)S(1)} collective-permute-done((s16[21,16,128]{2,1,0:T(8,128)(2,1)S(1)}, s16[21,16,128]{2,1,0:T(8,128)(2,1)S(1)}, u32[]{:S(2)}, u32[]{:S(2)}) %collective-permute-start.15) | collective-permute-done | bytes 86048 | tf_op jit(solution)/shard_map/ppermute | solution.py:393
  68.5 2.4 %collective-permute-start.22 = (s16[21,16,128]{2,1,0:T(8,128)(2,1)S(1)}, s16[21,16,128]{2,1,0:T(8,128)(2,1)S(1)}, u32[]{:S(2)}, u32[]{:S(2)}) collective-permute-start(s16[21,16,128]{2,1,0:T(8,128)(2,1)S(1)} %shard_map.111.refs_0_), channel_id=1, source_target_pairs={{0,7},{1,6},{2,5},{3,4},{4,3},{5,2},{6,1},{7,0},{8,15},{9,14},{10,... | collective-permute-start | bytes 258056 | tf_op jit(solution)/shard_map/ppermute | solution.py:393
  70.9 1.3 %collective-permute-start.21 = (s16[21,16,128]{2,1,0:T(8,128)(2,1)S(1)}, s16[21,16,128]{2,1,0:T(8,128)(2,1)S(1)}, u32[]{:S(2)}, u32[]{:S(2)}) collective-permute-start(s16[21,16,128]{2,1,0:T(8,128)(2,1)S(1)} %shard_map.111.refs_0_), channel_id=1, source_target_pairs={{0,6},{1,7},{2,4},{3,5},{4,2},{5,3},{6,0},{7,1},{8,14},{9,15},{10,... | collective-permute-start | bytes 258056 | tf_op jit(solution)/shard_map/ppermute | solution.py:393
  72.2 1.6 %collective-permute-start.20 = (s16[21,16,128]{2,1,0:T(8,128)(2,1)S(1)}, s16[21,16,128]{2,1,0:T(8,128)(2,1)S(1)}, u32[]{:S(2)}, u32[]{:S(2)}) collective-permute-start(s16[21,16,128]{2,1,0:T(8,128)(2,1)S(1)} %shard_map.111.refs_0_), channel_id=1, source_target_pairs={{0,5},{1,4},{2,7},{3,6},{4,1},{5,0},{6,3},{7,2},{8,13},{9,12},{10,... | collective-permute-start | bytes 258056 | tf_op jit(solution)/shard_map/ppermute | solution.py:393
  73.8 2.3 %collective-permute-start.19 = (s16[21,16,128]{2,1,0:T(8,128)(2,1)S(1)}, s16[21,16,128]{2,1,0:T(8,128)(2,1)S(1)}, u32[]{:S(2)}, u32[]{:S(2)}) collective-permute-start(s16[21,16,128]{2,1,0:T(8,128)(2,1)S(1)} %shard_map.111.refs_0_), channel_id=1, source_target_pairs={{0,4},{1,5},{2,6},{3,7},{4,0},{5,1},{6,2},{7,3},{8,12},{9,13},{10,... | collective-permute-start | bytes 258056 | tf_op jit(solution)/shard_map/ppermute | solution.py:393
  76.6 3.5 %collective-permute-start.17 = (s16[21,16,128]{2,1,0:T(8,128)(2,1)S(1)}, s16[21,16,128]{2,1,0:T(8,128)(2,1)S(1)}, u32[]{:S(2)}, u32[]{:S(2)}) collective-permute-start(s16[21,16,128]{2,1,0:T(8,128)(2,1)S(1)} %shard_map.111.refs_0_), channel_id=1, source_target_pairs={{0,2},{1,3},{2,0},{3,1},{4,6},{5,7},{6,4},{7,5},{8,10},{9,11},{10,... | collective-permute-start | bytes 258056 | tf_op jit(solution)/shard_map/ppermute | solution.py:393
  80.1 1.7 %collective-permute-start.16 = (s16[21,16,128]{2,1,0:T(8,128)(2,1)S(1)}, s16[21,16,128]{2,1,0:T(8,128)(2,1)S(1)}, u32[]{:S(2)}, u32[]{:S(2)}) collective-permute-start(s16[21,16,128]{2,1,0:T(8,128)(2,1)S(1)} %shard_map.111.refs_0_), channel_id=1, source_target_pairs={{0,1},{1,0},{2,3},{3,2},{4,5},{5,4},{6,7},{7,6},{8,9},{9,8},{10,11... | collective-permute-start | bytes 258056 | tf_op jit(solution)/shard_map/ppermute | solution.py:393
  81.8 2.4 %collective-permute-done.20.refs_5_ = s16[21,16,128]{2,1,0:T(8,128)(2,1)S(1)} collective-permute-done((s16[21,16,128]{2,1,0:T(8,128)(2,1)S(1)}, s16[21,16,128]{2,1,0:T(8,128)(2,1)S(1)}, u32[]{:S(2)}, u32[]{:S(2)}) %collective-permute-start.20) | collective-permute-done | bytes 86048 | tf_op jit(solution)/shard_map/ppermute | solution.py:393
  85.1 1.2 %shard_map.112 = (f32[256,1024]{1,0:T(8,128)}, f32[256,256]{1,0:T(8,128)}) custom-call(s32[1]{0:T(128)} %bitcast.me, s16[21,16,128]{2,1,0:T(8,128)(2,1)S(1)} %shard_map.111.refs_0_, s16[21,16,128]{2,1,0:T(8,128)(2,1)S(1)} %collective-permute-done.16.refs_1_, s16[21,16,128]{2,1,0:T(8,128)(2,1)S(1)} %collective-permute-done.17.refs_2_, ...), custom_call_target="tpu_custom_call" | custom-call | tf_op jit(solution)/shard_map/pallas_call | solution.py:531
  (46 shorter events, 7.9 us)
Async XLA Ops:
  0.6 19.9 %copy-start = (bf16[512,1024]{1,0:T(8,128)(2,1)S(1)}, bf16[512,1024]{1,0:T(8,128)(2,1)}, u32[]{:S(2)}) copy-start(bf16[512,1024]{1,0:T(8,128)(2,1)} %inputs.3) | copy-start | bytes 3145732
  0.6 20.5 %copy-start.2 = (s32[512,15]{0,1:T(8,128)S(1)}, s32[512,15]{0,1:T(8,128)}, u32[]{:S(2)}) copy-start(s32[512,15]{0,1:T(8,128)} %param.12) | copy-start | bytes 92164
  0.7 20.5 %copy-start.3 = (s32[512,15]{0,1:T(8,128)S(1)}, s32[512,15]{0,1:T(8,128)}, u32[]{:S(2)}) copy-start(s32[512,15]{0,1:T(8,128)} %param.14) | copy-start | bytes 92164
  0.7 20.5 %copy-start.5 = (s32[512]{0:T(512)S(1)}, s32[512]{0:T(512)}, u32[]{:S(2)}) copy-start(s32[512]{0:T(512)} %param.13) | copy-start | bytes 6148
  5.4 17.6 %copy-start.4 = (s32[4]{0:T(128)S(1)}, s32[4]{0:T(128)}, u32[]{:S(2)}) copy-start(s32[4]{0:T(128)} %offsets.7) | copy-start | bytes 52
  5.4 19.4 %copy-start.6 = (s32[4,128]{1,0:T(4,128)S(1)}, s32[4,128]{1,0:T(4,128)}, u32[]{:S(2)}) copy-start(s32[4,128]{1,0:T(4,128)} %requests.1) | copy-start | bytes 6148
  5.4 4.7 %collective-permute-start.5 = (bf16[512,256]{1,0:T(8,128)(2,1)S(1)}, bf16[512,256]{1,0:T(8,128)(2,1)S(1)}, u32[]{:S(2)}, u32[]{:S(2)}) collective-permute-start(bf16[512,256]{1,0:T(8,128)(2,1)S(1)} %get-tuple-element.20.rest_0_), channel_id=1, source_target_pairs={{0,8},{8,0},{16,24},{24,16},{1,9},{9,1},{17,25},{25,17},{2,10},{10... | collective-permute-start | bytes 786440 | tf_op jit(solution)/shard_map/ppermute | solution.py:393
  6.0 11.6 %collective-permute-start = (bf16[512,256]{1,0:T(8,128)(2,1)S(1)}, bf16[512,256]{1,0:T(8,128)(2,1)S(1)}, u32[]{:S(2)}, u32[]{:S(2)}) collective-permute-start(bf16[512,256]{1,0:T(8,128)(2,1)S(1)} %get-tuple-element.20.rest_0_), channel_id=1, source_target_pairs={{6,0},{7,1},{0,2},{1,3},{2,4},{3,5},{4,6},{5,7},{14,8},{15,9},{8,1... | collective-permute-start | bytes 786440 | tf_op jit(solution)/shard_map/ppermute | solution.py:389
  8.6 10.5 %collective-permute-start.6 = (bf16[512,256]{1,0:T(8,128)(2,1)S(1)}, bf16[512,256]{1,0:T(8,128)(2,1)S(1)}, u32[]{:S(2)}, u32[]{:S(2)}) collective-permute-start(bf16[512,256]{1,0:T(8,128)(2,1)S(1)} %get-tuple-element.20.rest_0_), channel_id=1, source_target_pairs={{0,16},{8,24},{16,0},{24,8},{1,17},{9,25},{17,1},{25,9},{2,18},{10... | collective-permute-start | bytes 786440 | tf_op jit(solution)/shard_map/ppermute | solution.py:393
  10.1 14.7 %collective-permute-start.7 = (bf16[512,256]{1,0:T(8,128)(2,1)S(1)}, bf16[512,256]{1,0:T(8,128)(2,1)S(1)}, u32[]{:S(2)}, u32[]{:S(2)}) collective-permute-start(bf16[512,256]{1,0:T(8,128)(2,1)S(1)} %collective-permute-done.5.rest_1_), channel_id=1, source_target_pairs={{0,16},{8,24},{16,0},{24,8},{1,17},{9,25},{17,1},{25,9},{2,18},{10... | collective-permute-start | bytes 786440 | tf_op jit(solution)/shard_map/ppermute | solution.py:393
  10.6 16.8 %collective-permute-start.4 = (bf16[512,256]{1,0:T(8,128)(2,1)S(1)}, bf16[512,256]{1,0:T(8,128)(2,1)S(1)}, u32[]{:S(2)}, u32[]{:S(2)}) collective-permute-start(bf16[512,256]{1,0:T(8,128)(2,1)S(1)} %get-tuple-element.20.rest_0_), channel_id=1, source_target_pairs={{0,1},{1,0},{2,3},{3,2},{4,5},{5,4},{6,7},{7,6},{8,9},{9,8},{10,11... | collective-permute-start | bytes 786440 | tf_op jit(solution)/shard_map/ppermute | solution.py:393
  17.5 9.9 %collective-permute-start.2 = (bf16[512,256]{1,0:T(8,128)(2,1)S(1)}, bf16[512,256]{1,0:T(8,128)(2,1)S(1)}, u32[]{:S(2)}, u32[]{:S(2)}) collective-permute-start(bf16[512,256]{1,0:T(8,128)(2,1)S(1)} %collective-permute-done.rest_0_), channel_id=1, source_target_pairs={{0,1},{1,0},{2,3},{3,2},{4,5},{5,4},{6,7},{7,6},{8,9},{9,8},{10,11... | collective-permute-start | bytes 786440 | tf_op jit(solution)/shard_map/ppermute | solution.py:393
  19.1 10.2 %collective-permute-start.3 = (bf16[512,256]{1,0:T(8,128)(2,1)S(1)}, bf16[512,256]{1,0:T(8,128)(2,1)S(1)}, u32[]{:S(2)}, u32[]{:S(2)}) collective-permute-start(bf16[512,256]{1,0:T(8,128)(2,1)S(1)} %collective-permute-done.rest_0_), channel_id=1, source_target_pairs={{6,0},{7,1},{0,2},{1,3},{2,4},{3,5},{4,6},{5,7},{14,8},{15,9},{8,1... | collective-permute-start | bytes 786440 | tf_op jit(solution)/shard_map/ppermute | solution.py:389
  19.1 15.1 %collective-permute-start.1 = (bf16[512,256]{1,0:T(8,128)(2,1)S(1)}, bf16[512,256]{1,0:T(8,128)(2,1)S(1)}, u32[]{:S(2)}, u32[]{:S(2)}) collective-permute-start(bf16[512,256]{1,0:T(8,128)(2,1)S(1)} %collective-permute-done.rest_0_), channel_id=1, source_target_pairs={{7,0},{1,2},{3,4},{5,6},{15,8},{9,10},{11,12},{13,14},{23,16},{17,... | collective-permute-start | bytes 786440 | tf_op jit(solution)/shard_map/ppermute | solution.py:435
  27.5 6.8 %copy-start.1 = (bf16[1024,256]{1,0:T(8,128)(2,1)S(1)}, bf16[1024,256]{1,0:T(8,128)(2,1)}, u32[]{:S(2)}) copy-start(bf16[1024,256]{1,0:T(8,128)(2,1)} %rest_3_.1) | copy-start | bytes 1572868
  37.3 3.3 %collective-permute-start.8 = (s16[2,256,1408]{2,1,0:T(8,128)(2,1)S(1)}, s16[2,256,1408]{2,1,0:T(8,128)(2,1)S(1)}, u32[]{:S(2)}, u32[]{:S(2)}) collective-permute-start(s16[2,256,1408]{2,1,0:T(8,128)(2,1)S(1)} %get-tuple-element.26), channel_id=1, source_target_pairs={{0,8},{8,0},{16,24},{24,16},{1,9},{9,1},{17,25},{25,17},{2,10},{10... | collective-permute-start | bytes 4325384 | tf_op jit(solution)/shard_map/ppermute | solution.py:393
  41.2 9.9 %collective-permute-start.9 = (s16[81,16,128]{2,1,0:T(8,128)(2,1)S(1)}, s16[81,16,128]{2,1,0:T(8,128)(2,1)S(1)}, u32[]{:S(2)}, u32[]{:S(2)}) collective-permute-start(s16[81,16,128]{2,1,0:T(8,128)(2,1)S(1)} %shard_map.105), channel_id=1, source_target_pairs={{0,16},{8,24},{16,0},{24,8},{1,17},{9,25},{17,1},{25,9},{2,18},{10... | collective-permute-start | bytes 995336 | tf_op jit(solution)/shard_map/ppermute | solution.py:393
  42.6 9.6 %collective-permute-start.10 = (s16[81,16,128]{2,1,0:T(8,128)(2,1)S(1)}, s16[81,16,128]{2,1,0:T(8,128)(2,1)S(1)}, u32[]{:S(2)}, u32[]{:S(2)}) collective-permute-start(s16[81,16,128]{2,1,0:T(8,128)(2,1)S(1)} %shard_map.106), channel_id=1, source_target_pairs={{0,1},{1,0},{2,3},{3,2},{4,5},{5,4},{6,7},{7,6},{8,9},{9,8},{10,11... | collective-permute-start | bytes 995336 | tf_op jit(solution)/shard_map/ppermute | solution.py:393
  52.4 5.4 %collective-permute-start.11 = (s16[41,16,128]{2,1,0:T(8,128)(2,1)S(1)}, s16[41,16,128]{2,1,0:T(8,128)(2,1)S(1)}, u32[]{:S(2)}, u32[]{:S(2)}) collective-permute-start(s16[41,16,128]{2,1,0:T(8,128)(2,1)S(1)} %get-tuple-element.31), channel_id=1, source_target_pairs={{0,1},{1,0},{2,3},{3,2},{4,5},{5,4},{6,7},{7,6},{8,9},{9,8},{10,11... | collective-permute-start | bytes 503816 | tf_op jit(solution)/shard_map/ppermute | solution.py:393
  53.0 5.4 %collective-permute-start.12 = (s16[41,16,128]{2,1,0:T(8,128)(2,1)S(1)}, s16[41,16,128]{2,1,0:T(8,128)(2,1)S(1)}, u32[]{:S(2)}, u32[]{:S(2)}) collective-permute-start(s16[41,16,128]{2,1,0:T(8,128)(2,1)S(1)} %get-tuple-element.32), channel_id=1, source_target_pairs={{0,16},{8,24},{16,0},{24,8},{1,17},{9,25},{17,1},{25,9},{2,18},{10... | collective-permute-start | bytes 503816 | tf_op jit(solution)/shard_map/ppermute | solution.py:393
  58.6 4.7 %collective-permute-start.13 = (s16[21,16,128]{2,1,0:T(8,128)(2,1)S(1)}, s16[21,16,128]{2,1,0:T(8,128)(2,1)S(1)}, u32[]{:S(2)}, u32[]{:S(2)}) collective-permute-start(s16[21,16,128]{2,1,0:T(8,128)(2,1)S(1)} %get-tuple-element.33), channel_id=1, source_target_pairs={{0,2},{1,3},{2,0},{3,1},{4,6},{5,7},{6,4},{7,5},{8,10},{9,11},{10,... | collective-permute-start | bytes 258056 | tf_op jit(solution)/shard_map/ppermute | solution.py:393
  60.3 6.9 %collective-permute-start.14 = (s16[21,16,128]{2,1,0:T(8,128)(2,1)S(1)}, s16[21,16,128]{2,1,0:T(8,128)(2,1)S(1)}, u32[]{:S(2)}, u32[]{:S(2)}) collective-permute-start(s16[21,16,128]{2,1,0:T(8,128)(2,1)S(1)} %get-tuple-element.34), channel_id=1, source_target_pairs={{0,4},{1,5},{2,6},{3,7},{4,0},{5,1},{6,2},{7,3},{8,12},{9,13},{10,... | collective-permute-start | bytes 258056 | tf_op jit(solution)/shard_map/ppermute | solution.py:393
  61.8 6.4 %collective-permute-start.15 = (s16[21,16,128]{2,1,0:T(8,128)(2,1)S(1)}, s16[21,16,128]{2,1,0:T(8,128)(2,1)S(1)}, u32[]{:S(2)}, u32[]{:S(2)}) collective-permute-start(s16[21,16,128]{2,1,0:T(8,128)(2,1)S(1)} %get-tuple-element.35), channel_id=1, source_target_pairs={{0,6},{1,7},{2,4},{3,5},{4,2},{5,3},{6,0},{7,1},{8,14},{9,15},{10,... | collective-permute-start | bytes 258056 | tf_op jit(solution)/shard_map/ppermute | solution.py:393
  68.5 8.1 %collective-permute-start.22 = (s16[21,16,128]{2,1,0:T(8,128)(2,1)S(1)}, s16[21,16,128]{2,1,0:T(8,128)(2,1)S(1)}, u32[]{:S(2)}, u32[]{:S(2)}) collective-permute-start(s16[21,16,128]{2,1,0:T(8,128)(2,1)S(1)} %shard_map.111.refs_0_), channel_id=1, source_target_pairs={{0,7},{1,6},{2,5},{3,4},{4,3},{5,2},{6,1},{7,0},{8,15},{9,14},{10,... | collective-permute-start | bytes 258056 | tf_op jit(solution)/shard_map/ppermute | solution.py:393
  70.9 9.2 %collective-permute-start.21 = (s16[21,16,128]{2,1,0:T(8,128)(2,1)S(1)}, s16[21,16,128]{2,1,0:T(8,128)(2,1)S(1)}, u32[]{:S(2)}, u32[]{:S(2)}) collective-permute-start(s16[21,16,128]{2,1,0:T(8,128)(2,1)S(1)} %shard_map.111.refs_0_), channel_id=1, source_target_pairs={{0,6},{1,7},{2,4},{3,5},{4,2},{5,3},{6,0},{7,1},{8,14},{9,15},{10,... | collective-permute-start | bytes 258056 | tf_op jit(solution)/shard_map/ppermute | solution.py:393
  72.2 12.0 %collective-permute-start.20 = (s16[21,16,128]{2,1,0:T(8,128)(2,1)S(1)}, s16[21,16,128]{2,1,0:T(8,128)(2,1)S(1)}, u32[]{:S(2)}, u32[]{:S(2)}) collective-permute-start(s16[21,16,128]{2,1,0:T(8,128)(2,1)S(1)} %shard_map.111.refs_0_), channel_id=1, source_target_pairs={{0,5},{1,4},{2,7},{3,6},{4,1},{5,0},{6,3},{7,2},{8,13},{9,12},{10,... | collective-permute-start | bytes 258056 | tf_op jit(solution)/shard_map/ppermute | solution.py:393
  73.8 10.5 %collective-permute-start.19 = (s16[21,16,128]{2,1,0:T(8,128)(2,1)S(1)}, s16[21,16,128]{2,1,0:T(8,128)(2,1)S(1)}, u32[]{:S(2)}, u32[]{:S(2)}) collective-permute-start(s16[21,16,128]{2,1,0:T(8,128)(2,1)S(1)} %shard_map.111.refs_0_), channel_id=1, source_target_pairs={{0,4},{1,5},{2,6},{3,7},{4,0},{5,1},{6,2},{7,3},{8,12},{9,13},{10,... | collective-permute-start | bytes 258056 | tf_op jit(solution)/shard_map/ppermute | solution.py:393
  76.2 8.2 %collective-permute-start.18 = (s16[21,16,128]{2,1,0:T(8,128)(2,1)S(1)}, s16[21,16,128]{2,1,0:T(8,128)(2,1)S(1)}, u32[]{:S(2)}, u32[]{:S(2)}) collective-permute-start(s16[21,16,128]{2,1,0:T(8,128)(2,1)S(1)} %shard_map.111.refs_0_), channel_id=1, source_target_pairs={{0,3},{1,2},{2,1},{3,0},{4,7},{5,6},{6,5},{7,4},{8,11},{9,10},{10,... | collective-permute-start | bytes 258056 | tf_op jit(solution)/shard_map/ppermute | solution.py:393
  76.6 8.4 %collective-permute-start.17 = (s16[21,16,128]{2,1,0:T(8,128)(2,1)S(1)}, s16[21,16,128]{2,1,0:T(8,128)(2,1)S(1)}, u32[]{:S(2)}, u32[]{:S(2)}) collective-permute-start(s16[21,16,128]{2,1,0:T(8,128)(2,1)S(1)} %shard_map.111.refs_0_), channel_id=1, source_target_pairs={{0,2},{1,3},{2,0},{3,1},{4,6},{5,7},{6,4},{7,5},{8,10},{9,11},{10,... | collective-permute-start | bytes 258056 | tf_op jit(solution)/shard_map/ppermute | solution.py:393
  80.1 5.0 %collective-permute-start.16 = (s16[21,16,128]{2,1,0:T(8,128)(2,1)S(1)}, s16[21,16,128]{2,1,0:T(8,128)(2,1)S(1)}, u32[]{:S(2)}, u32[]{:S(2)}) collective-permute-start(s16[21,16,128]{2,1,0:T(8,128)(2,1)S(1)} %shard_map.111.refs_0_), channel_id=1, source_target_pairs={{0,1},{1,0},{2,3},{3,2},{4,5},{5,4},{6,7},{7,6},{8,9},{9,8},{10,11... | collective-permute-start | bytes 258056 | tf_op jit(solution)/shard_map/ppermute | solution.py:393

commit v6 on v5

--- a/solution.py
+++ b/solution.py
@@ -407,7 +407,7 @@
     powers = peers & (peers - 1) == 0 and group & (group - 1) == 0 and peers > 1 and group > 1
     assert powers, "axis sizes"
     me = lax.axis_index(("wide", "narrow")).reshape(1).astype(jnp.int32)
-    count = 4 if hid % (4 * LANES) == 0 else 1
+    count = 2 if hid % (2 * LANES) == 0 else 1
     hidden, codes, sent = pl.pallas_call(
         forward_body,
         out_shape=(
@@ -551,7 +551,11 @@
     keep = do(functools.partial(deal_keep_body, first), plain(2, lines), (), rest)
     gots = [swapped(send, "narrow", 2 * k) for k, send in enumerate(sends, 1)]
     mine = do(functools.partial(close_body, first), message(2), (), (keep, *gots))
-    pieces = [mine] + [swapped(mine, "narrow", k) for k in range(1, group)]
+    held = {0: mine}
+    for k in range(1, group):
+        relayed = k % 2 == 1 and k > 3
+        held[k] = swapped(held[k - 1] if relayed else mine, "narrow", 1 if relayed else k)
+    pieces = [held[k] for k in range(group)]
     return do(
         functools.partial(spread_body, first),
         (

time: 86.5 us -> 82.5 us (0.954)
  starting transfers between devices: 30.3 us -> 23.8 us
  waiting for transfers between devices: 32.9 us -> 36 us
    ppermute x20, starting transfers between devices: 26.2 us -> 19.9 us  [swapped(): lax.ppermute(block, axis, [(i, i ^ bit) for i in range(lax.axis_size(axis...]
    ppermute x20, waiting for transfers between devices: 24.4 us -> 27.3 us  [swapped(): lax.ppermute(block, axis, [(i, i ^ bit) for i in range(lax.axis_size(axis...]
  transfers between devices with their start and end apart: 23 -> 23, of which waited for: 14 -> 15; matrix products, arithmetic and copies ran while one was open for 0% -> 0% of each run, Pallas kernels for 14% -> 14%
where the time goes in v6:
time: 82.5 us; the launch traced here: 82.3 us
  waiting for transfers between devices  36 us (44%)
  starting transfers between devices  23.8 us (29%)
  Pallas kernels  21.5 us (26%)
  between operations  0.93 us (1%)
    ppermute x20, waiting for transfers between devices, swapped(): lax.ppermute(block, axis, [(i, i ^ bit) for i in range(lax.axis_size(axis...  27.3 us
    ppermute x20, starting transfers between devices, swapped(): lax.ppermute(block, axis, [(i, i ^ bit) for i in range(lax.axis_size(axis...  19.9 us
    ppermute x2, waiting for transfers between devices, from_behind(): return lax.ppermute(block, axis, route)  5.4 us
    pallas_call x3, Pallas kernels, far(): call(body, like, 2, 1 + len(given), [twice])(me, offsets, codes, *given)  5.3 us
    pallas_call x1, Pallas kernels, shards(): pl.pallas_call(forward_body, out_shape=(jax.ShapeDtypeStruct((rows, hid),...  4.05 us
    ppermute x1, waiting for transfers between devices, shards(): lax.ppermute(two, 'narrow', [((n - 1) % group, n) for n in range(0, group...  3.34 us
    pallas_call x9, Pallas kernels, do(): return call(body, shapes, len(scalars), len(arrays))(*scalars, *arrays)  3.12 us
    pallas_call x1, Pallas kernels, shards(): call(functools.partial(give_body, step, scale, below), (coded(groups, lin...  3.1 us
  transfers between devices with their start and end apart: 23, of which 15 were waited for; matrix products, arithmetic and copies ran while one was open for 0% of the time, Pallas kernels for 14%

profile of v6, /device:TPU:0, one launch (start us, length us, event | category | flops | bytes accessed | tf_op | source)
XLA Modules:
  0.0 82.3 jit_solution(8628501621371725451)
XLA Ops:
  0.7 4.0 %shard_map.95 = (bf16[512,1024]{1,0:T(8,128)(2,1)S(1)}, f32[512,256]{1,0:T(8,128)S(1)}, bf16[512,256]{1,0:T(8,128)(2,1)S(1)}) custom-call(s32[1]{0:T(128)} %bitcast.me, bf16[512,1024]{1,0:T(8,128)(2,1)} %inputs.3, bf16[1024,1024]{1,0:T(8,128)(2,1)} %w_first.1, bf16[1024,256]{1,0:T(8,128)(2,1)} %rest_3_.1), custom_call_target="tpu_custom_call" | custom-call | tf_op jit(solution)/shard_map/pallas_call | solution.py:411
  5.3 2.6 %collective-permute-start = (bf16[512,256]{1,0:T(8,128)(2,1)S(1)}, bf16[512,256]{1,0:T(8,128)(2,1)S(1)}, u32[]{:S(2)}, u32[]{:S(2)}) collective-permute-start(bf16[512,256]{1,0:T(8,128)(2,1)S(1)} %get-tuple-element.20.rest_0_), channel_id=1, source_target_pairs={{6,0},{7,1},{0,2},{1,3},{2,4},{3,5},{4,6},{5,7},{14,8},{15,9},{8,1... | collective-permute-start | bytes 786440 | tf_op jit(solution)/shard_map/ppermute | solution.py:389
  7.9 1.5 %collective-permute-start.6 = (bf16[512,256]{1,0:T(8,128)(2,1)S(1)}, bf16[512,256]{1,0:T(8,128)(2,1)S(1)}, u32[]{:S(2)}, u32[]{:S(2)}) collective-permute-start(bf16[512,256]{1,0:T(8,128)(2,1)S(1)} %get-tuple-element.20.rest_0_), channel_id=1, source_target_pairs={{0,16},{8,24},{16,0},{24,8},{1,17},{9,25},{17,1},{25,9},{2,18},{10... | collective-permute-start | bytes 786440 | tf_op jit(solution)/shard_map/ppermute | solution.py:393
  10.0 1.5 %collective-permute-start.4 = (bf16[512,256]{1,0:T(8,128)(2,1)S(1)}, bf16[512,256]{1,0:T(8,128)(2,1)S(1)}, u32[]{:S(2)}, u32[]{:S(2)}) collective-permute-start(bf16[512,256]{1,0:T(8,128)(2,1)S(1)} %get-tuple-element.20.rest_0_), channel_id=1, source_target_pairs={{0,1},{1,0},{2,3},{3,2},{4,5},{5,4},{6,7},{7,6},{8,9},{9,8},{10,11... | collective-permute-start | bytes 786440 | tf_op jit(solution)/shard_map/ppermute | solution.py:393
  11.5 5.4 %collective-permute-done.rest_0_ = bf16[512,256]{1,0:T(8,128)(2,1)S(1)} collective-permute-done((bf16[512,256]{1,0:T(8,128)(2,1)S(1)}, bf16[512,256]{1,0:T(8,128)(2,1)S(1)}, u32[]{:S(2)}, u32[]{:S(2)}) %collective-permute-start) | collective-permute-done | bytes 262176 | tf_op jit(solution)/shard_map/ppermute | solution.py:389
  16.9 1.5 %collective-permute-start.2 = (bf16[512,256]{1,0:T(8,128)(2,1)S(1)}, bf16[512,256]{1,0:T(8,128)(2,1)S(1)}, u32[]{:S(2)}, u32[]{:S(2)}) collective-permute-start(bf16[512,256]{1,0:T(8,128)(2,1)S(1)} %collective-permute-done.rest_0_), channel_id=1, source_target_pairs={{0,1},{1,0},{2,3},{3,2},{4,5},{5,4},{6,7},{7,6},{8,9},{9,8},{10,11... | collective-permute-start | bytes 786440 | tf_op jit(solution)/shard_map/ppermute | solution.py:393
  18.4 1.3 %collective-permute-start.1 = (bf16[512,256]{1,0:T(8,128)(2,1)S(1)}, bf16[512,256]{1,0:T(8,128)(2,1)S(1)}, u32[]{:S(2)}, u32[]{:S(2)}) collective-permute-start(bf16[512,256]{1,0:T(8,128)(2,1)S(1)} %collective-permute-done.rest_0_), channel_id=1, source_target_pairs={{7,0},{1,2},{3,4},{5,6},{15,8},{9,10},{11,12},{13,14},{23,16},{17,... | collective-permute-start | bytes 786440 | tf_op jit(solution)/shard_map/ppermute | solution.py:435
  20.3 1.8 %shard_map.96.weight = bf16[512,512]{1,0:T(8,128)(2,1)S(1)} custom-call(s32[15,512]{1,0:T(8,128)S(1)} %bitcast.12, s32[1,512]{1,0:T(1,128)S(1)} %bitcast.14, s32[15,512]{1,0:T(8,128)S(1)} %bitcast.13), custom_call_target="tpu_custom_call" | custom-call | tf_op jit(solution)/shard_map/pallas_call | solution.py:454
  22.2 1.8 %shard_map.97.grad = f32[512,256]{1,0:T(8,128)S(1)} custom-call(s32[1]{0:T(128)} %bitcast.me, s32[4]{0:T(128)S(1)} %copy-done.4, f32[512,256]{1,0:T(8,128)S(1)} %get-tuple-element.19.codes, bf16[512,256]{1,0:T(8,128)(2,1)S(1)} %collective-permute-done.rest_0_), custom_call_target="tpu_custom_call" | custom-call | tf_op jit(solution)/shard_map/pallas_call | solution.py:467
  24.0 2.6 %shard_map.98.rest_2_ = f32[512,256]{1,0:T(8,128)S(1)} custom-call(s32[1]{0:T(128)} %bitcast.me, f32[512,256]{1,0:T(8,128)S(1)} %get-tuple-element.19.codes, s32[4,128]{1,0:T(4,128)S(1)} %copy-done.6, bf16[512,512]{1,0:T(8,128)(2,1)S(1)} %shard_map.96.weight, f32[512,256]{1,0:T(8,128)S(1)} %shard_map.97.grad, ...), custom_call_target="tpu_custom_call" | custom-call | tf_op jit(solution)/shard_map/pallas_call | solution.py:470
  26.6 1.8 %shard_map.99.rest_1_ = f32[512,256]{1,0:T(8,128)S(1)} custom-call(s32[1]{0:T(128)} %bitcast.me, s32[4]{0:T(128)S(1)} %copy-done.4, f32[512,256]{1,0:T(8,128)S(1)} %get-tuple-element.19.codes, bf16[512,256]{1,0:T(8,128)(2,1)S(1)} %collective-permute-done.2.rest_0_.rest_1_, bf16[512,256]{1,0:T(8,128)(2,1)S(1)} %collective-permute-done.4.rest_1_, ...), custom_call_target="tpu_custom_call" | custom-call | tf_op jit(solution)/shard_map/pallas_call | solution.py:467
  28.4 1.8 %shard_map.100.rest_2_ = f32[512,256]{1,0:T(8,128)S(1)} custom-call(s32[1]{0:T(128)} %bitcast.me, s32[4]{0:T(128)S(1)} %copy-done.4, f32[512,256]{1,0:T(8,128)S(1)} %get-tuple-element.19.codes, bf16[512,256]{1,0:T(8,128)(2,1)S(1)} %collective-permute-done.3.rest_0_, f32[512,256]{1,0:T(8,128)S(1)} %shard_map.99.rest_1_), custom_call_target="tpu_custom_call" | custom-call | tf_op jit(solution)/shard_map/pallas_call | solution.py:467
  30.2 3.3 %collective-permute-done.1.rest_0_ = bf16[512,256]{1,0:T(8,128)(2,1)S(1)} collective-permute-done((bf16[512,256]{1,0:T(8,128)(2,1)S(1)}, bf16[512,256]{1,0:T(8,128)(2,1)S(1)}, u32[]{:S(2)}, u32[]{:S(2)}) %collective-permute-start.1) | collective-permute-done | bytes 262176 | tf_op jit(solution)/shard_map/ppermute | solution.py:435
  33.6 3.1 %shard_map.102 = (s16[2,256,1408]{2,1,0:T(8,128)(2,1)S(1)}, bf16[512,256]{1,0:T(8,128)(2,1)S(1)}, bf16[512,1024]{1,0:T(8,128)(2,1)S(1)}) custom-call(s32[1]{0:T(128)} %bitcast.me, s32[4]{0:T(128)S(1)} %copy-done.4, f32[512,256]{1,0:T(8,128)S(1)} %get-tuple-element.19.codes, bf16[512,256]{1,0:T(8,128)(2,1)S(1)} %collective-permute-done.1.rest_0_, ...), custom_call_target="tpu_custom_call" | custom-call | tf_op jit(solution)/shard_map/pallas_call | solution.py:507
  37.6 2.3 %collective-permute-done.8 = s16[2,256,1408]{2,1,0:T(8,128)(2,1)S(1)} collective-permute-done((s16[2,256,1408]{2,1,0:T(8,128)(2,1)S(1)}, s16[2,256,1408]{2,1,0:T(8,128)(2,1)S(1)}, u32[]{:S(2)}, u32[]{:S(2)}) %collective-permute-start.8) | collective-permute-done | bytes 1441824 | tf_op jit(solution)/shard_map/ppermute | solution.py:393
  40.6 1.3 %collective-permute-start.9 = (s16[81,16,128]{2,1,0:T(8,128)(2,1)S(1)}, s16[81,16,128]{2,1,0:T(8,128)(2,1)S(1)}, u32[]{:S(2)}, u32[]{:S(2)}) collective-permute-start(s16[81,16,128]{2,1,0:T(8,128)(2,1)S(1)} %shard_map.105), channel_id=1, source_target_pairs={{0,16},{8,24},{16,0},{24,8},{1,17},{9,25},{17,1},{25,9},{2,18},{10... | collective-permute-start | bytes 995336 | tf_op jit(solution)/shard_map/ppermute | solution.py:393
  42.5 8.0 %collective-permute-done.9.p_got = s16[81,16,128]{2,1,0:T(8,128)(2,1)S(1)} collective-permute-done((s16[81,16,128]{2,1,0:T(8,128)(2,1)S(1)}, s16[81,16,128]{2,1,0:T(8,128)(2,1)S(1)}, u32[]{:S(2)}, u32[]{:S(2)}) %collective-permute-start.9) | collective-permute-done | bytes 331808 | tf_op jit(solution)/shard_map/ppermute | solution.py:393
  50.5 1.0 %collective-permute-done.10.q_got = s16[81,16,128]{2,1,0:T(8,128)(2,1)S(1)} collective-permute-done((s16[81,16,128]{2,1,0:T(8,128)(2,1)S(1)}, s16[81,16,128]{2,1,0:T(8,128)(2,1)S(1)}, u32[]{:S(2)}, u32[]{:S(2)}) %collective-permute-start.10) | collective-permute-done | bytes 331808 | tf_op jit(solution)/shard_map/ppermute | solution.py:393
  53.1 4.2 %collective-permute-done.11.p_got = s16[41,16,128]{2,1,0:T(8,128)(2,1)S(1)} collective-permute-done((s16[41,16,128]{2,1,0:T(8,128)(2,1)S(1)}, s16[41,16,128]{2,1,0:T(8,128)(2,1)S(1)}, u32[]{:S(2)}, u32[]{:S(2)}) %collective-permute-start.11) | collective-permute-done | bytes 167968 | tf_op jit(solution)/shard_map/ppermute | solution.py:393
  57.8 1.6 %collective-permute-start.13 = (s16[21,16,128]{2,1,0:T(8,128)(2,1)S(1)}, s16[21,16,128]{2,1,0:T(8,128)(2,1)S(1)}, u32[]{:S(2)}, u32[]{:S(2)}) collective-permute-start(s16[21,16,128]{2,1,0:T(8,128)(2,1)S(1)} %get-tuple-element.33), channel_id=1, source_target_pairs={{0,2},{1,3},{2,0},{3,1},{4,6},{5,7},{6,4},{7,5},{8,10},{9,11},{10,... | collective-permute-start | bytes 258056 | tf_op jit(solution)/shard_map/ppermute | solution.py:393
  59.4 1.6 %collective-permute-start.14 = (s16[21,16,128]{2,1,0:T(8,128)(2,1)S(1)}, s16[21,16,128]{2,1,0:T(8,128)(2,1)S(1)}, u32[]{:S(2)}, u32[]{:S(2)}) collective-permute-start(s16[21,16,128]{2,1,0:T(8,128)(2,1)S(1)} %get-tuple-element.34), channel_id=1, source_target_pairs={{0,4},{1,5},{2,6},{3,7},{4,0},{5,1},{6,2},{7,3},{8,12},{9,13},{10,... | collective-permute-start | bytes 258056 | tf_op jit(solution)/shard_map/ppermute | solution.py:393
  61.0 1.4 %collective-permute-start.15 = (s16[21,16,128]{2,1,0:T(8,128)(2,1)S(1)}, s16[21,16,128]{2,1,0:T(8,128)(2,1)S(1)}, u32[]{:S(2)}, u32[]{:S(2)}) collective-permute-start(s16[21,16,128]{2,1,0:T(8,128)(2,1)S(1)} %get-tuple-element.35), channel_id=1, source_target_pairs={{0,6},{1,7},{2,4},{3,5},{4,2},{5,3},{6,0},{7,1},{8,14},{9,15},{10,... | collective-permute-start | bytes 258056 | tf_op jit(solution)/shard_map/ppermute | solution.py:393
  62.5 3.8 %collective-permute-done.14.refs_1_ = s16[21,16,128]{2,1,0:T(8,128)(2,1)S(1)} collective-permute-done((s16[21,16,128]{2,1,0:T(8,128)(2,1)S(1)}, s16[21,16,128]{2,1,0:T(8,128)(2,1)S(1)}, u32[]{:S(2)}, u32[]{:S(2)}) %collective-permute-start.14) | collective-permute-done | bytes 86048 | tf_op jit(solution)/shard_map/ppermute | solution.py:393
  66.3 1.0 %collective-permute-done.15.refs_2_ = s16[21,16,128]{2,1,0:T(8,128)(2,1)S(1)} collective-permute-done((s16[21,16,128]{2,1,0:T(8,128)(2,1)S(1)}, s16[21,16,128]{2,1,0:T(8,128)(2,1)S(1)}, u32[]{:S(2)}, u32[]{:S(2)}) %collective-permute-start.15) | collective-permute-done | bytes 86048 | tf_op jit(solution)/shard_map/ppermute | solution.py:393
  67.6 2.4 %collective-permute-start.21 = (s16[21,16,128]{2,1,0:T(8,128)(2,1)S(1)}, s16[21,16,128]{2,1,0:T(8,128)(2,1)S(1)}, u32[]{:S(2)}, u32[]{:S(2)}) collective-permute-start(s16[21,16,128]{2,1,0:T(8,128)(2,1)S(1)} %shard_map.111.refs_0_), channel_id=1, source_target_pairs={{0,6},{1,7},{2,4},{3,5},{4,2},{5,3},{6,0},{7,1},{8,14},{9,15},{10,... | collective-permute-start | bytes 258056 | tf_op jit(solution)/shard_map/ppermute | solution.py:393
  70.5 1.4 %collective-permute-start.18 = (s16[21,16,128]{2,1,0:T(8,128)(2,1)S(1)}, s16[21,16,128]{2,1,0:T(8,128)(2,1)S(1)}, u32[]{:S(2)}, u32[]{:S(2)}) collective-permute-start(s16[21,16,128]{2,1,0:T(8,128)(2,1)S(1)} %shard_map.111.refs_0_), channel_id=1, source_target_pairs={{0,3},{1,2},{2,1},{3,0},{4,7},{5,6},{6,5},{7,4},{8,11},{9,10},{10,... | collective-permute-start | bytes 258056 | tf_op jit(solution)/shard_map/ppermute | solution.py:393
  72.5 1.5 %collective-permute-start.16 = (s16[21,16,128]{2,1,0:T(8,128)(2,1)S(1)}, s16[21,16,128]{2,1,0:T(8,128)(2,1)S(1)}, u32[]{:S(2)}, u32[]{:S(2)}) collective-permute-start(s16[21,16,128]{2,1,0:T(8,128)(2,1)S(1)} %shard_map.111.refs_0_), channel_id=1, source_target_pairs={{0,1},{1,0},{2,3},{3,2},{4,5},{5,4},{6,7},{7,6},{8,9},{9,8},{10,11... | collective-permute-start | bytes 258056 | tf_op jit(solution)/shard_map/ppermute | solution.py:393
  74.0 1.0 %collective-permute-done.21.refs_6_ = s16[21,16,128]{2,1,0:T(8,128)(2,1)S(1)} collective-permute-done((s16[21,16,128]{2,1,0:T(8,128)(2,1)S(1)}, s16[21,16,128]{2,1,0:T(8,128)(2,1)S(1)}, u32[]{:S(2)}, u32[]{:S(2)}) %collective-permute-start.21) | collective-permute-done | bytes 86048 | tf_op jit(solution)/shard_map/ppermute | solution.py:393
  75.0 1.6 %collective-permute-done.19.refs_4_ = s16[21,16,128]{2,1,0:T(8,128)(2,1)S(1)} collective-permute-done((s16[21,16,128]{2,1,0:T(8,128)(2,1)S(1)}, s16[21,16,128]{2,1,0:T(8,128)(2,1)S(1)}, u32[]{:S(2)}, u32[]{:S(2)}) %collective-permute-start.19) | collective-permute-done | bytes 86048 | tf_op jit(solution)/shard_map/ppermute | solution.py:393
  77.6 1.8 %collective-permute-done.22.refs_7_ = s16[21,16,128]{2,1,0:T(8,128)(2,1)S(1)} collective-permute-done((s16[21,16,128]{2,1,0:T(8,128)(2,1)S(1)}, s16[21,16,128]{2,1,0:T(8,128)(2,1)S(1)}, u32[]{:S(2)}, u32[]{:S(2)}) %collective-permute-start.22) | collective-permute-done | bytes 86048 | tf_op jit(solution)/shard_map/ppermute | solution.py:393
  79.5 1.6 %collective-permute-done.20.refs_5_ = s16[21,16,128]{2,1,0:T(8,128)(2,1)S(1)} collective-permute-done((s16[21,16,128]{2,1,0:T(8,128)(2,1)S(1)}, s16[21,16,128]{2,1,0:T(8,128)(2,1)S(1)}, u32[]{:S(2)}, u32[]{:S(2)}) %collective-permute-start.20) | collective-permute-done | bytes 86048 | tf_op jit(solution)/shard_map/ppermute | solution.py:393
  81.0 1.3 %shard_map.112 = (f32[256,1024]{1,0:T(8,128)}, f32[256,256]{1,0:T(8,128)}) custom-call(s32[1]{0:T(128)} %bitcast.me, s16[21,16,128]{2,1,0:T(8,128)(2,1)S(1)} %shard_map.111.refs_0_, s16[21,16,128]{2,1,0:T(8,128)(2,1)S(1)} %collective-permute-done.16.refs_1_, s16[21,16,128]{2,1,0:T(8,128)(2,1)S(1)} %collective-permute-done.17.refs_2_, ...), custom_call_target="tpu_custom_call" | custom-call | tf_op jit(solution)/shard_map/pallas_call | solution.py:531
  (46 shorter events, 8.4 us)
Async XLA Ops:
  0.6 19.1 %copy-start = (bf16[512,1024]{1,0:T(8,128)(2,1)S(1)}, bf16[512,1024]{1,0:T(8,128)(2,1)}, u32[]{:S(2)}) copy-start(bf16[512,1024]{1,0:T(8,128)(2,1)} %inputs.3) | copy-start | bytes 3145732
  0.6 19.7 %copy-start.2 = (s32[512,15]{0,1:T(8,128)S(1)}, s32[512,15]{0,1:T(8,128)}, u32[]{:S(2)}) copy-start(s32[512,15]{0,1:T(8,128)} %param.12) | copy-start | bytes 92164
  0.7 19.7 %copy-start.3 = (s32[512,15]{0,1:T(8,128)S(1)}, s32[512,15]{0,1:T(8,128)}, u32[]{:S(2)}) copy-start(s32[512,15]{0,1:T(8,128)} %param.14) | copy-start | bytes 92164
  0.7 19.7 %copy-start.5 = (s32[512]{0:T(512)S(1)}, s32[512]{0:T(512)}, u32[]{:S(2)}) copy-start(s32[512]{0:T(512)} %param.13) | copy-start | bytes 6148
  4.7 17.4 %copy-start.4 = (s32[4]{0:T(128)S(1)}, s32[4]{0:T(128)}, u32[]{:S(2)}) copy-start(s32[4]{0:T(128)} %offsets.7) | copy-start | bytes 52
  4.7 19.2 %copy-start.6 = (s32[4,128]{1,0:T(4,128)S(1)}, s32[4,128]{1,0:T(4,128)}, u32[]{:S(2)}) copy-start(s32[4,128]{1,0:T(4,128)} %requests.1) | copy-start | bytes 6148
  4.8 4.7 %collective-permute-start.5 = (bf16[512,256]{1,0:T(8,128)(2,1)S(1)}, bf16[512,256]{1,0:T(8,128)(2,1)S(1)}, u32[]{:S(2)}, u32[]{:S(2)}) collective-permute-start(bf16[512,256]{1,0:T(8,128)(2,1)S(1)} %get-tuple-element.20.rest_0_), channel_id=1, source_target_pairs={{0,8},{8,0},{16,24},{24,16},{1,9},{9,1},{17,25},{25,17},{2,10},{10... | collective-permute-start | bytes 786440 | tf_op jit(solution)/shard_map/ppermute | solution.py:393
  5.3 11.6 %collective-permute-start = (bf16[512,256]{1,0:T(8,128)(2,1)S(1)}, bf16[512,256]{1,0:T(8,128)(2,1)S(1)}, u32[]{:S(2)}, u32[]{:S(2)}) collective-permute-start(bf16[512,256]{1,0:T(8,128)(2,1)S(1)} %get-tuple-element.20.rest_0_), channel_id=1, source_target_pairs={{6,0},{7,1},{0,2},{1,3},{2,4},{3,5},{4,6},{5,7},{14,8},{15,9},{8,1... | collective-permute-start | bytes 786440 | tf_op jit(solution)/shard_map/ppermute | solution.py:389
  7.9 10.5 %collective-permute-start.6 = (bf16[512,256]{1,0:T(8,128)(2,1)S(1)}, bf16[512,256]{1,0:T(8,128)(2,1)S(1)}, u32[]{:S(2)}, u32[]{:S(2)}) collective-permute-start(bf16[512,256]{1,0:T(8,128)(2,1)S(1)} %get-tuple-element.20.rest_0_), channel_id=1, source_target_pairs={{0,16},{8,24},{16,0},{24,8},{1,17},{9,25},{17,1},{25,9},{2,18},{10... | collective-permute-start | bytes 786440 | tf_op jit(solution)/shard_map/ppermute | solution.py:393
  9.4 14.5 %collective-permute-start.7 = (bf16[512,256]{1,0:T(8,128)(2,1)S(1)}, bf16[512,256]{1,0:T(8,128)(2,1)S(1)}, u32[]{:S(2)}, u32[]{:S(2)}) collective-permute-start(bf16[512,256]{1,0:T(8,128)(2,1)S(1)} %collective-permute-done.5.rest_1_), channel_id=1, source_target_pairs={{0,16},{8,24},{16,0},{24,8},{1,17},{9,25},{17,1},{25,9},{2,18},{10... | collective-permute-start | bytes 786440 | tf_op jit(solution)/shard_map/ppermute | solution.py:393
  10.0 16.7 %collective-permute-start.4 = (bf16[512,256]{1,0:T(8,128)(2,1)S(1)}, bf16[512,256]{1,0:T(8,128)(2,1)S(1)}, u32[]{:S(2)}, u32[]{:S(2)}) collective-permute-start(bf16[512,256]{1,0:T(8,128)(2,1)S(1)} %get-tuple-element.20.rest_0_), channel_id=1, source_target_pairs={{0,1},{1,0},{2,3},{3,2},{4,5},{5,4},{6,7},{7,6},{8,9},{9,8},{10,11... | collective-permute-start | bytes 786440 | tf_op jit(solution)/shard_map/ppermute | solution.py:393
  16.9 9.8 %collective-permute-start.2 = (bf16[512,256]{1,0:T(8,128)(2,1)S(1)}, bf16[512,256]{1,0:T(8,128)(2,1)S(1)}, u32[]{:S(2)}, u32[]{:S(2)}) collective-permute-start(bf16[512,256]{1,0:T(8,128)(2,1)S(1)} %collective-permute-done.rest_0_), channel_id=1, source_target_pairs={{0,1},{1,0},{2,3},{3,2},{4,5},{5,4},{6,7},{7,6},{8,9},{9,8},{10,11... | collective-permute-start | bytes 786440 | tf_op jit(solution)/shard_map/ppermute | solution.py:393
  18.4 10.0 %collective-permute-start.3 = (bf16[512,256]{1,0:T(8,128)(2,1)S(1)}, bf16[512,256]{1,0:T(8,128)(2,1)S(1)}, u32[]{:S(2)}, u32[]{:S(2)}) collective-permute-start(bf16[512,256]{1,0:T(8,128)(2,1)S(1)} %collective-permute-done.rest_0_), channel_id=1, source_target_pairs={{6,0},{7,1},{0,2},{1,3},{2,4},{3,5},{4,6},{5,7},{14,8},{15,9},{8,1... | collective-permute-start | bytes 786440 | tf_op jit(solution)/shard_map/ppermute | solution.py:389
  18.4 15.2 %collective-permute-start.1 = (bf16[512,256]{1,0:T(8,128)(2,1)S(1)}, bf16[512,256]{1,0:T(8,128)(2,1)S(1)}, u32[]{:S(2)}, u32[]{:S(2)}) collective-permute-start(bf16[512,256]{1,0:T(8,128)(2,1)S(1)} %collective-permute-done.rest_0_), channel_id=1, source_target_pairs={{7,0},{1,2},{3,4},{5,6},{15,8},{9,10},{11,12},{13,14},{23,16},{17,... | collective-permute-start | bytes 786440 | tf_op jit(solution)/shard_map/ppermute | solution.py:435
  26.6 7.0 %copy-start.1 = (bf16[1024,256]{1,0:T(8,128)(2,1)S(1)}, bf16[1024,256]{1,0:T(8,128)(2,1)}, u32[]{:S(2)}) copy-start(bf16[1024,256]{1,0:T(8,128)(2,1)} %rest_3_.1) | copy-start | bytes 1572868
  36.7 3.3 %collective-permute-start.8 = (s16[2,256,1408]{2,1,0:T(8,128)(2,1)S(1)}, s16[2,256,1408]{2,1,0:T(8,128)(2,1)S(1)}, u32[]{:S(2)}, u32[]{:S(2)}) collective-permute-start(s16[2,256,1408]{2,1,0:T(8,128)(2,1)S(1)} %get-tuple-element.26), channel_id=1, source_target_pairs={{0,8},{8,0},{16,24},{24,16},{1,9},{9,1},{17,25},{25,17},{2,10},{10... | collective-permute-start | bytes 4325384 | tf_op jit(solution)/shard_map/ppermute | solution.py:393
  40.6 9.9 %collective-permute-start.9 = (s16[81,16,128]{2,1,0:T(8,128)(2,1)S(1)}, s16[81,16,128]{2,1,0:T(8,128)(2,1)S(1)}, u32[]{:S(2)}, u32[]{:S(2)}) collective-permute-start(s16[81,16,128]{2,1,0:T(8,128)(2,1)S(1)} %shard_map.105), channel_id=1, source_target_pairs={{0,16},{8,24},{16,0},{24,8},{1,17},{9,25},{17,1},{25,9},{2,18},{10... | collective-permute-start | bytes 995336 | tf_op jit(solution)/shard_map/ppermute | solution.py:393
  41.9 9.6 %collective-permute-start.10 = (s16[81,16,128]{2,1,0:T(8,128)(2,1)S(1)}, s16[81,16,128]{2,1,0:T(8,128)(2,1)S(1)}, u32[]{:S(2)}, u32[]{:S(2)}) collective-permute-start(s16[81,16,128]{2,1,0:T(8,128)(2,1)S(1)} %shard_map.106), channel_id=1, source_target_pairs={{0,1},{1,0},{2,3},{3,2},{4,5},{5,4},{6,7},{7,6},{8,9},{9,8},{10,11... | collective-permute-start | bytes 995336 | tf_op jit(solution)/shard_map/ppermute | solution.py:393
  51.8 5.4 %collective-permute-start.11 = (s16[41,16,128]{2,1,0:T(8,128)(2,1)S(1)}, s16[41,16,128]{2,1,0:T(8,128)(2,1)S(1)}, u32[]{:S(2)}, u32[]{:S(2)}) collective-permute-start(s16[41,16,128]{2,1,0:T(8,128)(2,1)S(1)} %get-tuple-element.31), channel_id=1, source_target_pairs={{0,1},{1,0},{2,3},{3,2},{4,5},{5,4},{6,7},{7,6},{8,9},{9,8},{10,11... | collective-permute-start | bytes 503816 | tf_op jit(solution)/shard_map/ppermute | solution.py:393
  52.1 5.4 %collective-permute-start.12 = (s16[41,16,128]{2,1,0:T(8,128)(2,1)S(1)}, s16[41,16,128]{2,1,0:T(8,128)(2,1)S(1)}, u32[]{:S(2)}, u32[]{:S(2)}) collective-permute-start(s16[41,16,128]{2,1,0:T(8,128)(2,1)S(1)} %get-tuple-element.32), channel_id=1, source_target_pairs={{0,16},{8,24},{16,0},{24,8},{1,17},{9,25},{17,1},{25,9},{2,18},{10... | collective-permute-start | bytes 503816 | tf_op jit(solution)/shard_map/ppermute | solution.py:393
  57.8 4.7 %collective-permute-start.13 = (s16[21,16,128]{2,1,0:T(8,128)(2,1)S(1)}, s16[21,16,128]{2,1,0:T(8,128)(2,1)S(1)}, u32[]{:S(2)}, u32[]{:S(2)}) collective-permute-start(s16[21,16,128]{2,1,0:T(8,128)(2,1)S(1)} %get-tuple-element.33), channel_id=1, source_target_pairs={{0,2},{1,3},{2,0},{3,1},{4,6},{5,7},{6,4},{7,5},{8,10},{9,11},{10,... | collective-permute-start | bytes 258056 | tf_op jit(solution)/shard_map/ppermute | solution.py:393
  59.4 6.9 %collective-permute-start.14 = (s16[21,16,128]{2,1,0:T(8,128)(2,1)S(1)}, s16[21,16,128]{2,1,0:T(8,128)(2,1)S(1)}, u32[]{:S(2)}, u32[]{:S(2)}) collective-permute-start(s16[21,16,128]{2,1,0:T(8,128)(2,1)S(1)} %get-tuple-element.34), channel_id=1, source_target_pairs={{0,4},{1,5},{2,6},{3,7},{4,0},{5,1},{6,2},{7,3},{8,12},{9,13},{10,... | collective-permute-start | bytes 258056 | tf_op jit(solution)/shard_map/ppermute | solution.py:393
  61.0 6.4 %collective-permute-start.15 = (s16[21,16,128]{2,1,0:T(8,128)(2,1)S(1)}, s16[21,16,128]{2,1,0:T(8,128)(2,1)S(1)}, u32[]{:S(2)}, u32[]{:S(2)}) collective-permute-start(s16[21,16,128]{2,1,0:T(8,128)(2,1)S(1)} %get-tuple-element.35), channel_id=1, source_target_pairs={{0,6},{1,7},{2,4},{3,5},{4,2},{5,3},{6,0},{7,1},{8,14},{9,15},{10,... | collective-permute-start | bytes 258056 | tf_op jit(solution)/shard_map/ppermute | solution.py:393
  67.6 7.4 %collective-permute-start.21 = (s16[21,16,128]{2,1,0:T(8,128)(2,1)S(1)}, s16[21,16,128]{2,1,0:T(8,128)(2,1)S(1)}, u32[]{:S(2)}, u32[]{:S(2)}) collective-permute-start(s16[21,16,128]{2,1,0:T(8,128)(2,1)S(1)} %shard_map.111.refs_0_), channel_id=1, source_target_pairs={{0,6},{1,7},{2,4},{3,5},{4,2},{5,3},{6,0},{7,1},{8,14},{9,15},{10,... | collective-permute-start | bytes 258056 | tf_op jit(solution)/shard_map/ppermute | solution.py:393
  70.1 6.5 %collective-permute-start.19 = (s16[21,16,128]{2,1,0:T(8,128)(2,1)S(1)}, s16[21,16,128]{2,1,0:T(8,128)(2,1)S(1)}, u32[]{:S(2)}, u32[]{:S(2)}) collective-permute-start(s16[21,16,128]{2,1,0:T(8,128)(2,1)S(1)} %shard_map.111.refs_0_), channel_id=1, source_target_pairs={{0,4},{1,5},{2,6},{3,7},{4,0},{5,1},{6,2},{7,3},{8,12},{9,13},{10,... | collective-permute-start | bytes 258056 | tf_op jit(solution)/shard_map/ppermute | solution.py:393
  70.5 6.6 %collective-permute-start.18 = (s16[21,16,128]{2,1,0:T(8,128)(2,1)S(1)}, s16[21,16,128]{2,1,0:T(8,128)(2,1)S(1)}, u32[]{:S(2)}, u32[]{:S(2)}) collective-permute-start(s16[21,16,128]{2,1,0:T(8,128)(2,1)S(1)} %shard_map.111.refs_0_), channel_id=1, source_target_pairs={{0,3},{1,2},{2,1},{3,0},{4,7},{5,6},{6,5},{7,4},{8,11},{9,10},{10,... | collective-permute-start | bytes 258056 | tf_op jit(solution)/shard_map/ppermute | solution.py:393
  72.0 5.3 %collective-permute-start.17 = (s16[21,16,128]{2,1,0:T(8,128)(2,1)S(1)}, s16[21,16,128]{2,1,0:T(8,128)(2,1)S(1)}, u32[]{:S(2)}, u32[]{:S(2)}) collective-permute-start(s16[21,16,128]{2,1,0:T(8,128)(2,1)S(1)} %shard_map.111.refs_0_), channel_id=1, source_target_pairs={{0,2},{1,3},{2,0},{3,1},{4,6},{5,7},{6,4},{7,5},{8,10},{9,11},{10,... | collective-permute-start | bytes 258056 | tf_op jit(solution)/shard_map/ppermute | solution.py:393
  72.5 5.1 %collective-permute-start.16 = (s16[21,16,128]{2,1,0:T(8,128)(2,1)S(1)}, s16[21,16,128]{2,1,0:T(8,128)(2,1)S(1)}, u32[]{:S(2)}, u32[]{:S(2)}) collective-permute-start(s16[21,16,128]{2,1,0:T(8,128)(2,1)S(1)} %shard_map.111.refs_0_), channel_id=1, source_target_pairs={{0,1},{1,0},{2,3},{3,2},{4,5},{5,4},{6,7},{7,6},{8,9},{9,8},{10,11... | collective-permute-start | bytes 258056 | tf_op jit(solution)/shard_map/ppermute | solution.py:393
  75.0 4.5 %collective-permute-start.22 = (s16[21,16,128]{2,1,0:T(8,128)(2,1)S(1)}, s16[21,16,128]{2,1,0:T(8,128)(2,1)S(1)}, u32[]{:S(2)}, u32[]{:S(2)}) collective-permute-start(s16[21,16,128]{2,1,0:T(8,128)(2,1)S(1)} %collective-permute-done.21.refs_6_), channel_id=1, source_target_pairs={{0,1},{1,0},{2,3},{3,2},{4,5},{5,4},{6,7},{7,6},{8,9},{9,8},{10,11... | collective-permute-start | bytes 258056 | tf_op jit(solution)/shard_map/ppermute | solution.py:393
  76.5 4.5 %collective-permute-start.20 = (s16[21,16,128]{2,1,0:T(8,128)(2,1)S(1)}, s16[21,16,128]{2,1,0:T(8,128)(2,1)S(1)}, u32[]{:S(2)}, u32[]{:S(2)}) collective-permute-start(s16[21,16,128]{2,1,0:T(8,128)(2,1)S(1)} %collective-permute-done.19.refs_4_), channel_id=1, source_target_pairs={{0,1},{1,0},{2,3},{3,2},{4,5},{5,4},{6,7},{7,6},{8,9},{9,8},{10,11... | collective-permute-start | bytes 258056 | tf_op jit(solution)/shard_map/ppermute | solution.py:393
